TPU v7x, 16 devices: a 4x2x1 block of a 4x4x8 slice. The times are simulated.
16 devices in a mesh: dp: 2 (over y, z), tp: 8 (over x, core).
Axes of the slice: x: 4, y: 2, z: 1, core: 2. Of those that a mesh axis runs over, the one named last changes fastest.
The devices are a block of a 4x4x8 slice.
Arguments:
- x: bfloat16 [48, 192, 5120], P('dp'), parts along dimension 0
- seq_lens: int32 [48], P('dp'), parts along dimension 0
- w_query: bfloat16 [5120, 5120], P(None, 'tp')
- w_key: bfloat16 [5120, 1024], P(None, 'tp')
- w_value: bfloat16 [5120, 1024], P(None, 'tp')
- w_out: bfloat16 [5120, 5120], P('tp')
- w_gate: bfloat16 [5120, 27648], P(None, 'tp')
- w_up: bfloat16 [5120, 27648], P(None, 'tp')
- w_down: bfloat16 [27648, 5120], P('tp')
- attn_gain: bfloat16 [5120], replicated
- mlp_gain: bfloat16 [5120], replicated
- k_cache: bfloat16 [48, 384, 8, 128], P('dp', None, 'tp'), parts along dimension 0
- v_cache: bfloat16 [48, 384, 8, 128], P('dp', None, 'tp'), parts along dimension 0
Outputs:
- output 1: bfloat16 [48, 192, 5120], P('dp'), parts along dimension 0
- output 2: bfloat16 [48, 384, 8, 128], P('dp', None, 'tp'), parts along dimension 0
- output 3: bfloat16 [48, 384, 8, 128], P('dp', None, 'tp'), parts along dimension 0
There are 2 independent parts. A program takes and returns all parts, laid end to end along the dimension named above; an argument that names none is the same for every part.
All inputs are finite; a program needn't handle non-finite values.
Results may differ from a plain program's by a relative error of at most 0.0113584.
Values are sent between devices in bfloat16 or wider.
A program may use at most 768 MiB of HBM per device.

v0:
```python
import jax
import jax.numpy as jnp
from jax import lax
from jax.sharding import PartitionSpec as P

EPS = 1e-5
ROPE_BASE = 10000.0


def rms_norm(rows, gain):
    rows32 = rows.astype(jnp.float32)
    inv_rms = lax.rsqrt(jnp.mean(rows32 * rows32, axis=-1, keepdims=True) + EPS)
    return (rows32 * inv_rms * gain.astype(jnp.float32)).astype(jnp.bfloat16)


def rotary(vecs):
    seq_len = vecs.shape[1]
    head_dim = vecs.shape[-1]
    half_dim = head_dim // 2
    inv_freq = ROPE_BASE ** (-jnp.arange(0, head_dim, 2).astype(jnp.float32) / head_dim)
    angles = jnp.arange(seq_len).astype(jnp.float32)[:, None] * inv_freq[None, :]
    table_shape = (1, seq_len) + (1,) * (vecs.ndim - 3) + (half_dim,)
    cos_tab = jnp.cos(angles).reshape(table_shape)
    sin_tab = jnp.sin(angles).reshape(table_shape)
    pairs = vecs.reshape(vecs.shape[:-1] + (half_dim, 2))
    even_part = pairs[..., 0]
    odd_part = pairs[..., 1]
    turned = jnp.stack([even_part * cos_tab - odd_part * sin_tab, even_part * sin_tab + odd_part * cos_tab], axis=-1)
    return turned.reshape(vecs.shape).astype(jnp.bfloat16)


def causal_attention(queries, keys, values, seq_lens):
    seq_len = queries.shape[1]
    head_dim = queries.shape[-1]
    scores = jnp.einsum("bqkgh,bskh->bkgqs", queries, keys, preferred_element_type=jnp.float32) * head_dim ** -0.5
    positions = jnp.arange(seq_len)
    allowed = (positions[None, None, :] <= positions[None, :, None]) & (positions[None, None, :] < seq_lens[:, None, None])
    scores = jnp.where(allowed[:, None, None], scores, -jnp.inf)
    probs = jax.nn.softmax(scores, axis=-1).astype(jnp.bfloat16)
    return jnp.einsum("bkgqs,bskh->bqkgh", probs, values, preferred_element_type=jnp.float32).astype(jnp.bfloat16)


def sum_partials(partial, resid_rows, tp_size):
    batch_size, seq_len, model_width = partial.shape
    stacked = partial.reshape(batch_size, tp_size, seq_len // tp_size, model_width)
    received = lax.all_to_all(stacked, "tp", 1, 1, tiled=True)
    summed = jnp.sum(received.astype(jnp.float32), axis=1)
    return (resid_rows.astype(jnp.float32) + summed).astype(jnp.bfloat16)


def solution(mesh):
    tp_size = mesh.shape["tp"]

    def layer_shard(x, seq_lens, w_query, w_key, w_value, w_out, w_gate, w_up, w_down, attn_gain, mlp_gain, k_cache, v_cache):
        batch_size, seq_len, model_width = x.shape
        head_dim = k_cache.shape[3]
        kv_local = k_cache.shape[2]
        group_size = w_query.shape[1] // (head_dim * kv_local)
        rows_each = seq_len // tp_size
        tp_index = lax.axis_index("tp")
        normed = rms_norm(x, attn_gain)
        queries = rotary(jnp.einsum("bsd,dk->bsk", normed, w_query, preferred_element_type=jnp.float32).reshape(batch_size, seq_len, kv_local, group_size, head_dim))
        keys = rotary(jnp.einsum("bsd,dk->bsk", normed, w_key, preferred_element_type=jnp.float32).reshape(batch_size, seq_len, kv_local, head_dim))
        values = jnp.einsum("bsd,dk->bsk", normed, w_value, preferred_element_type=jnp.float32).astype(jnp.bfloat16).reshape(batch_size, seq_len, kv_local, head_dim)
        valid = (jnp.arange(seq_len)[None, :] < seq_lens[:, None])[:, :, None, None]
        keys = jnp.where(valid, keys, jnp.zeros_like(keys))
        values = jnp.where(valid, values, jnp.zeros_like(values))
        k_cache_out = lax.dynamic_update_slice(k_cache, keys, (0, 0, 0, 0))
        v_cache_out = lax.dynamic_update_slice(v_cache, values, (0, 0, 0, 0))
        attn_rows = causal_attention(queries, keys, values, seq_lens).reshape(batch_size, seq_len, -1)
        attn_part = jnp.einsum("bsk,kd->bsd", attn_rows, w_out, preferred_element_type=jnp.float32).astype(jnp.bfloat16)
        x_rows = lax.dynamic_slice_in_dim(x, tp_index * rows_each, rows_each, axis=1)
        hidden_rows = sum_partials(attn_part, x_rows, tp_size)
        normed_mlp = lax.all_gather(rms_norm(hidden_rows, mlp_gain), "tp", axis=1, tiled=True)
        gate_pre = jnp.einsum("bsd,df->bsf", normed_mlp, w_gate, preferred_element_type=jnp.float32)
        up_pre = jnp.einsum("bsd,df->bsf", normed_mlp, w_up, preferred_element_type=jnp.float32)
        gated = (jax.nn.silu(gate_pre) * up_pre).astype(jnp.bfloat16)
        mlp_part = jnp.einsum("bsf,fd->bsd", gated, w_down, preferred_element_type=jnp.float32).astype(jnp.bfloat16)
        out_rows = sum_partials(mlp_part, hidden_rows, tp_size)
        y = lax.all_gather(out_rows, "tp", axis=1, tiled=True)
        return y, k_cache_out, v_cache_out

    cache_spec = P("dp", None, "tp", None)
    return jax.shard_map(layer_shard, mesh=mesh, in_specs=(P("dp", None, None), P("dp"), P(None, "tp"), P(None, "tp"), P(None, "tp"), P("tp", None), P(None, "tp"), P(None, "tp"), P("tp", None), P(), P(), cache_spec, cache_spec), out_specs=(P("dp", None, None), cache_spec, cache_spec), check_vma=False)
```

profile of v0, /device:TPU:113, one launch (start us, length us, event | category | flops | bytes accessed | tf_op | source)
XLA Modules:
  0.0 2443.9 jit_solution(3970739538116399673)
XLA Ops:
  7.2 0.0 copy-start
  7.2 3.4 copy.53
  10.6 3.3 copy.52
  13.9 0.0 copy-start.6
  13.9 0.0 copy-start.9
  14.0 15.3 fusion
  29.3 0.0 copy-done.6
  29.3 0.0 copy-done.9
  29.3 21.3 fusion.18
  50.6 3.5 copy.28
  54.2 0.3 multiply_cosine_fusion
  54.5 2.4 multiply_subtract_fusion
  56.9 0.3 maximum_convert_fusion
  57.1 0.0 copy-start.2
  57.1 1.9 copy.29
  59.1 44.5 %fusion.16 = f32[24,192,640]{2,1,0:T(8,128)} fusion(bf16[24,192,5120]{2,1,0:T(8,128)(2,1)} %param.13, f32[5120]{0:T(1024)S(1)} %convert_element_type.129, f32[24,192]{1,0:T(8,128)S(1)} %add_rsqrt_fusion, bf16[5120,640]{1,0:T(8,128)(2,1)} %param.15), kind=kOutput, calls=%fused_computation.16 | convolution fusion | flops 30293360640 | bytes 65574912 | tf_op jit(solution)/shard_map/bsd,dk->bsk/dot_general | solution.py:62
  103.6 0.0 copy-done.2
  103.6 15.8 copy.30
  119.4 0.0 copy-start.8
  119.4 6.9 subtract_convert_fusion
  126.3 0.0 copy-done.8
  126.3 0.1 iota_compare_fusion.1
  126.4 0.0 copy-start.4
  126.4 4.3 pad_maximum_fusion
  130.7 0.9 broadcast_and_fusion
  131.6 18.0 fusion.23
  149.6 10.8 fusion.22
  160.4 0.0 copy-done.4
  160.4 0.0 copy-done
  160.4 21.5 bitcast_dynamic-update-slice_fusion
  181.9 13.7 convert_bitcast_fusion
  195.7 9.7 copy.33
  205.4 46.4 %convolution_convert_fusion = bf16[24,192,5120]{2,1,0:T(8,128)(2,1)} fusion(bf16[24,192,640]{1,2,0:T(8,128)(2,1)} %bitcast.97, bf16[640,5120]{1,0:T(8,128)(2,1)} %param.18), kind=kOutput, calls=%fused_computation.14 | convolution fusion | flops 30222581760 | bytes 59637760 | tf_op jit(solution)/shard_map/bsk,kd->bsd/dot_general | solution.py:71
  251.8 31.0 %copy.35 = bf16[24,8,24,5120]{3,2,0,1:T(8,128)(2,1)} copy(bf16[24,8,24,5120]{3,2,1,0:T(8,128)(2,1)} %bitcast.91) | data formatting | bytes 94371840 | tf_op jit(solution)/shard_map/reshape | solution.py:45
  282.8 0.0 copy-start.7
  282.8 8.9 all-to-all-start
  291.7 0.0 all-gather.3.cloned.1.call-start
  291.7 0.0 copy-done.7
  291.7 509.1 %all-to-all-done = bf16[24,8,24,5120]{3,2,0,1:T(8,128)(2,1)} async-done(((bf16[24,8,24,5120]{3,2,0,1:T(8,128)(2,1)}), bf16[24,8,24,5120]{3,2,0,1:T(8,128)(2,1)}, u32[]{:S(2)}, u32[]{:S(2)}) %all-to-all-start) | async-done | bytes 47185952 | tf_op jit(solution)/shard_map/all_to_all | solution.py:46
  800.8 20.5 convert_reduce_fusion.1
  821.3 11.0 fusion.24
  832.3 7.3 fusion.26
  839.6 0.1 all-gather.3.cloned.1.call-update
  839.6 0.1 all-gather.5.cloned.1.call-start
  839.7 212.6 %all-gather.3.cloned.1.call-done = bf16[24,192,5120]{2,1,0:T(8,128)(2,1)} async-done(((bf16[24,24,5120]{2,1,0:T(8,128)(2,1)}), bf16[24,192,5120]{2,1,0:T(8,128)(2,1)}) %all-gather.3.cloned.1.call-update) | async-done | bytes 47185936 | tf_op jit(solution)/shard_map/all_gather | solution.py:74
  1052.3 183.1 %fusion.5 = f32[24,192,3456]{2,1,0:T(8,128)} fusion(bf16[24,192,5120]{2,1,0:T(8,128)(2,1)} %all-gather.3.cloned.1.call-done, bf16[5120,3456]{1,0:T(8,128)(2,1)} %param.20), kind=kOutput, calls=%fused_computation.10 | convolution fusion | flops 163074539520 | bytes 146276352 | tf_op jit(solution)/shard_map/bsd,df->bsf/dot_general | solution.py:76
  1235.4 191.1 %multiply_convert_fusion.clone.6 = bf16[24,192,3456]{2,1,0:T(8,128)(2,1)} fusion(f32[24,192,3456]{2,1,0:T(8,128)} %fusion.5, bf16[24,192,5120]{2,1,0:T(8,128)(2,1)} %all-gather.3.cloned.1.call-done, bf16[5120,3456]{1,0:T(8,128)(2,1)} %param.19), kind=kOutput, calls=%fused_computation.7.clone.clone.clone.clone.clone.1 | convolution fusion | flops 163170091008 | bytes 178126848 | tf_op jit(solution)/shard_map/bsd,df->bsf/dot_general | solution.py:75
  1426.5 182.6 %fusion.10 = bf16[24,192,5120]{2,1,0:T(8,128)(2,1)} fusion(bf16[3456,5120]{1,0:T(8,128)(2,1)} %param.21, bf16[24,192,3456]{2,1,0:T(8,128)(2,1)} %multiply_convert_fusion.clone.6), kind=kOutput, calls=%fused_computation.13 | convolution fusion | flops 163098132480 | bytes 114425856 | tf_op jit(solution)/shard_map/bsf,fd->bsd/dot_general | solution.py:78
  1609.0 31.0 %copy.36 = bf16[24,8,24,5120]{3,2,0,1:T(8,128)(2,1)} copy(bf16[24,8,24,5120]{3,2,1,0:T(8,128)(2,1)} %bitcast.92) | data formatting | bytes 94371840 | tf_op jit(solution)/shard_map/reshape | solution.py:45
  1640.0 523.4 %all_to_all.10 = bf16[24,8,24,5120]{3,2,0,1:T(8,128)(2,1)} all-to-all(bf16[24,8,24,5120]{3,2,0,1:T(8,128)(2,1)} %copy.36), channel_id=1, replica_groups=mesh['dp'=2,'tp'=8] {'tp'}, dimensions={1} | all-to-all | bytes 94371840 | tf_op jit(solution)/shard_map/all_to_all | solution.py:46
  2163.4 20.3 convert_reduce_fusion
  2183.7 0.0 copy-start.3
  2183.7 0.0 copy-start.5
  2183.7 10.5 fusion.27
  2194.3 0.1 all-gather.5.cloned.1.call-update
  2194.3 0.0 copy-done.3
  2194.3 0.0 copy-done.5
  2194.4 1.2 broadcast_select_fusion
  2195.6 2.2 copy.37
  2197.8 1.2 constant_dynamic-update-slice_fusion
  2199.0 206.5 %all-gather.5.cloned.1.call-done = bf16[24,192,5120]{2,1,0:T(8,128)(2,1)} async-done(((bf16[24,24,5120]{2,1,0:T(8,128)(2,1)}), bf16[24,192,5120]{2,1,0:T(8,128)(2,1)}) %all-gather.5.cloned.1.call-update) | async-done | bytes 47185936 | tf_op jit(solution)/shard_map/all_gather | solution.py:80
  2405.5 0.0 copy-start.1
  2405.5 31.1 %copy.54 = bf16[24,192,5120]{2,1,0:T(8,128)(2,1)} copy(bf16[24,192,5120]{2,1,0:T(8,128)(2,1)} %all-gather.5.cloned.1.call-done) | data formatting | bytes 94371840
  2436.6 0.0 copy-done.1
  (7 shorter events, 0.1 us)
Async XLA Ops:
  7.2 153.2 %copy-start = (bf16[5120,128]{1,0:T(8,128)(2,1)S(1)}, bf16[5120,128]{1,0:T(8,128)(2,1)}, u32[]{:S(2)}) copy-start(bf16[5120,128]{1,0:T(8,128)(2,1)} %param.17) | copy-start | bytes 3932164
  13.9 15.4 copy-start.6
  13.9 15.4 copy-start.9
  57.1 46.5 %copy-start.2 = (bf16[24,192,1,64,2]{1,0,4,3,2:T(8,128)(2,1)}, bf16[24,192,1,64,2]{1,0,4,3,2:T(8,128)(2,1)S(1)}, u32[]{:S(2)}) copy-start(bf16[24,192,1,64,2]{1,0,4,3,2:T(8,128)(2,1)S(1)} %maximum_convert_fusion) | copy-start | bytes 3538948
  119.4 6.9 copy-start.8
  126.4 34.0 %copy-start.4 = (pred[24,192]{1,0:T(8,128)(4,1)}, pred[24,192]{1,0:T(8,128)(4,1)S(1)}, u32[]{:S(2)}) copy-start(pred[24,192]{1,0:T(8,128)(4,1)S(1)} %iota_compare_fusion.1) | copy-start | bytes 13828
  282.8 9.0 copy-start.7
  282.8 518.0 %all-to-all-start = ((bf16[24,8,24,5120]{3,2,0,1:T(8,128)(2,1)}), bf16[24,8,24,5120]{3,2,0,1:T(8,128)(2,1)}, u32[]{:S(2)}, u32[]{:S(2)}) async-start(bf16[24,8,24,5120]{3,2,0,1:T(8,128)(2,1)} %copy.35), calls=%async_computation | async-start | bytes 94371840 | tf_op jit(solution)/shard_map/all_to_all | solution.py:46
  291.7 760.6 %all-gather.3.cloned.1.call-start = ((), (), s32[]{:S(2)}) async-start(), calls=%async_computation.2 | async-start | bytes 53084160 | tf_op jit(solution)/shard_map/all_gather | solution.py:74
  839.6 1565.9 %all-gather.5.cloned.1.call-start = ((), (), s32[]{:S(2)}) async-start(), calls=%async_computation.3 | async-start | bytes 53084160 | tf_op jit(solution)/shard_map/all_gather | solution.py:80
  2183.7 10.6 copy-start.3
  2183.7 10.6 copy-start.5
  2405.5 31.1 %copy-start.1 = (bf16[5120,128]{1,0:T(8,128)(2,1)S(1)}, bf16[5120,128]{1,0:T(8,128)(2,1)}, u32[]{:S(2)}) copy-start(bf16[5120,128]{1,0:T(8,128)(2,1)} %param.17) | copy-start | bytes 3932164
Sparse Core Ops, SparseCore 0:
  839.7 212.4 all-gather.2
  2194.5 211.0 all-gather.4
where the time goes:
time: 2450 us; the launch traced here: 2440 us
  waiting for transfers between devices  928 us (38%)
  matrix products  722 us (29%)
  blocking collectives  523 us (21%)
  local copies, waits for them, and re-layouts  134 us (5%)
  other arithmetic  112 us (5%)
    all_to_all x1, blocking collectives, sum_partials(): received = lax.all_to_all(stacked, 'tp', 1, 1, tiled=True)  523 us
    all_to_all x1, waiting for transfers between devices, sum_partials(): received = lax.all_to_all(stacked, 'tp', 1, 1, tiled=True)  509 us
    all_gather x1, waiting for transfers between devices, layer_shard(): lax.all_gather(rms_norm(hidden_rows, mlp_gain), 'tp', axis=1, tiled=True)  213 us
    all_gather x1, waiting for transfers between devices, layer_shard(): y = lax.all_gather(out_rows, 'tp', axis=1, tiled=True)  206 us
    dot_general x1, matrix products, layer_shard(): jnp.einsum('bsd,df->bsf', normed_mlp, w_gate, preferred_element_type=jnp....  191 us
    dot_general x1, matrix products, layer_shard(): jnp.einsum('bsd,df->bsf', normed_mlp, w_up, preferred_element_type=jnp.fl...  183 us
    dot_general x1, matrix products, layer_shard(): jnp.einsum('bsf,fd->bsd', gated, w_down, preferred_element_type=jnp.float32)  183 us
    reshape x2, local copies, waits for them, and re-layouts, sum_partials(): partial.reshape(batch_size, tp_size, seq_len // tp_size, model_width)  62 us
  transfers between devices with their start and end apart: 3, of which 3 were waited for; matrix products, arithmetic and copies ran while one was open for 0% of the time, Pallas kernels for 0%

commit v1 on v0

--- a/solution.py
+++ b/solution.py
@@ -1,10 +1,14 @@
 import jax
 import jax.numpy as jnp
 from jax import lax
+from jax.experimental import pallas as pl
+from jax.experimental.pallas import tpu as pltpu
 from jax.sharding import PartitionSpec as P
+
 
 EPS = 1e-5
 ROPE_BASE = 10000.0
+CHUNK_SEQS = (4, 4, 4, 4, 4, 4)
 
 
 def rms_norm(rows, gain):
@@ -40,24 +44,100 @@
     return jnp.einsum("bkgqs,bskh->bqkgh", probs, values, preferred_element_type=jnp.float32).astype(jnp.bfloat16)
 
 
-def sum_partials(partial, resid_rows, tp_size):
-    batch_size, seq_len, model_width = partial.shape
-    stacked = partial.reshape(batch_size, tp_size, seq_len // tp_size, model_width)
-    received = lax.all_to_all(stacked, "tp", 1, 1, tiled=True)
-    summed = jnp.sum(received.astype(jnp.float32), axis=1)
-    return (resid_rows.astype(jnp.float32) + summed).astype(jnp.bfloat16)
+def out_kernel(o_ref, w_ref, x_ref, h_ref):
+    groups, _, depth = o_ref.shape
+    total = jnp.zeros(h_ref.shape, jnp.float32)
+    for group in range(groups):
+        part = jnp.dot(o_ref[group], w_ref[pl.ds(group * depth, depth), :], preferred_element_type=jnp.float32)
+        total = total + part.astype(jnp.bfloat16).astype(jnp.float32)
+    h_ref[...] = (x_ref[...].astype(jnp.float32) + total).astype(jnp.bfloat16)
+
+
+def out_project(o_rows, w_full, x_rows, tile):
+    groups, rows, depth = o_rows.shape
+    width = w_full.shape[1]
+    return pl.pallas_call(
+        out_kernel,
+        grid=(width // tile,),
+        in_specs=[
+            pl.BlockSpec((groups, rows, depth), lambda n: (0, 0, 0)),
+            pl.BlockSpec((groups * depth, tile), lambda n: (0, n)),
+            pl.BlockSpec((rows, tile), lambda n: (0, n)),
+        ],
+        out_specs=pl.BlockSpec((rows, tile), lambda n: (0, n)),
+        out_shape=jax.ShapeDtypeStruct((rows, width), jnp.bfloat16),
+        compiler_params=pltpu.CompilerParams(vmem_limit_bytes=56 * 2**20),
+        cost_estimate=pl.CostEstimate(flops=2 * rows * groups * depth * width, bytes_accessed=2 * groups * depth * width, transcendentals=0),
+        name="out_project",
+    )(o_rows, w_full, x_rows)
 
 
 def solution(mesh):
     tp_size = mesh.shape["tp"]
+    cores = 2
+    chips = tp_size // cores
+
+    def chip_perm(shift):
+        return [(chip * cores + core, ((chip + shift) % chips) * cores + core) for chip in range(chips) for core in range(cores)]
+
+    partner_perm = [(index, index ^ 1) for index in range(tp_size)]
+
+    def places():
+        index = lax.axis_index("tp")
+        chip, core = lax.shift_right_logical(index, 1), index & 1
+        return [core, 1 - core] + [(chip + shift) & (chips - 1) for shift in (0, 1, 2, chips - 1)]
+
+    def reduce_rows(partial, resid_rows, where):
+        rows = resid_rows.shape[0]
+        width = partial.shape[-1]
+        half = width // 2
+        fence = lax.optimization_barrier
+
+        def move(piece, perm):
+            return lax.ppermute(piece, "tp", perm)
+
+        def pick(array, axis, place):
+            begin = [0] * array.ndim
+            begin[axis] = place
+            size = list(array.shape)
+            size[axis] = 1
+            return lax.squeeze(lax.dynamic_slice(array, begin, size, allow_negative_indices=False), (axis,))
+
+        partial, where = fence((partial, where))
+        blocks = partial.reshape(chips, cores, rows, width)
+        keep, give = fence((pick(blocks, 1, where[0]), pick(blocks, 1, where[1])))
+        got = move(give, partner_perm)
+        low, high = slice(0, half), slice(half, width)
+
+        def both(place, columns):
+            return pick(keep, 0, place)[:, columns].astype(jnp.float32) + pick(got, 0, place)[:, columns].astype(jnp.float32)
+
+        keep, got, where = fence((keep, got, where))
+        pieces = fence((both(where[4], low), both(where[4], high), both(where[3], high), both(where[5], low)))
+        far_low = move(pieces[0], chip_perm(1))
+        far_high = move(pieces[1], chip_perm(-1))
+        near_high = move(pieces[2], chip_perm(1))
+        near_low = move(pieces[3], chip_perm(-1))
+        keep, got, where, far_low, far_high = fence((keep, got, where, far_low, far_high))
+        pieces = fence((both(where[3], low) + far_low, both(where[5], high) + far_high))
+        run_low = move(pieces[0], chip_perm(1))
+        run_high = move(pieces[1], chip_perm(-1))
+        keep, got, where, near_low, near_high, run_low, run_high = fence((keep, got, where, near_low, near_high, run_low, run_high))
+        sum_low = both(where[2], low) + near_low + run_low
+        sum_high = both(where[2], high) + near_high + run_high
+        summed = jnp.concatenate([sum_low, sum_high], axis=1)
+        return fence((resid_rows.astype(jnp.float32) + summed).astype(jnp.bfloat16))
 
     def layer_shard(x, seq_lens, w_query, w_key, w_value, w_out, w_gate, w_up, w_down, attn_gain, mlp_gain, k_cache, v_cache):
         batch_size, seq_len, model_width = x.shape
         head_dim = k_cache.shape[3]
         kv_local = k_cache.shape[2]
         group_size = w_query.shape[1] // (head_dim * kv_local)
-        rows_each = seq_len // tp_size
+        all_rows = batch_size * seq_len
+        chunk_rows = [seqs * seq_len for seqs in CHUNK_SEQS]
+        starts = [sum(chunk_rows[:chunk]) for chunk in range(len(chunk_rows))]
         tp_index = lax.axis_index("tp")
+        w_out_full = lax.all_gather(w_out, "tp", axis=0, tiled=True)
         normed = rms_norm(x, attn_gain)
         queries = rotary(jnp.einsum("bsd,dk->bsk", normed, w_query, preferred_element_type=jnp.float32).reshape(batch_size, seq_len, kv_local, group_size, head_dim))
         keys = rotary(jnp.einsum("bsd,dk->bsk", normed, w_key, preferred_element_type=jnp.float32).reshape(batch_size, seq_len, kv_local, head_dim))
@@ -67,18 +147,29 @@
         values = jnp.where(valid, values, jnp.zeros_like(values))
         k_cache_out = lax.dynamic_update_slice(k_cache, keys, (0, 0, 0, 0))
         v_cache_out = lax.dynamic_update_slice(v_cache, values, (0, 0, 0, 0))
-        attn_rows = causal_attention(queries, keys, values, seq_lens).reshape(batch_size, seq_len, -1)
-        attn_part = jnp.einsum("bsk,kd->bsd", attn_rows, w_out, preferred_element_type=jnp.float32).astype(jnp.bfloat16)
-        x_rows = lax.dynamic_slice_in_dim(x, tp_index * rows_each, rows_each, axis=1)
-        hidden_rows = sum_partials(attn_part, x_rows, tp_size)
-        normed_mlp = lax.all_gather(rms_norm(hidden_rows, mlp_gain), "tp", axis=1, tiled=True)
-        gate_pre = jnp.einsum("bsd,df->bsf", normed_mlp, w_gate, preferred_element_type=jnp.float32)
-        up_pre = jnp.einsum("bsd,df->bsf", normed_mlp, w_up, preferred_element_type=jnp.float32)
-        gated = (jax.nn.silu(gate_pre) * up_pre).astype(jnp.bfloat16)
-        mlp_part = jnp.einsum("bsf,fd->bsd", gated, w_down, preferred_element_type=jnp.float32).astype(jnp.bfloat16)
-        out_rows = sum_partials(mlp_part, hidden_rows, tp_size)
-        y = lax.all_gather(out_rows, "tp", axis=1, tiled=True)
-        return y, k_cache_out, v_cache_out
+        attn_rows = causal_attention(queries, keys, values, seq_lens).reshape(all_rows, -1)
+
+        def by_owner(array):
+            pieces = [array[start:start + size].reshape(tp_size, size // tp_size, array.shape[1]) for start, size in zip(starts, chunk_rows)]
+            return jnp.concatenate(pieces, axis=1)
+
+        o_rows = lax.all_to_all(by_owner(attn_rows), "tp", 0, 0, tiled=True)
+        x_rows = jnp.concatenate([lax.dynamic_slice_in_dim(x.reshape(all_rows, model_width), start + tp_index * (size // tp_size), size // tp_size, axis=0) for start, size in zip(starts, chunk_rows)], axis=0)
+        hidden_rows = out_project(o_rows, w_out_full, x_rows, 512)
+        normed_rows = rms_norm(hidden_rows, mlp_gain)
+        where = places()
+        y = jnp.zeros((all_rows, model_width), jnp.bfloat16)
+        for start, size in zip(starts, chunk_rows):
+            own = slice(start // tp_size, (start + size) // tp_size)
+            normed_mlp = lax.all_gather(normed_rows[own], "tp", axis=0, tiled=True)
+            gate_pre = jnp.dot(normed_mlp, w_gate, preferred_element_type=jnp.float32)
+            up_pre = jnp.dot(normed_mlp, w_up, preferred_element_type=jnp.float32)
+            gated = (jax.nn.silu(gate_pre) * up_pre).astype(jnp.bfloat16)
+            mlp_part = jnp.dot(gated, w_down, preferred_element_type=jnp.float32).astype(jnp.bfloat16)
+            out_rows = reduce_rows(mlp_part, hidden_rows[own], where)
+            y_chunk = lax.all_gather(out_rows, "tp", axis=0, tiled=True)
+            y = lax.dynamic_update_slice(y, y_chunk, (start, 0))
+        return y.reshape(batch_size, seq_len, model_width), k_cache_out, v_cache_out
 
     cache_spec = P("dp", None, "tp", None)
     return jax.shard_map(layer_shard, mesh=mesh, in_specs=(P("dp", None, None), P("dp"), P(None, "tp"), P(None, "tp"), P(None, "tp"), P("tp", None), P(None, "tp"), P(None, "tp"), P("tp", None), P(), P(), cache_spec, cache_spec), out_specs=(P("dp", None, None), cache_spec, cache_spec), check_vma=False)

time: 2450 us -> 1770 us (0.72)
  blocking collectives: 523 us -> 0 us
  waiting for transfers between devices: 928 us -> 601 us
  local copies, waits for them, and re-layouts: 134 us -> 209 us
  Pallas kernels: 0 us -> 44.3 us
  starting transfers between devices: 9.01 us -> 48.6 us
    all_to_all x1 -> x0, blocking collectives: 523 us -> none  [sum_partials(): received = lax.all_to_all(stacked, 'tp', 1, 1, tiled=True)]
    all_to_all x1, waiting for transfers between devices: 509 us -> 53.6 us  [layer_shard(): o_rows = lax.all_to_all(by_owner(attn_rows), 'tp', 0, 0, tiled=True)]
    ppermute x0 -> x42, waiting for transfers between devices: none -> 282 us  [move(): return lax.ppermute(piece, 'tp', perm)]
    all_gather x2 -> x13, waiting for transfers between devices: 419 us -> 260 us  [the longest x6 219 us: layer_shard(): y_chunk = lax.all_gather(out_rows, 'tp', axis=0, tiled=True)]
    squeeze x0 -> x36, local copies, waits for them, and re-layouts: none -> 64 us  [pick(): lax.squeeze(lax.dynamic_slice(array, begin, size, allow_negative_indices=...]
    add x0 -> x36, other arithmetic: none -> 61.6 us  [the longest x18 34.1 us: both(): pick(keep, 0, place)[:, columns].astype(jnp.float32)]
    dynamic_update_slice x0 -> x6, local copies, waits for them, and re-layouts: none -> 53.8 us  [layer_shard(): y = lax.dynamic_update_slice(y, y_chunk, (start, 0))]
    reshape x2 -> x6, local copies, waits for them, and re-layouts: 62 us -> 12 us  [by_owner(): array[start:start + size].reshape(tp_size, size // tp_size, array.shape[1])]
  transfers between devices with their start and end apart: 3 -> 56, of which waited for: 3 -> 25; matrix products, arithmetic and copies ran while one was open for 0% -> 58% of each run, Pallas kernels for 0% -> 0%
where the time goes in v1:
time: 1770 us; the launch traced here: 1760 us
  matrix products  725 us (41%)
  waiting for transfers between devices  601 us (34%)
  local copies, waits for them, and re-layouts  209 us (12%)
  other arithmetic  120 us (7%)
  starting transfers between devices  48.6 us (3%)
  Pallas kernels  44.3 us (3%)
    ppermute x42, waiting for transfers between devices, move(): return lax.ppermute(piece, 'tp', perm)  282 us
    all_gather x6, waiting for transfers between devices, layer_shard(): y_chunk = lax.all_gather(out_rows, 'tp', axis=0, tiled=True)  219 us
    dot_general x6, matrix products, layer_shard(): gate_pre = jnp.dot(normed_mlp, w_gate, preferred_element_type=jnp.float32)  203 us
    dot_general x6, matrix products, layer_shard(): up_pre = jnp.dot(normed_mlp, w_up, preferred_element_type=jnp.float32)  202 us
    dot_general x6, matrix products, layer_shard(): jnp.dot(gated, w_down, preferred_element_type=jnp.float32)  197 us
    squeeze x36, local copies, waits for them, and re-layouts, pick(): lax.squeeze(lax.dynamic_slice(array, begin, size, allow_negative_indices=...  64 us
    dynamic_update_slice x6, local copies, waits for them, and re-layouts, layer_shard(): y = lax.dynamic_update_slice(y, y_chunk, (start, 0))  53.8 us
    all_to_all x1, waiting for transfers between devices, layer_shard(): o_rows = lax.all_to_all(by_owner(attn_rows), 'tp', 0, 0, tiled=True)  53.6 us
  transfers between devices with their start and end apart: 56, of which 25 were waited for; matrix products, arithmetic and copies ran while one was open for 58% of the time, Pallas kernels for 0%

profile of v1, /device:TPU:113, one launch (start us, length us, event | category | flops | bytes accessed | tf_op | source)
XLA Modules:
  0.0 1763.8 jit_solution(1667796171508783727)
XLA Ops:
  14.1 20.4 %fusion = f32[24,192]{1,0:T(8,128)S(1)} fusion(bf16[24,192,5120]{2,1,0:T(8,128)(2,1)} %param.13), kind=kLoop, calls=%fused_computation.2 | loop fusion | flops 70774272 | bytes 47204352 | tf_op jit(solution)/shard_map/reduce_sum | solution.py:16
  34.5 23.5 %fusion.5 = f32[24,192,128]{2,1,0:T(8,128)} fusion(bf16[24,192,5120]{2,1,0:T(8,128)(2,1)} %param.13, f32[5120]{0:T(1024)S(1)} %convert_element_type.463, f32[24,192]{1,0:T(8,128)S(1)} %add_rsqrt_fusion, bf16[5120,128]{1,0:T(8,128)(2,1)S(1)} %copy-done.80), kind=kOutput, calls=%fused_computation.6 | convolution fusion | flops 6134169600 | bytes 50894848 | tf_op jit(solution)/shard_map/bsd,dk->bsk/dot_general | solution.py:143
  66.4 44.9 %fusion.3 = f32[24,192,640]{2,1,0:T(8,128)} fusion(bf16[24,192,5120]{2,1,0:T(8,128)(2,1)} %param.13, f32[5120]{0:T(1024)S(1)} %convert_element_type.463, f32[24,192]{1,0:T(8,128)S(1)} %add_rsqrt_fusion, bf16[5120,640]{1,0:T(8,128)(2,1)} %param.15), kind=kOutput, calls=%fused_computation.5 | convolution fusion | flops 30293360640 | bytes 65574912 | tf_op jit(solution)/shard_map/bsd,dk->bsk/dot_general | solution.py:142
  111.3 16.0 copy.27
  129.5 7.0 subtract_convert_fusion
  136.5 4.4 pad_maximum_fusion
  140.9 18.4 %fusion.10 = (f32[24,5,192]{2,1,0:T(8,128)S(1)}, f32[24,192,192,5]{2,1,3,0:T(8,128)}) fusion(pred[24,192,192]{1,2,0:T(8,128)(4,1)} %broadcast_and_fusion, bf16[24,192,5,128]{1,0,3,2:T(8,128)(2,1)} %bitcast.295, bf16[24,192,128]{2,1,0:T(8,128)(2,1)} %copy.26, pred[24,192]{1,0:T(8,128)(4,1)S(1)} %iota_compare_fusion.1), kind=kOutput, calls=%fused_computation.12 | convolution fusion | flops 1146299904 | bytes 25754112 | tf_op jit(solution)/shard_map/bqkgh,bskh->bkgqs/dot_general | solution.py:39
  159.2 11.0 fusion.9
  170.2 21.9 %bitcast_dynamic-update-slice_fusion = (bf16[24,384,1,128]{3,1,2,0:T(8,128)(2,1)}, bf16[24,192,128]{2,1,0:T(8,128)(2,1)}) fusion(bf16[24,384,1,128]{3,1,2,0:T(8,128)(2,1)} %copy.65, bf16[5120,128]{1,0:T(8,128)(2,1)S(1)} %copy-done, bf16[24,192,5120]{2,1,0:T(8,128)(2,1)} %param.13, f32[5120]{0:T(1024)S(1)} %convert_element_type.463, ...), kind=kOutput, calls=%fused_computation.72 | convolution fusion | flops 6135349248 | bytes 50899456 | tf_op jit(solution)/shard_map/bsd,dk->bsk/dot_general | solution.py:144
  192.1 14.2 convert_bitcast_fusion
  206.3 4.9 fusion.46
  243.4 6.9 all-to-all-start
  263.8 53.6 %all-to-all-done.o_ref = bf16[8,576,640]{2,1,0:T(8,128)(2,1)} async-done(((bf16[8,576,640]{2,1,0:T(8,128)(2,1)}), bf16[8,576,640]{2,1,0:T(8,128)(2,1)}, u32[]{:S(2)}, u32[]{:S(2)}) %all-to-all-start) | async-done | bytes 5898272 | tf_op jit(solution)/shard_map/all_to_all | solution.py:156
  317.4 44.3 %out_project.1 = bf16[576,5120]{1,0:T(8,128)(2,1)} custom-call(bf16[8,576,640]{2,1,0:T(8,128)(2,1)} %all-to-all-done.o_ref, bf16[5120,5120]{1,0:T(8,128)(2,1)} %all-gather.14.cloned.1.call-done.w_ref, bf16[576,5120]{1,0:T(8,128)(2,1)} %dynamic-slice_dynamic-update-slice_fusion.x_ref), custom_call_target="tpu_custom_call" | custom-call | flops 30198988800 | bytes 52428800 | tf_op jit(solution)/shard_map/out_project/pallas_call | solution.py:59
  374.6 40.8 %all-gather.16.cloned.1.call-done = bf16[768,5120]{1,0:T(8,128)(2,1)} async-done(((bf16[96,5120]{1,0:T(8,128)(2,1)}), bf16[768,5120]{1,0:T(8,128)(2,1)}) %all-gather.16.cloned.1.call-update) | async-done | bytes 7864336 | tf_op jit(solution)/shard_map/all_gather | solution.py:164
  415.3 33.7 %fusion.47 = f32[768,3456]{1,0:T(8,128)S(1)} fusion(bf16[768,5120]{1,0:T(8,128)(2,1)} %all-gather.16.cloned.1.call-done, bf16[5120,3456]{1,0:T(8,128)(2,1)} %param.19), kind=kOutput, calls=%fused_computation.230 | convolution fusion | flops 27179089920 | bytes 53870592 | tf_op jit(solution)/shard_map/dot_general | solution.py:165
  449.1 33.7 %multiply_convert_fusion.5 = bf16[768,3456]{1,0:T(8,128)(2,1)S(1)} fusion(f32[768,3456]{1,0:T(8,128)S(1)} %fusion.47, bf16[768,5120]{1,0:T(8,128)(2,1)S(1)} %copy-done.79, bf16[5120,3456]{1,0:T(8,128)(2,1)} %param.20), kind=kOutput, calls=%fused_computation.26 | convolution fusion | flops 27195015168 | bytes 59179008 | tf_op jit(solution)/shard_map/dot_general | solution.py:166
  482.8 32.7 %convolution_convert_fusion.5 = bf16[768,5120]{1,0:T(8,128)(2,1)S(1)} fusion(bf16[768,3456]{1,0:T(8,128)(2,1)S(1)} %multiply_convert_fusion.5, bf16[3456,5120]{1,0:T(8,128)(2,1)} %param.21), kind=kOutput, calls=%fused_computation.32 | convolution fusion | flops 27183022080 | bytes 48562176 | tf_op jit(solution)/shard_map/dot_general | solution.py:168
  519.8 34.1 %fusion.48 = f32[768,3456]{1,0:T(8,128)S(1)} fusion(bf16[768,5120]{1,0:T(8,128)(2,1)} %all-gather.20.cloned.1.call-done, bf16[5120,3456]{1,0:T(8,128)(2,1)} %param.19), kind=kOutput, calls=%fused_computation.231 | convolution fusion | flops 27179089920 | bytes 53870592 | tf_op jit(solution)/shard_map/dot_general | solution.py:165
  554.0 33.6 %multiply_convert_fusion.4 = bf16[768,3456]{1,0:T(8,128)(2,1)S(1)} fusion(f32[768,3456]{1,0:T(8,128)S(1)} %fusion.48, bf16[768,5120]{1,0:T(8,128)(2,1)S(1)} %copy-done.78, bf16[5120,3456]{1,0:T(8,128)(2,1)} %param.20), kind=kOutput, calls=%fused_computation.25 | convolution fusion | flops 27195015168 | bytes 59179008 | tf_op jit(solution)/shard_map/dot_general | solution.py:166
  587.7 32.7 %convolution_convert_fusion.4 = bf16[768,5120]{1,0:T(8,128)(2,1)S(1)} fusion(bf16[768,3456]{1,0:T(8,128)(2,1)S(1)} %multiply_convert_fusion.4, bf16[3456,5120]{1,0:T(8,128)(2,1)} %param.21), kind=kOutput, calls=%fused_computation.31 | convolution fusion | flops 27183022080 | bytes 48562176 | tf_op jit(solution)/shard_map/dot_general | solution.py:168
  624.5 33.9 %fusion.49 = f32[768,3456]{1,0:T(8,128)S(1)} fusion(bf16[768,5120]{1,0:T(8,128)(2,1)} %all-gather.24.cloned.1.call-done, bf16[5120,3456]{1,0:T(8,128)(2,1)} %param.19), kind=kOutput, calls=%fused_computation.232 | convolution fusion | flops 27179089920 | bytes 53870592 | tf_op jit(solution)/shard_map/dot_general | solution.py:165
  658.4 33.6 %multiply_convert_fusion.3 = bf16[768,3456]{1,0:T(8,128)(2,1)S(1)} fusion(f32[768,3456]{1,0:T(8,128)S(1)} %fusion.49, bf16[768,5120]{1,0:T(8,128)(2,1)S(1)} %copy-done.77, bf16[5120,3456]{1,0:T(8,128)(2,1)} %param.20), kind=kOutput, calls=%fused_computation.24 | convolution fusion | flops 27195015168 | bytes 59179008 | tf_op jit(solution)/shard_map/dot_general | solution.py:166
  692.0 32.7 %convolution_convert_fusion.3 = bf16[768,5120]{1,0:T(8,128)(2,1)S(1)} fusion(bf16[768,3456]{1,0:T(8,128)(2,1)S(1)} %multiply_convert_fusion.3, bf16[3456,5120]{1,0:T(8,128)(2,1)} %param.21), kind=kOutput, calls=%fused_computation.30 | convolution fusion | flops 27183022080 | bytes 48562176 | tf_op jit(solution)/shard_map/dot_general | solution.py:168
  728.9 33.7 %fusion.50 = f32[768,3456]{1,0:T(8,128)S(1)} fusion(bf16[768,5120]{1,0:T(8,128)(2,1)} %all-gather.28.cloned.1.call-done, bf16[5120,3456]{1,0:T(8,128)(2,1)} %param.19), kind=kOutput, calls=%fused_computation.233 | convolution fusion | flops 27179089920 | bytes 53870592 | tf_op jit(solution)/shard_map/dot_general | solution.py:165
  762.7 33.6 %multiply_convert_fusion.2 = bf16[768,3456]{1,0:T(8,128)(2,1)S(1)} fusion(f32[768,3456]{1,0:T(8,128)S(1)} %fusion.50, bf16[768,5120]{1,0:T(8,128)(2,1)S(1)} %copy-done.75, bf16[5120,3456]{1,0:T(8,128)(2,1)} %param.20), kind=kOutput, calls=%fused_computation.23 | convolution fusion | flops 27195015168 | bytes 59179008 | tf_op jit(solution)/shard_map/dot_general | solution.py:166
  796.3 32.7 %convolution_convert_fusion.2 = bf16[768,5120]{1,0:T(8,128)(2,1)S(1)} fusion(bf16[768,3456]{1,0:T(8,128)(2,1)S(1)} %multiply_convert_fusion.2, bf16[3456,5120]{1,0:T(8,128)(2,1)} %param.21), kind=kOutput, calls=%fused_computation.29 | convolution fusion | flops 27183022080 | bytes 48562176 | tf_op jit(solution)/shard_map/dot_general | solution.py:168
  833.1 34.0 %fusion.51 = f32[768,3456]{1,0:T(8,128)S(1)} fusion(bf16[768,5120]{1,0:T(8,128)(2,1)} %all-gather.32.cloned.1.call-done, bf16[5120,3456]{1,0:T(8,128)(2,1)} %param.19), kind=kOutput, calls=%fused_computation.234 | convolution fusion | flops 27179089920 | bytes 53870592 | tf_op jit(solution)/shard_map/dot_general | solution.py:165
  867.0 33.6 %multiply_convert_fusion.1 = bf16[768,3456]{1,0:T(8,128)(2,1)S(1)} fusion(f32[768,3456]{1,0:T(8,128)S(1)} %fusion.51, bf16[768,5120]{1,0:T(8,128)(2,1)S(1)} %copy-done.74, bf16[5120,3456]{1,0:T(8,128)(2,1)} %param.20), kind=kOutput, calls=%fused_computation.22 | convolution fusion | flops 27195015168 | bytes 59179008 | tf_op jit(solution)/shard_map/dot_general | solution.py:166
  900.6 32.7 %convolution_convert_fusion.1 = bf16[768,5120]{1,0:T(8,128)(2,1)S(1)} fusion(bf16[768,3456]{1,0:T(8,128)(2,1)S(1)} %multiply_convert_fusion.1, bf16[3456,5120]{1,0:T(8,128)(2,1)} %param.21), kind=kOutput, calls=%fused_computation.28 | convolution fusion | flops 27183022080 | bytes 48562176 | tf_op jit(solution)/shard_map/dot_general | solution.py:168
  937.6 33.7 %fusion.52 = f32[768,3456]{1,0:T(8,128)S(1)} fusion(bf16[768,5120]{1,0:T(8,128)(2,1)} %all-gather.36.cloned.1.call-done, bf16[5120,3456]{1,0:T(8,128)(2,1)} %param.19), kind=kOutput, calls=%fused_computation.235 | convolution fusion | flops 27179089920 | bytes 53870592 | tf_op jit(solution)/shard_map/dot_general | solution.py:165
  971.3 33.6 %multiply_convert_fusion = bf16[768,3456]{1,0:T(8,128)(2,1)S(1)} fusion(f32[768,3456]{1,0:T(8,128)S(1)} %fusion.52, bf16[768,5120]{1,0:T(8,128)(2,1)S(1)} %copy-done.76, bf16[5120,3456]{1,0:T(8,128)(2,1)} %param.20), kind=kOutput, calls=%fused_computation.21 | convolution fusion | flops 27195015168 | bytes 59179008 | tf_op jit(solution)/shard_map/dot_general | solution.py:166
  1004.9 34.0 %convolution_convert_fusion = bf16[768,5120]{1,0:T(8,128)(2,1)} fusion(bf16[768,3456]{1,0:T(8,128)(2,1)S(1)} %multiply_convert_fusion, bf16[3456,5120]{1,0:T(8,128)(2,1)} %param.21), kind=kOutput, calls=%fused_computation.27 | convolution fusion | flops 27183022080 | bytes 48562176 | tf_op jit(solution)/shard_map/dot_general | solution.py:168
  1038.9 6.2 dynamic-slice_bitcast_fusion
  1070.1 4.3 dynamic-slice_bitcast_fusion.42
  1112.2 6.0 collective-permute-done.8
  1118.2 6.6 collective-permute-done.9
  1130.0 11.5 collective-permute-done.15
  1141.5 25.4 %collective-permute-done.16 = f32[96,2560]{1,0:T(8,128)S(1)} collective-permute-done((f32[96,2560]{1,0:T(8,128)S(1)}, f32[96,2560]{1,0:T(8,128)S(1)}, u32[]{:S(2)}, u32[]{:S(2)}) %collective-permute-start.16) | collective-permute-done | bytes 983072 | tf_op jit(solution)/shard_map/ppermute | solution.py:97
  1173.2 16.6 collective-permute-done.23
  1195.2 15.7 collective-permute-done.30
  1216.2 15.2 collective-permute-done.37
  1260.7 11.4 collective-permute-done.11
  1272.1 21.1 %collective-permute-done.12 = f32[96,2560]{1,0:T(8,128)S(1)} collective-permute-done((f32[96,2560]{1,0:T(8,128)S(1)}, f32[96,2560]{1,0:T(8,128)S(1)}, u32[]{:S(2)}, u32[]{:S(2)}) %collective-permute-start.12) | collective-permute-done | bytes 983072 | tf_op jit(solution)/shard_map/ppermute | solution.py:97
  1297.7 16.5 collective-permute-done.18
  1314.3 21.1 %collective-permute-done.19 = f32[96,2560]{1,0:T(8,128)S(1)} collective-permute-done((f32[96,2560]{1,0:T(8,128)}, f32[96,2560]{1,0:T(8,128)S(1)}, u32[]{:S(2)}, u32[]{:S(2)}) %collective-permute-start.19) | collective-permute-done | bytes 983072 | tf_op jit(solution)/shard_map/ppermute | solution.py:97
  1339.9 16.5 collective-permute-done.25
  1356.4 21.1 %collective-permute-done.26 = f32[96,2560]{1,0:T(8,128)S(1)} collective-permute-done((f32[96,2560]{1,0:T(8,128)}, f32[96,2560]{1,0:T(8,128)S(1)}, u32[]{:S(2)}, u32[]{:S(2)}) %collective-permute-start.26) | collective-permute-done | bytes 983072 | tf_op jit(solution)/shard_map/ppermute | solution.py:97
  1382.9 15.6 collective-permute-done.32
  1398.5 21.1 %collective-permute-done.33 = f32[96,2560]{1,0:T(8,128)S(1)} collective-permute-done((f32[96,2560]{1,0:T(8,128)S(1)}, f32[96,2560]{1,0:T(8,128)S(1)}, u32[]{:S(2)}, u32[]{:S(2)}) %collective-permute-start.33) | collective-permute-done | bytes 983072 | tf_op jit(solution)/shard_map/ppermute | solution.py:97
  1421.6 19.1 %collective-permute-done.39 = f32[96,2560]{1,0:T(8,128)S(1)} collective-permute-done((f32[96,2560]{1,0:T(8,128)S(1)}, f32[96,2560]{1,0:T(8,128)S(1)}, u32[]{:S(2)}, u32[]{:S(2)}) %collective-permute-start.39) | collective-permute-done | bytes 983072 | tf_op jit(solution)/shard_map/ppermute | solution.py:97
  1440.7 21.1 %collective-permute-done.40 = f32[96,2560]{1,0:T(8,128)S(1)} collective-permute-done((f32[96,2560]{1,0:T(8,128)S(1)}, f32[96,2560]{1,0:T(8,128)S(1)}, u32[]{:S(2)}, u32[]{:S(2)}) %collective-permute-start.40) | collective-permute-done | bytes 983072 | tf_op jit(solution)/shard_map/ppermute | solution.py:97
  1484.1 40.5 %all-gather.18.cloned.1.call-done = bf16[768,5120]{1,0:T(8,128)(2,1)} async-done(((bf16[96,5120]{1,0:T(8,128)(2,1)}), bf16[768,5120]{1,0:T(8,128)(2,1)}) %all-gather.18.cloned.1.call-update) | async-done | bytes 7864336 | tf_op jit(solution)/shard_map/all_gather | solution.py:170
  1524.6 18.8 %dynamic_update_slice.24 = bf16[4608,5120]{1,0:T(8,128)(2,1)} pad(bf16[768,5120]{1,0:T(8,128)(2,1)} %all-gather.18.cloned.1.call-done, bf16[]{:T(256)} %constant.17.clone.1), padding=0_3840x0_0 | pad | bytes 55050240 | tf_op jit(solution)/shard_map/dynamic_update_slice | solution.py:171
  1543.4 26.3 %all-gather.22.cloned.1.call-done = bf16[768,5120]{1,0:T(8,128)(2,1)} async-done(((bf16[96,5120]{1,0:T(8,128)(2,1)}), bf16[768,5120]{1,0:T(8,128)(2,1)}) %all-gather.22.cloned.1.call-update) | async-done | bytes 7864336 | tf_op jit(solution)/shard_map/all_gather | solution.py:170
  1569.7 7.0 constant_dynamic-update-slice_fusion.11
  1576.7 38.0 %all-gather.26.cloned.1.call-done = bf16[768,5120]{1,0:T(8,128)(2,1)} async-done(((bf16[96,5120]{1,0:T(8,128)(2,1)}), bf16[768,5120]{1,0:T(8,128)(2,1)}) %all-gather.26.cloned.1.call-update) | async-done | bytes 7864336 | tf_op jit(solution)/shard_map/all_gather | solution.py:170
  1614.6 7.0 constant_dynamic-update-slice_fusion.10
  1621.6 38.1 %all-gather.30.cloned.1.call-done = bf16[768,5120]{1,0:T(8,128)(2,1)} async-done(((bf16[96,5120]{1,0:T(8,128)(2,1)}), bf16[768,5120]{1,0:T(8,128)(2,1)}) %all-gather.30.cloned.1.call-update) | async-done | bytes 7864336 | tf_op jit(solution)/shard_map/all_gather | solution.py:170
  1659.8 7.0 constant_dynamic-update-slice_fusion.9
  1666.7 38.0 %all-gather.34.cloned.1.call-done = bf16[768,5120]{1,0:T(8,128)(2,1)} async-done(((bf16[96,5120]{1,0:T(8,128)(2,1)}), bf16[768,5120]{1,0:T(8,128)(2,1)}) %all-gather.34.cloned.1.call-update) | async-done | bytes 7864336 | tf_op jit(solution)/shard_map/all_gather | solution.py:170
  1704.7 7.1 constant_dynamic-update-slice_fusion.8
  1711.8 38.0 %all-gather.38.cloned.1.call-done = bf16[768,5120]{1,0:T(8,128)(2,1)} async-done(((bf16[96,5120]{1,0:T(8,128)(2,1)}), bf16[768,5120]{1,0:T(8,128)(2,1)}) %all-gather.38.cloned.1.call-update) | async-done | bytes 7864336 | tf_op jit(solution)/shard_map/all_gather | solution.py:170
  1749.8 7.0 constant_dynamic-update-slice_fusion.7
  (383 shorter events, 249.4 us)
Async XLA Ops:
  7.2 163.0 %copy-start = (bf16[5120,128]{1,0:T(8,128)(2,1)S(1)}, bf16[5120,128]{1,0:T(8,128)(2,1)}, u32[]{:S(2)}) copy-start(bf16[5120,128]{1,0:T(8,128)(2,1)} %param.17) | copy-start | bytes 3932164
  7.2 310.1 %all-gather.14.cloned.1.call-start = ((), (), s32[]{:S(2)}) async-start(), calls=%async_computation.1 | async-start | bytes 58982400 | tf_op jit(solution)/shard_map/all_gather | solution.py:140
  243.4 74.0 %all-to-all-start = ((bf16[8,576,640]{2,1,0:T(8,128)(2,1)}), bf16[8,576,640]{2,1,0:T(8,128)(2,1)}, u32[]{:S(2)}, u32[]{:S(2)}) async-start(bf16[8,576,640]{2,1,0:T(8,128)(2,1)} %constant_dynamic-update-slice_fusion), calls=%async_computation | async-start | bytes 11796480 | tf_op jit(solution)/shard_map/all_to_all | solution.py:156
  250.3 165.0 %all-gather.16.cloned.1.call-start = ((), (), s32[]{:S(2)}) async-start(), calls=%async_computation.2 | async-start | bytes 8847360 | tf_op jit(solution)/shard_map/all_gather | solution.py:164
  371.0 148.9 %all-gather.20.cloned.1.call-start = ((), (), s32[]{:S(2)}) async-start(), calls=%async_computation.4 | async-start | bytes 8847360 | tf_op jit(solution)/shard_map/all_gather | solution.py:164
  371.8 252.7 %all-gather.24.cloned.1.call-start = ((), (), s32[]{:S(2)}) async-start(), calls=%async_computation.6 | async-start | bytes 8847360 | tf_op jit(solution)/shard_map/all_gather | solution.py:164
  372.4 356.5 %all-gather.28.cloned.1.call-start = ((), (), s32[]{:S(2)}) async-start(), calls=%async_computation.8 | async-start | bytes 8847360 | tf_op jit(solution)/shard_map/all_gather | solution.py:164
  373.1 460.0 %all-gather.32.cloned.1.call-start = ((), (), s32[]{:S(2)}) async-start(), calls=%async_computation.10 | async-start | bytes 8847360 | tf_op jit(solution)/shard_map/all_gather | solution.py:164
  373.7 563.9 %all-gather.36.cloned.1.call-start = ((), (), s32[]{:S(2)}) async-start(), calls=%async_computation.12 | async-start | bytes 8847360 | tf_op jit(solution)/shard_map/all_gather | solution.py:164
  374.5 1150.1 %all-gather.18.cloned.1.call-start = ((), (), s32[]{:S(2)}) async-start(), calls=%async_computation.3 | async-start | bytes 8847360 | tf_op jit(solution)/shard_map/all_gather | solution.py:170
  519.5 525.6 %collective-permute-start = (bf16[4,96,5120]{2,1,0:T(8,128)(2,1)}, bf16[4,96,5120]{2,1,0:T(8,128)(2,1)}, u32[]{:S(2)}, u32[]{:S(2)}) collective-permute-start(bf16[4,96,5120]{2,1,0:T(8,128)(2,1)} %get-tuple-element.217), channel_id=1, source_target_pairs={{0,1},{1,0},{2,3},{3,2},{4,5},{5,4},{6,7},{7,6},{8,9},{9,8},{10,11... | collective-permute-start | bytes 11796488 | tf_op jit(solution)/shard_map/ppermute | solution.py:97
  624.4 427.2 %collective-permute-start.7 = (bf16[4,96,5120]{2,1,0:T(8,128)(2,1)}, bf16[4,96,5120]{2,1,0:T(8,128)(2,1)}, u32[]{:S(2)}, u32[]{:S(2)}) collective-permute-start(bf16[4,96,5120]{2,1,0:T(8,128)(2,1)} %get-tuple-element.252), channel_id=1, source_target_pairs={{0,1},{1,0},{2,3},{3,2},{4,5},{5,4},{6,7},{7,6},{8,9},{9,8},{10,11... | collective-permute-start | bytes 11796488 | tf_op jit(solution)/shard_map/ppermute | solution.py:97
  728.6 329.8 %collective-permute-start.14 = (bf16[4,96,5120]{2,1,0:T(8,128)(2,1)}, bf16[4,96,5120]{2,1,0:T(8,128)(2,1)}, u32[]{:S(2)}, u32[]{:S(2)}) collective-permute-start(bf16[4,96,5120]{2,1,0:T(8,128)(2,1)} %get-tuple-element.287), channel_id=1, source_target_pairs={{0,1},{1,0},{2,3},{3,2},{4,5},{5,4},{6,7},{7,6},{8,9},{9,8},{10,11... | collective-permute-start | bytes 11796488 | tf_op jit(solution)/shard_map/ppermute | solution.py:97
  832.9 227.7 %collective-permute-start.21 = (bf16[4,96,5120]{2,1,0:T(8,128)(2,1)}, bf16[4,96,5120]{2,1,0:T(8,128)(2,1)}, u32[]{:S(2)}, u32[]{:S(2)}) collective-permute-start(bf16[4,96,5120]{2,1,0:T(8,128)(2,1)} %get-tuple-element.322), channel_id=1, source_target_pairs={{0,1},{1,0},{2,3},{3,2},{4,5},{5,4},{6,7},{7,6},{8,9},{9,8},{10,11... | collective-permute-start | bytes 11796488 | tf_op jit(solution)/shard_map/ppermute | solution.py:97
  937.3 123.4 %collective-permute-start.28 = (bf16[4,96,5120]{2,1,0:T(8,128)(2,1)}, bf16[4,96,5120]{2,1,0:T(8,128)(2,1)}, u32[]{:S(2)}, u32[]{:S(2)}) collective-permute-start(bf16[4,96,5120]{2,1,0:T(8,128)(2,1)} %get-tuple-element.357), channel_id=1, source_target_pairs={{0,1},{1,0},{2,3},{3,2},{4,5},{5,4},{6,7},{7,6},{8,9},{9,8},{10,11... | collective-permute-start | bytes 11796488 | tf_op jit(solution)/shard_map/ppermute | solution.py:97
  1045.1 17.0 collective-permute-start.35
  1051.6 51.2 %collective-permute-start.1 = (f32[96,2560]{1,0:T(8,128)}, f32[96,2560]{1,0:T(8,128)}, u32[]{:S(2)}, u32[]{:S(2)}) collective-permute-start(f32[96,2560]{1,0:T(8,128)} %get-tuple-element.228), channel_id=1, source_target_pairs={{0,2},{1,3},{2,4},{3,5},{4,6},{5,7},{6,0},{7,1},{8,10},{9,11},{10,... | collective-permute-start | bytes 2949128 | tf_op jit(solution)/shard_map/ppermute | solution.py:97
  1058.4 47.0 %collective-permute-start.2 = (f32[96,2560]{1,0:T(8,128)}, f32[96,2560]{1,0:T(8,128)}, u32[]{:S(2)}, u32[]{:S(2)}) collective-permute-start(f32[96,2560]{1,0:T(8,128)} %get-tuple-element.229), channel_id=1, source_target_pairs={{0,6},{1,7},{2,0},{3,1},{4,2},{5,3},{6,4},{7,5},{8,14},{9,15},{10,... | collective-permute-start | bytes 2949128 | tf_op jit(solution)/shard_map/ppermute | solution.py:97
  1060.6 193.0 %collective-permute-start.3 = (f32[96,2560]{1,0:T(8,128)}, f32[96,2560]{1,0:T(8,128)}, u32[]{:S(2)}, u32[]{:S(2)}) collective-permute-start(f32[96,2560]{1,0:T(8,128)} %convert_add_fusion.20), channel_id=1, source_target_pairs={{0,6},{1,7},{2,0},{3,1},{4,2},{5,3},{6,4},{7,5},{8,14},{9,15},{10,... | collective-permute-start | bytes 2949128 | tf_op jit(solution)/shard_map/ppermute | solution.py:97
  1060.7 193.0 %collective-permute-start.4 = (f32[96,2560]{1,0:T(8,128)}, f32[96,2560]{1,0:T(8,128)}, u32[]{:S(2)}, u32[]{:S(2)}) collective-permute-start(f32[96,2560]{1,0:T(8,128)} %convert_add_fusion.21), channel_id=1, source_target_pairs={{0,2},{1,3},{2,4},{3,5},{4,6},{5,7},{6,0},{7,1},{8,10},{9,11},{10,... | collective-permute-start | bytes 2949128 | tf_op jit(solution)/shard_map/ppermute | solution.py:97
  1062.0 56.2 %collective-permute-start.8 = (f32[96,2560]{1,0:T(8,128)}, f32[96,2560]{1,0:T(8,128)}, u32[]{:S(2)}, u32[]{:S(2)}) collective-permute-start(f32[96,2560]{1,0:T(8,128)} %get-tuple-element.263), channel_id=1, source_target_pairs={{0,2},{1,3},{2,4},{3,5},{4,6},{5,7},{6,0},{7,1},{8,10},{9,11},{10,... | collective-permute-start | bytes 2949128 | tf_op jit(solution)/shard_map/ppermute | solution.py:97
  1102.8 22.0 %collective-permute-start.9 = (f32[96,2560]{1,0:T(8,128)S(1)}, f32[96,2560]{1,0:T(8,128)S(1)}, u32[]{:S(2)}, u32[]{:S(2)}) collective-permute-start(f32[96,2560]{1,0:T(8,128)S(1)} %copy-done.62), channel_id=1, source_target_pairs={{0,6},{1,7},{2,0},{3,1},{4,2},{5,3},{6,4},{7,5},{8,14},{9,15},{10,... | collective-permute-start | bytes 2949128 | tf_op jit(solution)/shard_map/ppermute | solution.py:97
  1105.5 154.9 %collective-permute-start.10 = (f32[96,2560]{1,0:T(8,128)}, f32[96,2560]{1,0:T(8,128)}, u32[]{:S(2)}, u32[]{:S(2)}) collective-permute-start(f32[96,2560]{1,0:T(8,128)} %convert_add_fusion.16), channel_id=1, source_target_pairs={{0,6},{1,7},{2,0},{3,1},{4,2},{5,3},{6,4},{7,5},{8,14},{9,15},{10,... | collective-permute-start | bytes 2949128 | tf_op jit(solution)/shard_map/ppermute | solution.py:97
  1118.2 23.3 %collective-permute-start.15 = (f32[96,2560]{1,0:T(8,128)S(1)}, f32[96,2560]{1,0:T(8,128)S(1)}, u32[]{:S(2)}, u32[]{:S(2)}) collective-permute-start(f32[96,2560]{1,0:T(8,128)S(1)} %copy-done.68), channel_id=1, source_target_pairs={{0,2},{1,3},{2,4},{3,5},{4,6},{5,7},{6,0},{7,1},{8,10},{9,11},{10,... | collective-permute-start | bytes 2949128 | tf_op jit(solution)/shard_map/ppermute | solution.py:97
  1124.8 42.1 %collective-permute-start.16 = (f32[96,2560]{1,0:T(8,128)S(1)}, f32[96,2560]{1,0:T(8,128)S(1)}, u32[]{:S(2)}, u32[]{:S(2)}) collective-permute-start(f32[96,2560]{1,0:T(8,128)S(1)} %copy-done.65), channel_id=1, source_target_pairs={{0,6},{1,7},{2,0},{3,1},{4,2},{5,3},{6,4},{7,5},{8,14},{9,15},{10,... | collective-permute-start | bytes 2949128 | tf_op jit(solution)/shard_map/ppermute | solution.py:97
  1141.5 31.5 %collective-permute-start.22 = (f32[96,2560]{1,0:T(8,128)S(1)}, f32[96,2560]{1,0:T(8,128)S(1)}, u32[]{:S(2)}, u32[]{:S(2)}) collective-permute-start(f32[96,2560]{1,0:T(8,128)S(1)} %copy-done.67), channel_id=1, source_target_pairs={{0,2},{1,3},{2,4},{3,5},{4,6},{5,7},{6,0},{7,1},{8,10},{9,11},{10,... | collective-permute-start | bytes 2949128 | tf_op jit(solution)/shard_map/ppermute | solution.py:97
  1167.9 21.9 %collective-permute-start.23 = (f32[96,2560]{1,0:T(8,128)S(1)}, f32[96,2560]{1,0:T(8,128)S(1)}, u32[]{:S(2)}, u32[]{:S(2)}) collective-permute-start(f32[96,2560]{1,0:T(8,128)S(1)} %copy-done.64), channel_id=1, source_target_pairs={{0,6},{1,7},{2,0},{3,1},{4,2},{5,3},{6,4},{7,5},{8,14},{9,15},{10,... | collective-permute-start | bytes 2949128 | tf_op jit(solution)/shard_map/ppermute | solution.py:97
  1173.1 22.0 %collective-permute-start.29 = (f32[96,2560]{1,0:T(8,128)S(1)}, f32[96,2560]{1,0:T(8,128)S(1)}, u32[]{:S(2)}, u32[]{:S(2)}) collective-permute-start(f32[96,2560]{1,0:T(8,128)S(1)} %copy-done.66), channel_id=1, source_target_pairs={{0,2},{1,3},{2,4},{3,5},{4,6},{5,7},{6,0},{7,1},{8,10},{9,11},{10,... | collective-permute-start | bytes 2949128 | tf_op jit(solution)/shard_map/ppermute | solution.py:97
  1189.8 21.1 %collective-permute-start.30 = (f32[96,2560]{1,0:T(8,128)S(1)}, f32[96,2560]{1,0:T(8,128)S(1)}, u32[]{:S(2)}, u32[]{:S(2)}) collective-permute-start(f32[96,2560]{1,0:T(8,128)S(1)} %copy-done.63), channel_id=1, source_target_pairs={{0,6},{1,7},{2,0},{3,1},{4,2},{5,3},{6,4},{7,5},{8,14},{9,15},{10,... | collective-permute-start | bytes 2949128 | tf_op jit(solution)/shard_map/ppermute | solution.py:97
  1195.1 21.1 %collective-permute-start.36 = (f32[96,2560]{1,0:T(8,128)}, f32[96,2560]{1,0:T(8,128)S(1)}, u32[]{:S(2)}, u32[]{:S(2)}) collective-permute-start(f32[96,2560]{1,0:T(8,128)} %get-tuple-element.403), channel_id=1, source_target_pairs={{0,2},{1,3},{2,4},{3,5},{4,6},{5,7},{6,0},{7,1},{8,10},{9,11},{10,... | collective-permute-start | bytes 2949128 | tf_op jit(solution)/shard_map/ppermute | solution.py:97
  1210.9 20.5 %collective-permute-start.37 = (f32[96,2560]{1,0:T(8,128)}, f32[96,2560]{1,0:T(8,128)}, u32[]{:S(2)}, u32[]{:S(2)}) collective-permute-start(f32[96,2560]{1,0:T(8,128)} %get-tuple-element.404), channel_id=1, source_target_pairs={{0,6},{1,7},{2,0},{3,1},{4,2},{5,3},{6,4},{7,5},{8,14},{9,15},{10,... | collective-permute-start | bytes 2949128 | tf_op jit(solution)/shard_map/ppermute | solution.py:97
  1216.1 40.2 %collective-permute-start.5 = (f32[96,2560]{1,0:T(8,128)}, f32[96,2560]{1,0:T(8,128)}, u32[]{:S(2)}, u32[]{:S(2)}) collective-permute-start(f32[96,2560]{1,0:T(8,128)} %add_add_fusion.23), channel_id=1, source_target_pairs={{0,2},{1,3},{2,4},{3,5},{4,6},{5,7},{6,0},{7,1},{8,10},{9,11},{10,... | collective-permute-start | bytes 2949128 | tf_op jit(solution)/shard_map/ppermute | solution.py:97
  1231.4 24.9 %collective-permute-start.6 = (f32[96,2560]{1,0:T(8,128)}, f32[96,2560]{1,0:T(8,128)}, u32[]{:S(2)}, u32[]{:S(2)}) collective-permute-start(f32[96,2560]{1,0:T(8,128)} %add_add_fusion.22), channel_id=1, source_target_pairs={{0,6},{1,7},{2,0},{3,1},{4,2},{5,3},{6,4},{7,5},{8,14},{9,15},{10,... | collective-permute-start | bytes 2949128 | tf_op jit(solution)/shard_map/ppermute | solution.py:97
  1252.0 87.8 %copy-start.18 = (f32[96,2560]{1,0:T(8,128)S(1)}, f32[96,2560]{1,0:T(8,128)}, u32[]{:S(2)}) copy-start(f32[96,2560]{1,0:T(8,128)} %convert_add_fusion.5) | copy-start | bytes 2949124
  1252.0 104.4 %copy-start.17 = (f32[96,2560]{1,0:T(8,128)S(1)}, f32[96,2560]{1,0:T(8,128)}, u32[]{:S(2)}) copy-start(f32[96,2560]{1,0:T(8,128)} %convert_add_fusion) | copy-start | bytes 2949124
  1253.5 129.3 %copy-start.16 = (f32[96,2560]{1,0:T(8,128)S(1)}, f32[96,2560]{1,0:T(8,128)}, u32[]{:S(2)}) copy-start(f32[96,2560]{1,0:T(8,128)} %convert_add_fusion.1) | copy-start | bytes 2949124
  1253.6 18.6 %collective-permute-start.11 = (f32[96,2560]{1,0:T(8,128)S(1)}, f32[96,2560]{1,0:T(8,128)S(1)}, u32[]{:S(2)}, u32[]{:S(2)}) collective-permute-start(f32[96,2560]{1,0:T(8,128)S(1)} %copy-done.21), channel_id=1, source_target_pairs={{0,2},{1,3},{2,4},{3,5},{4,6},{5,7},{6,0},{7,1},{8,10},{9,11},{10,... | collective-permute-start | bytes 2949128 | tf_op jit(solution)/shard_map/ppermute | solution.py:97
  1253.7 43.9 %collective-permute-start.17 = (f32[96,2560]{1,0:T(8,128)S(1)}, f32[96,2560]{1,0:T(8,128)S(1)}, u32[]{:S(2)}, u32[]{:S(2)}) collective-permute-start(f32[96,2560]{1,0:T(8,128)S(1)} %copy-done.24), channel_id=1, source_target_pairs={{0,6},{1,7},{2,0},{3,1},{4,2},{5,3},{6,4},{7,5},{8,14},{9,15},{10,... | collective-permute-start | bytes 2949128 | tf_op jit(solution)/shard_map/ppermute | solution.py:97
  1256.3 36.9 %collective-permute-start.12 = (f32[96,2560]{1,0:T(8,128)S(1)}, f32[96,2560]{1,0:T(8,128)S(1)}, u32[]{:S(2)}, u32[]{:S(2)}) collective-permute-start(f32[96,2560]{1,0:T(8,128)S(1)} %copy-done.55), channel_id=1, source_target_pairs={{0,2},{1,3},{2,4},{3,5},{4,6},{5,7},{6,0},{7,1},{8,10},{9,11},{10,... | collective-permute-start | bytes 2949128 | tf_op jit(solution)/shard_map/ppermute | solution.py:97
  1256.4 36.8 %collective-permute-start.13 = (f32[96,2560]{1,0:T(8,128)S(1)}, f32[96,2560]{1,0:T(8,128)S(1)}, u32[]{:S(2)}, u32[]{:S(2)}) collective-permute-start(f32[96,2560]{1,0:T(8,128)S(1)} %copy-done.45), channel_id=1, source_target_pairs={{0,6},{1,7},{2,0},{3,1},{4,2},{5,3},{6,4},{7,5},{8,14},{9,15},{10,... | collective-permute-start | bytes 2949128 | tf_op jit(solution)/shard_map/ppermute | solution.py:97
  1260.4 53.9 %collective-permute-start.18 = (f32[96,2560]{1,0:T(8,128)S(1)}, f32[96,2560]{1,0:T(8,128)S(1)}, u32[]{:S(2)}, u32[]{:S(2)}) collective-permute-start(f32[96,2560]{1,0:T(8,128)S(1)} %copy-done.23), channel_id=1, source_target_pairs={{0,2},{1,3},{2,4},{3,5},{4,6},{5,7},{6,0},{7,1},{8,10},{9,11},{10,... | collective-permute-start | bytes 2949128 | tf_op jit(solution)/shard_map/ppermute | solution.py:97
  1272.1 67.6 %collective-permute-start.24 = (f32[96,2560]{1,0:T(8,128)S(1)}, f32[96,2560]{1,0:T(8,128)S(1)}, u32[]{:S(2)}, u32[]{:S(2)}) collective-permute-start(f32[96,2560]{1,0:T(8,128)S(1)} %copy-done.22), channel_id=1, source_target_pairs={{0,6},{1,7},{2,0},{3,1},{4,2},{5,3},{6,4},{7,5},{8,14},{9,15},{10,... | collective-permute-start | bytes 2949128 | tf_op jit(solution)/shard_map/ppermute | solution.py:97
  1293.2 42.1 %collective-permute-start.19 = (f32[96,2560]{1,0:T(8,128)}, f32[96,2560]{1,0:T(8,128)S(1)}, u32[]{:S(2)}, u32[]{:S(2)}) collective-permute-start(f32[96,2560]{1,0:T(8,128)} %add_add_fusion.15), channel_id=1, source_target_pairs={{0,2},{1,3},{2,4},{3,5},{4,6},{5,7},{6,0},{7,1},{8,10},{9,11},{10,... | collective-permute-start | bytes 2949128 | tf_op jit(solution)/shard_map/ppermute | solution.py:97
  1293.2 42.1 %collective-permute-start.20 = (f32[96,2560]{1,0:T(8,128)}, f32[96,2560]{1,0:T(8,128)S(1)}, u32[]{:S(2)}, u32[]{:S(2)}) collective-permute-start(f32[96,2560]{1,0:T(8,128)} %add_add_fusion.14), channel_id=1, source_target_pairs={{0,6},{1,7},{2,0},{3,1},{4,2},{5,3},{6,4},{7,5},{8,14},{9,15},{10,... | collective-permute-start | bytes 2949128 | tf_op jit(solution)/shard_map/ppermute | solution.py:97
  1297.6 58.8 %collective-permute-start.25 = (f32[96,2560]{1,0:T(8,128)S(1)}, f32[96,2560]{1,0:T(8,128)S(1)}, u32[]{:S(2)}, u32[]{:S(2)}) collective-permute-start(f32[96,2560]{1,0:T(8,128)S(1)} %copy-done.20), channel_id=1, source_target_pairs={{0,2},{1,3},{2,4},{3,5},{4,6},{5,7},{6,0},{7,1},{8,10},{9,11},{10,... | collective-permute-start | bytes 2949128 | tf_op jit(solution)/shard_map/ppermute | solution.py:97
  1314.3 68.5 %collective-permute-start.31 = (f32[96,2560]{1,0:T(8,128)S(1)}, f32[96,2560]{1,0:T(8,128)S(1)}, u32[]{:S(2)}, u32[]{:S(2)}) collective-permute-start(f32[96,2560]{1,0:T(8,128)S(1)} %copy-done.19), channel_id=1, source_target_pairs={{0,6},{1,7},{2,0},{3,1},{4,2},{5,3},{6,4},{7,5},{8,14},{9,15},{10,... | collective-permute-start | bytes 2949128 | tf_op jit(solution)/shard_map/ppermute | solution.py:97
  1335.3 126.5 %copy-start.27 = (f32[96,2560]{1,0:T(8,128)}, f32[96,2560]{1,0:T(8,128)S(1)}, u32[]{:S(2)}) copy-start(f32[96,2560]{1,0:T(8,128)S(1)} %collective-permute-done.19) | copy-start | bytes 2949124
  1335.3 42.1 %collective-permute-start.26 = (f32[96,2560]{1,0:T(8,128)}, f32[96,2560]{1,0:T(8,128)S(1)}, u32[]{:S(2)}, u32[]{:S(2)}) collective-permute-start(f32[96,2560]{1,0:T(8,128)} %add_add_fusion.11), channel_id=1, source_target_pairs={{0,2},{1,3},{2,4},{3,5},{4,6},{5,7},{6,0},{7,1},{8,10},{9,11},{10,... | collective-permute-start | bytes 2949128 | tf_op jit(solution)/shard_map/ppermute | solution.py:97
  1335.3 126.5 %copy-start.29 = (f32[96,2560]{1,0:T(8,128)}, f32[96,2560]{1,0:T(8,128)S(1)}, u32[]{:S(2)}) copy-start(f32[96,2560]{1,0:T(8,128)S(1)} %collective-permute-done.20) | copy-start | bytes 2949124
  1335.4 42.1 %collective-permute-start.27 = (f32[96,2560]{1,0:T(8,128)S(1)}, f32[96,2560]{1,0:T(8,128)S(1)}, u32[]{:S(2)}, u32[]{:S(2)}) collective-permute-start(f32[96,2560]{1,0:T(8,128)S(1)} %add_add_fusion.10), channel_id=1, source_target_pairs={{0,6},{1,7},{2,0},{3,1},{4,2},{5,3},{6,4},{7,5},{8,14},{9,15},{10,... | collective-permute-start | bytes 2949128 | tf_op jit(solution)/shard_map/ppermute | solution.py:97
  1339.8 58.8 %collective-permute-start.32 = (f32[96,2560]{1,0:T(8,128)S(1)}, f32[96,2560]{1,0:T(8,128)S(1)}, u32[]{:S(2)}, u32[]{:S(2)}) collective-permute-start(f32[96,2560]{1,0:T(8,128)S(1)} %copy-done.18), channel_id=1, source_target_pairs={{0,2},{1,3},{2,4},{3,5},{4,6},{5,7},{6,0},{7,1},{8,10},{9,11},{10,... | collective-permute-start | bytes 2949128 | tf_op jit(solution)/shard_map/ppermute | solution.py:97
  1356.4 105.4 %copy-start.31 = (f32[96,2560]{1,0:T(8,128)}, f32[96,2560]{1,0:T(8,128)S(1)}, u32[]{:S(2)}) copy-start(f32[96,2560]{1,0:T(8,128)S(1)} %collective-permute-done.25) | copy-start | bytes 2949124
  1356.4 65.2 %collective-permute-start.38 = (f32[96,2560]{1,0:T(8,128)S(1)}, f32[96,2560]{1,0:T(8,128)S(1)}, u32[]{:S(2)}, u32[]{:S(2)}) collective-permute-start(f32[96,2560]{1,0:T(8,128)S(1)} %copy-done.17), channel_id=1, source_target_pairs={{0,6},{1,7},{2,0},{3,1},{4,2},{5,3},{6,4},{7,5},{8,14},{9,15},{10,... | collective-permute-start | bytes 2949128 | tf_op jit(solution)/shard_map/ppermute | solution.py:97
  1377.5 84.4 %copy-start.36 = (f32[96,2560]{1,0:T(8,128)}, f32[96,2560]{1,0:T(8,128)S(1)}, u32[]{:S(2)}) copy-start(f32[96,2560]{1,0:T(8,128)S(1)} %collective-permute-done.26) | copy-start | bytes 2949124
  1377.5 42.1 %collective-permute-start.33 = (f32[96,2560]{1,0:T(8,128)S(1)}, f32[96,2560]{1,0:T(8,128)S(1)}, u32[]{:S(2)}, u32[]{:S(2)}) collective-permute-start(f32[96,2560]{1,0:T(8,128)S(1)} %add_add_fusion.7), channel_id=1, source_target_pairs={{0,2},{1,3},{2,4},{3,5},{4,6},{5,7},{6,0},{7,1},{8,10},{9,11},{10,... | collective-permute-start | bytes 2949128 | tf_op jit(solution)/shard_map/ppermute | solution.py:97
  1378.5 41.1 %collective-permute-start.34 = (f32[96,2560]{1,0:T(8,128)S(1)}, f32[96,2560]{1,0:T(8,128)S(1)}, u32[]{:S(2)}, u32[]{:S(2)}) collective-permute-start(f32[96,2560]{1,0:T(8,128)S(1)} %add_add_fusion.6), channel_id=1, source_target_pairs={{0,6},{1,7},{2,0},{3,1},{4,2},{5,3},{6,4},{7,5},{8,14},{9,15},{10,... | collective-permute-start | bytes 2949128 | tf_op jit(solution)/shard_map/ppermute | solution.py:97
  1382.8 57.8 %collective-permute-start.39 = (f32[96,2560]{1,0:T(8,128)S(1)}, f32[96,2560]{1,0:T(8,128)S(1)}, u32[]{:S(2)}, u32[]{:S(2)}) collective-permute-start(f32[96,2560]{1,0:T(8,128)S(1)} %copy-done.16), channel_id=1, source_target_pairs={{0,2},{1,3},{2,4},{3,5},{4,6},{5,7},{6,0},{7,1},{8,10},{9,11},{10,... | collective-permute-start | bytes 2949128 | tf_op jit(solution)/shard_map/ppermute | solution.py:97
  1398.5 63.2 %collective-permute-start.40 = (f32[96,2560]{1,0:T(8,128)S(1)}, f32[96,2560]{1,0:T(8,128)S(1)}, u32[]{:S(2)}, u32[]{:S(2)}) collective-permute-start(f32[96,2560]{1,0:T(8,128)S(1)} %add_add_fusion.3), channel_id=1, source_target_pairs={{0,2},{1,3},{2,4},{3,5},{4,6},{5,7},{6,0},{7,1},{8,10},{9,11},{10,... | collective-permute-start | bytes 2949128 | tf_op jit(solution)/shard_map/ppermute | solution.py:97
  1419.6 42.1 %collective-permute-start.41 = (f32[96,2560]{1,0:T(8,128)S(1)}, f32[96,2560]{1,0:T(8,128)S(1)}, u32[]{:S(2)}, u32[]{:S(2)}) collective-permute-start(f32[96,2560]{1,0:T(8,128)S(1)} %add_add_fusion.2), channel_id=1, source_target_pairs={{0,6},{1,7},{2,0},{3,1},{4,2},{5,3},{6,4},{7,5},{8,14},{9,15},{10,... | collective-permute-start | bytes 2949128 | tf_op jit(solution)/shard_map/ppermute | solution.py:97
  1475.7 94.0 %all-gather.22.cloned.1.call-start = ((), (), s32[]{:S(2)}) async-start(), calls=%async_computation.5 | async-start | bytes 8847360 | tf_op jit(solution)/shard_map/all_gather | solution.py:170
  1476.5 138.1 %all-gather.26.cloned.1.call-start = ((), (), s32[]{:S(2)}) async-start(), calls=%async_computation.7 | async-start | bytes 8847360 | tf_op jit(solution)/shard_map/all_gather | solution.py:170
  1477.2 182.6 %all-gather.30.cloned.1.call-start = ((), (), s32[]{:S(2)}) async-start(), calls=%async_computation.9 | async-start | bytes 8847360 | tf_op jit(solution)/shard_map/all_gather | solution.py:170
  1478.0 226.8 %all-gather.34.cloned.1.call-start = ((), (), s32[]{:S(2)}) async-start(), calls=%async_computation.11 | async-start | bytes 8847360 | tf_op jit(solution)/shard_map/all_gather | solution.py:170
  1478.6 271.2 %all-gather.38.cloned.1.call-start = ((), (), s32[]{:S(2)}) async-start(), calls=%async_computation.13 | async-start | bytes 8847360 | tf_op jit(solution)/shard_map/all_gather | solution.py:170
  (75 other events, 1380.4 us)
Sparse Core Ops, SparseCore 0:
  14.1 235.0 all-gather.13
  371.1 44.2 all-gather.15
  416.9 43.4 all-gather.19
  461.9 43.4 all-gather.23
  506.9 43.4 all-gather.27
  551.8 43.4 all-gather.31
  597.5 43.4 all-gather.35
  1475.8 48.6 all-gather.17
  1526.2 43.4 all-gather.21
  1571.1 43.4 all-gather.25
  1616.2 43.4 all-gather.29
  1661.2 43.4 all-gather.33
  1706.3 43.4 all-gather.37

commit v2 on v1

--- a/solution.py
+++ b/solution.py
@@ -8,7 +8,8 @@
 
 EPS = 1e-5
 ROPE_BASE = 10000.0
-CHUNK_SEQS = (4, 4, 4, 4, 4, 4)
+CHUNK_SEQS = (2, 4, 4, 4, 4, 4, 2)
+TILE = 48
 
 
 def rms_norm(rows, gain):
@@ -72,6 +73,47 @@
     )(o_rows, w_full, x_rows)
 
 
+def wide(ref):
+    return ref[0].astype(jnp.float32)
+
+
+def pieces_kernel(where_ref, far_a, far_b, far_c, far_d, up_a, up_b, down_a, down_b, plus_ref, minus_ref):
+    plus_ref[0] = wide(far_a) + wide(far_b)
+    plus_ref[1] = wide(up_a) + wide(up_b)
+    minus_ref[0] = wide(far_c) + wide(far_d)
+    minus_ref[1] = wide(down_a) + wide(down_b)
+
+
+def runs_kernel(where_ref, up_a, up_b, down_a, down_b, far_low, far_high, low_ref, high_ref):
+    low_ref[...] = wide(up_a) + wide(up_b) + far_low[0]
+    high_ref[...] = wide(down_a) + wide(down_b) + far_high[0]
+
+
+def final_kernel(where_ref, low_a, low_b, high_a, high_b, near_low, near_high, run_low, run_high, resid_ref, out_ref):
+    half = run_low.shape[1]
+    low = wide(low_a) + wide(low_b) + near_low[0] + run_low[...]
+    high = wide(high_a) + wide(high_b) + near_high[0] + run_high[...]
+    out_ref[:, :half] = (resid_ref[:, :half].astype(jnp.float32) + low).astype(jnp.bfloat16)
+    out_ref[:, half:] = (resid_ref[:, half:].astype(jnp.float32) + high).astype(jnp.bfloat16)
+
+
+def ring_call(kernel, where, operands, specs, out_shapes, out_specs, rows):
+    return pl.pallas_call(
+        kernel,
+        grid_spec=pltpu.PrefetchScalarGridSpec(num_scalar_prefetch=1, grid=(rows // TILE,), in_specs=specs, out_specs=out_specs),
+        out_shape=out_shapes,
+    )(where, *operands)
+
+
+def unwritten(shape, dtype):
+    return pl.pallas_call(
+        lambda out_ref: None,
+        out_specs=pl.BlockSpec(memory_space=pl.ANY),
+        out_shape=jax.ShapeDtypeStruct(shape, dtype),
+        name="unwritten",
+    )()
+
+
 def solution(mesh):
     tp_size = mesh.shape["tp"]
     cores = 2
@@ -83,50 +125,50 @@
     partner_perm = [(index, index ^ 1) for index in range(tp_size)]
 
     def places():
-        index = lax.axis_index("tp")
-        chip, core = lax.shift_right_logical(index, 1), index & 1
-        return [core, 1 - core] + [(chip + shift) & (chips - 1) for shift in (0, 1, 2, chips - 1)]
-
-    def reduce_rows(partial, resid_rows, where):
-        rows = resid_rows.shape[0]
-        width = partial.shape[-1]
+        chip = lax.shift_right_logical(lax.axis_index("tp"), 1)
+        return jnp.stack([(chip + shift) & (chips - 1) for shift in (0, 1, 2, chips - 1)]).astype(jnp.int32)
+
+    def reduce_rows(keep, give, resid_rows, where):
+        rows, width = resid_rows.shape
         half = width // 2
-        fence = lax.optimization_barrier
+        own, up, far, down = range(4)
+        low, high = 0, 1
 
         def move(piece, perm):
             return lax.ppermute(piece, "tp", perm)
 
-        def pick(array, axis, place):
-            begin = [0] * array.ndim
-            begin[axis] = place
-            size = list(array.shape)
-            size[axis] = 1
-            return lax.squeeze(lax.dynamic_slice(array, begin, size, allow_negative_indices=False), (axis,))
-
-        partial, where = fence((partial, where))
-        blocks = partial.reshape(chips, cores, rows, width)
-        keep, give = fence((pick(blocks, 1, where[0]), pick(blocks, 1, where[1])))
+        def at(place, side):
+            return pl.BlockSpec((1, TILE, half), lambda n, where_ref: (where_ref[place], n, side))
+
+        def part(side):
+            return pl.BlockSpec((1, TILE, half), lambda n, where_ref: (side, n, 0))
+
+        flat = pl.BlockSpec((TILE, half), lambda n, where_ref: (n, 0))
+        full = pl.BlockSpec((TILE, width), lambda n, where_ref: (n, 0))
+        message = jax.ShapeDtypeStruct((2, rows, half), jnp.float32)
+        message_spec = pl.BlockSpec((2, TILE, half), lambda n, where_ref: (0, n, 0))
+        running = jax.ShapeDtypeStruct((rows, half), jnp.float32)
+
         got = move(give, partner_perm)
-        low, high = slice(0, half), slice(half, width)
-
-        def both(place, columns):
-            return pick(keep, 0, place)[:, columns].astype(jnp.float32) + pick(got, 0, place)[:, columns].astype(jnp.float32)
-
-        keep, got, where = fence((keep, got, where))
-        pieces = fence((both(where[4], low), both(where[4], high), both(where[3], high), both(where[5], low)))
-        far_low = move(pieces[0], chip_perm(1))
-        far_high = move(pieces[1], chip_perm(-1))
-        near_high = move(pieces[2], chip_perm(1))
-        near_low = move(pieces[3], chip_perm(-1))
-        keep, got, where, far_low, far_high = fence((keep, got, where, far_low, far_high))
-        pieces = fence((both(where[3], low) + far_low, both(where[5], high) + far_high))
-        run_low = move(pieces[0], chip_perm(1))
-        run_high = move(pieces[1], chip_perm(-1))
-        keep, got, where, near_low, near_high, run_low, run_high = fence((keep, got, where, near_low, near_high, run_low, run_high))
-        sum_low = both(where[2], low) + near_low + run_low
-        sum_high = both(where[2], high) + near_high + run_high
-        summed = jnp.concatenate([sum_low, sum_high], axis=1)
-        return fence((resid_rows.astype(jnp.float32) + summed).astype(jnp.bfloat16))
+        plus, minus = ring_call(
+            pieces_kernel, where, [keep, got] * 4,
+            [at(far, low), at(far, low), at(far, high), at(far, high), at(up, high), at(up, high), at(down, low), at(down, low)],
+            [message, message], [message_spec, message_spec], rows,
+        )
+        plus = move(plus, chip_perm(1))
+        minus = move(minus, chip_perm(-1))
+        run_low, run_high = ring_call(
+            runs_kernel, where, [keep, got] * 2 + [plus, minus],
+            [at(up, low), at(up, low), at(down, high), at(down, high), part(0), part(0)],
+            [running, running], [flat, flat], rows,
+        )
+        run_low = move(run_low, chip_perm(1))
+        run_high = move(run_high, chip_perm(-1))
+        return ring_call(
+            final_kernel, where, [keep, got] * 2 + [minus, plus, run_low, run_high, resid_rows],
+            [at(own, low), at(own, low), at(own, high), at(own, high), part(1), part(1), flat, flat, full],
+            jax.ShapeDtypeStruct((rows, width), jnp.bfloat16), full, rows,
+        )
 
     def layer_shard(x, seq_lens, w_query, w_key, w_value, w_out, w_gate, w_up, w_down, attn_gain, mlp_gain, k_cache, v_cache):
         batch_size, seq_len, model_width = x.shape
@@ -155,18 +197,39 @@
 
         o_rows = lax.all_to_all(by_owner(attn_rows), "tp", 0, 0, tiled=True)
         x_rows = jnp.concatenate([lax.dynamic_slice_in_dim(x.reshape(all_rows, model_width), start + tp_index * (size // tp_size), size // tp_size, axis=0) for start, size in zip(starts, chunk_rows)], axis=0)
-        hidden_rows = out_project(o_rows, w_out_full, x_rows, 512)
-        normed_rows = rms_norm(hidden_rows, mlp_gain)
+        first = chunk_rows[0] // tp_size
+        fence = lax.optimization_barrier
+        hidden_first = out_project(o_rows[:, :first], w_out_full, x_rows[:first], 512)
+        normed_first, o_rest = fence((rms_norm(hidden_first, mlp_gain), o_rows[:, first:]))
+        hidden_rest = out_project(o_rest, w_out_full, x_rows[first:], 512)
+        hidden = [hidden_first, hidden_rest]
+        normed_parts = [normed_first, rms_norm(hidden_rest, mlp_gain)]
+        keep = hidden_first
         where = places()
-        y = jnp.zeros((all_rows, model_width), jnp.bfloat16)
-        for start, size in zip(starts, chunk_rows):
-            own = slice(start // tp_size, (start + size) // tp_size)
-            normed_mlp = lax.all_gather(normed_rows[own], "tp", axis=0, tiled=True)
+        core = lax.axis_index("tp") & 1
+        y = unwritten((all_rows, model_width), jnp.bfloat16)
+        for chunk, (start, size) in enumerate(zip(starts, chunk_rows)):
+            rows = size // tp_size
+            begin = start // tp_size - (first if chunk else 0)
+            own = slice(begin, begin + rows)
+            normed_mlp = lax.all_gather(normed_parts[min(chunk, 1)][own], "tp", axis=0, tiled=True)
+            if chunk:
+                normed_mlp, keep = fence((normed_mlp, keep))
             gate_pre = jnp.dot(normed_mlp, w_gate, preferred_element_type=jnp.float32)
             up_pre = jnp.dot(normed_mlp, w_up, preferred_element_type=jnp.float32)
             gated = (jax.nn.silu(gate_pre) * up_pre).astype(jnp.bfloat16)
-            mlp_part = jnp.dot(gated, w_down, preferred_element_type=jnp.float32).astype(jnp.bfloat16)
-            out_rows = reduce_rows(mlp_part, hidden_rows[own], where)
+
+            def down(which, gated):
+                blocks = gated.reshape(chips, cores, rows, gated.shape[1])
+                picked = lax.dynamic_slice(blocks, (0, which, 0, 0), (chips, 1, rows, gated.shape[1]), allow_negative_indices=False)
+                partial = jnp.dot(picked.reshape(chips * rows, gated.shape[1]), w_down, preferred_element_type=jnp.float32)
+                return partial.astype(jnp.bfloat16).reshape(chips, rows, model_width)
+
+            gated, core = fence((gated, core))
+            give = down(1 - core, gated)
+            gated, give, core = fence((gated, give, core))
+            keep = down(core, gated)
+            out_rows = reduce_rows(keep, give, hidden[min(chunk, 1)][own], where)
             y_chunk = lax.all_gather(out_rows, "tp", axis=0, tiled=True)
             y = lax.dynamic_update_slice(y, y_chunk, (start, 0))
         return y.reshape(batch_size, seq_len, model_width), k_cache_out, v_cache_out

time: 1770 us -> 1630 us (0.921)
  waiting for transfers between devices: 601 us -> 292 us
  matrix products: 725 us -> 859 us
  Pallas kernels: 44.3 us -> 150 us
  other arithmetic: 120 us -> 58.7 us
    all_gather x6 -> x7, waiting for transfers between devices: 219 us -> 0.01 us  [layer_shard(): y_chunk = lax.all_gather(out_rows, 'tp', axis=0, tiled=True)]
    dot_general x6 -> x14, matrix products: 197 us -> 291 us  [down(): jnp.dot(picked.reshape(chips * rows, gated.shape[1]), w_down, preferred_e...]
    pallas_call x0 -> x22, Pallas kernels: none -> 87.4 us  [the longest x21 87.4 us: ring_call(): pl.pallas_call(kernel, grid_spec=pltpu.PrefetchScalarGridSpec(num_scalar_...]
    squeeze x36 -> x0, local copies, waits for them, and re-layouts: 64 us -> none  [pick(): lax.squeeze(lax.dynamic_slice(array, begin, size, allow_negative_indices=...]
    add x36 -> x0, other arithmetic: 61.6 us -> none  [the longest x18 34.1 us: both(): pick(keep, 0, place)[:, columns].astype(jnp.float32)]
    ppermute x42 -> x35, waiting for transfers between devices: 282 us -> 235 us  [move(): return lax.ppermute(piece, 'tp', perm)]
    all_gather x6 -> x7, waiting for transfers between devices: 40.8 us -> 0.04 us  [layer_shard(): lax.all_gather(normed_parts[min(chunk, 1)][own], 'tp', axis=0, tiled=True)]
    dynamic_slice x0 -> x14, local copies, waits for them, and re-layouts: none -> 30.1 us  [down(): lax.dynamic_slice(blocks, (0, which, 0, 0), (chips, 1, rows, gated.shape[...]
  transfers between devices with their start and end apart: 56 -> 51, of which waited for: 25 -> 18; matrix products, arithmetic and copies ran while one was open for 58% -> 67% of each run, Pallas kernels for 0% -> 8%
where the time goes in v2:
time: 1630 us; the launch traced here: 1620 us
  matrix products  859 us (53%)
  waiting for transfers between devices  292 us (18%)
  local copies, waits for them, and re-layouts  197 us (12%)
  Pallas kernels  150 us (9%)
  other arithmetic  58.7 us (4%)
  starting transfers between devices  48 us (3%)
    dot_general x14, matrix products, down(): jnp.dot(picked.reshape(chips * rows, gated.shape[1]), w_down, preferred_e...  291 us
    ppermute x35, waiting for transfers between devices, move(): return lax.ppermute(piece, 'tp', perm)  235 us
    dot_general x7, matrix products, layer_shard(): up_pre = jnp.dot(normed_mlp, w_up, preferred_element_type=jnp.float32)  223 us
    dot_general x7, matrix products, layer_shard(): gate_pre = jnp.dot(normed_mlp, w_gate, preferred_element_type=jnp.float32)  222 us
    pallas_call x21, Pallas kernels, ring_call(): pl.pallas_call(kernel, grid_spec=pltpu.PrefetchScalarGridSpec(num_scalar_...  87.4 us
    pallas_call x2, Pallas kernels, out_project(): pl.pallas_call(out_kernel, grid=(width // tile,), in_specs=[pl.BlockSpec(...  62.4 us
    all_to_all x1, waiting for transfers between devices, layer_shard(): o_rows = lax.all_to_all(by_owner(attn_rows), 'tp', 0, 0, tiled=True)  53.7 us
    unnamed x109, local copies, waits for them, and re-layouts  45.4 us
  transfers between devices with their start and end apart: 51, of which 18 were waited for; matrix products, arithmetic and copies ran while one was open for 67% of the time, Pallas kernels for 8%

profile of v2, /device:TPU:113, one launch (start us, length us, event | category | flops | bytes accessed | tf_op | source)
XLA Modules:
  0.0 1619.5 jit_solution(12339591364247077952)
XLA Ops:
  12.2 20.4 %fusion = f32[24,192]{1,0:T(8,128)S(1)} fusion(bf16[24,192,5120]{2,1,0:T(8,128)(2,1)} %param.13), kind=kLoop, calls=%fused_computation.2 | loop fusion | flops 70774272 | bytes 47204352 | tf_op jit(solution)/shard_map/reduce_sum | solution.py:17
  32.6 23.4 %fusion.5 = f32[24,192,128]{2,1,0:T(8,128)} fusion(bf16[24,192,5120]{2,1,0:T(8,128)(2,1)} %param.13, f32[5120]{0:T(1024)S(1)} %convert_element_type.173, f32[24,192]{1,0:T(8,128)S(1)} %add_rsqrt_fusion, bf16[5120,128]{1,0:T(8,128)(2,1)S(1)} %copy-done.47), kind=kOutput, calls=%fused_computation.6 | convolution fusion | flops 6134169600 | bytes 50894848 | tf_op jit(solution)/shard_map/bsd,dk->bsk/dot_general | solution.py:185
  64.5 44.9 %fusion.3 = f32[24,192,640]{2,1,0:T(8,128)} fusion(bf16[24,192,5120]{2,1,0:T(8,128)(2,1)} %param.13, f32[5120]{0:T(1024)S(1)} %convert_element_type.173, f32[24,192]{1,0:T(8,128)S(1)} %add_rsqrt_fusion, bf16[5120,640]{1,0:T(8,128)(2,1)} %param.15), kind=kOutput, calls=%fused_computation.5 | convolution fusion | flops 30293360640 | bytes 65574912 | tf_op jit(solution)/shard_map/bsd,dk->bsk/dot_general | solution.py:184
  109.4 16.0 copy.28
  127.6 7.0 subtract_convert_fusion
  138.9 18.4 %fusion.10 = (f32[24,5,192]{2,1,0:T(8,128)S(1)}, f32[24,192,192,5]{2,1,3,0:T(8,128)}) fusion(pred[24,192,192]{1,2,0:T(8,128)(4,1)} %broadcast_and_fusion, bf16[24,192,5,128]{1,0,3,2:T(8,128)(2,1)} %bitcast.243, bf16[24,192,128]{2,1,0:T(8,128)(2,1)} %copy.27, pred[24,192]{1,0:T(8,128)(4,1)S(1)} %iota_compare_fusion.1), kind=kOutput, calls=%fused_computation.12 | convolution fusion | flops 1146299904 | bytes 25754112 | tf_op jit(solution)/shard_map/bqkgh,bskh->bkgqs/dot_general | solution.py:40
  157.3 11.0 fusion.9
  168.3 21.9 %bitcast_dynamic-update-slice_fusion = (bf16[24,384,1,128]{3,1,2,0:T(8,128)(2,1)}, bf16[24,192,128]{2,1,0:T(8,128)(2,1)}) fusion(bf16[24,384,1,128]{3,1,2,0:T(8,128)(2,1)} %copy.70, bf16[5120,128]{1,0:T(8,128)(2,1)S(1)} %copy-done, bf16[24,192,5120]{2,1,0:T(8,128)(2,1)} %param.13, f32[5120]{0:T(1024)S(1)} %convert_element_type.173, ...), kind=kOutput, calls=%fused_computation.61 | convolution fusion | flops 6135349248 | bytes 50899456 | tf_op jit(solution)/shard_map/bsd,dk->bsk/dot_general | solution.py:186
  190.2 14.1 convert_bitcast_fusion
  245.7 7.0 all-to-all-start
  266.0 53.7 %all-to-all-done = bf16[8,576,640]{2,1,0:T(8,128)(2,1)} async-done(((bf16[8,576,640]{2,1,0:T(8,128)(2,1)}), bf16[8,576,640]{2,1,0:T(8,128)(2,1)}, u32[]{:S(2)}, u32[]{:S(2)}) %all-to-all-start) | async-done | bytes 5898272 | tf_op jit(solution)/shard_map/all_to_all | solution.py:198
  321.5 5.4 slice.119.o_ref
  327.0 20.9 %out_project.2.resid_ref = bf16[48,5120]{1,0:T(8,128)(2,1)} custom-call(bf16[8,48,640]{2,1,0:T(8,128)(2,1)} %slice.118.o_ref, bf16[5120,5120]{1,0:T(8,128)(2,1)} %all-gather.16.cloned.1.call-done.w_ref, bf16[48,5120]{1,0:T(8,128)(2,1)} %get-tuple-element.146.x_ref), custom_call_target="tpu_custom_call" | custom-call | flops 2516582400 | bytes 52428800 | tf_op jit(solution)/shard_map/out_project/pallas_call | solution.py:60
  351.3 41.5 %out_project.3 = bf16[528,5120]{1,0:T(8,128)(2,1)} custom-call(bf16[8,528,640]{2,1,0:T(8,128)(2,1)} %slice.119.o_ref, bf16[5120,5120]{1,0:T(8,128)(2,1)} %all-gather.16.cloned.1.call-done.w_ref, bf16[528,5120]{1,0:T(8,128)(2,1)} %get-tuple-element.145.x_ref), custom_call_target="tpu_custom_call" | custom-call | flops 27682406400 | bytes 52428800 | tf_op jit(solution)/shard_map/out_project/pallas_call | solution.py:60
  409.0 23.0 %fusion.48 = f32[384,3456]{1,0:T(8,128)S(1)} fusion(bf16[384,5120]{1,0:T(8,128)(2,1)} %all-gather.18.cloned.1.call-done, bf16[5120,3456]{1,0:T(8,128)(2,1)} %param.19), kind=kOutput, calls=%fused_computation.124 | convolution fusion | flops 13589544960 | bytes 44630016 | tf_op jit(solution)/shard_map/dot_general | solution.py:218
  432.1 21.6 %fusion.20 = bf16[384,3456]{1,0:T(8,128)(2,1)} fusion(bf16[384,5120]{1,0:T(8,128)(2,1)S(1)} %copy-done.46, bf16[5120,3456]{1,0:T(8,128)(2,1)} %param.20, f32[384,3456]{1,0:T(8,128)S(1)} %fusion.48), kind=kOutput, calls=%fused_computation.49 | convolution fusion | flops 13597507584 | bytes 47284224 | tf_op jit(solution)/shard_map/dot_general | solution.py:219
  455.2 15.8 convolution_convert_fusion.13
  471.8 16.6 %convolution_convert_fusion.12 = bf16[192,5120]{1,0:T(8,128)(2,1)} fusion(bf16[192,3456]{1,0:T(8,128)(2,1)S(1)} %bitcast.270, bf16[3456,5120]{1,0:T(8,128)(2,1)} %param.21), kind=kOutput, calls=%fused_computation.44 | convolution fusion | flops 6795755520 | bytes 38682624 | tf_op jit(solution)/shard_map/dot_general | solution.py:225
  495.2 36.1 %collective-permute-done.1.far_high.near_low = f32[2,48,2560]{2,1,0:T(8,128)S(1)} collective-permute-done((f32[2,48,2560]{2,1,0:T(8,128)}, f32[2,48,2560]{2,1,0:T(8,128)S(1)}, u32[]{:S(2)}, u32[]{:S(2)}) %collective-permute-start.1) | collective-permute-done | bytes 983072 | tf_op jit(solution)/shard_map/ppermute | solution.py:138
  541.8 4.9 fusion.46
  546.6 14.8 collective-permute-done.3.run_low
  566.9 34.7 %fusion.49 = f32[768,3456]{1,0:T(8,128)S(1)} fusion(bf16[768,5120]{1,0:T(8,128)(2,1)} %all-gather.22.cloned.1.call-done, bf16[5120,3456]{1,0:T(8,128)(2,1)} %param.19), kind=kOutput, calls=%fused_computation.125 | convolution fusion | flops 27179089920 | bytes 53870592 | tf_op jit(solution)/shard_map/dot_general | solution.py:218
  601.6 34.4 %multiply_convert_fusion.4 = bf16[768,3456]{1,0:T(8,128)(2,1)} fusion(f32[768,3456]{1,0:T(8,128)S(1)} %fusion.49, bf16[768,5120]{1,0:T(8,128)(2,1)S(1)} %copy-done.44, bf16[5120,3456]{1,0:T(8,128)(2,1)} %param.20), kind=kOutput, calls=%fused_computation.25 | convolution fusion | flops 27195015168 | bytes 59179008 | tf_op jit(solution)/shard_map/dot_general | solution.py:219
  638.1 22.3 %convolution_convert_fusion.9 = bf16[384,5120]{1,0:T(8,128)(2,1)} fusion(bf16[384,3456]{1,0:T(8,128)(2,1)S(1)} %bitcast.263, bf16[3456,5120]{1,0:T(8,128)(2,1)} %param.21), kind=kOutput, calls=%fused_computation.40 | convolution fusion | flops 13591511040 | bytes 41975808 | tf_op jit(solution)/shard_map/dot_general | solution.py:225
  662.3 22.6 %convolution_convert_fusion.8 = bf16[384,5120]{1,0:T(8,128)(2,1)} fusion(bf16[384,3456]{1,0:T(8,128)(2,1)S(1)} %bitcast.264, bf16[3456,5120]{1,0:T(8,128)(2,1)} %param.21), kind=kOutput, calls=%fused_computation.39 | convolution fusion | flops 13591511040 | bytes 41975808 | tf_op jit(solution)/shard_map/dot_general | solution.py:225
  684.9 34.2 %fusion.50 = f32[768,3456]{1,0:T(8,128)S(1)} fusion(bf16[768,5120]{1,0:T(8,128)(2,1)} %all-gather.26.cloned.1.call-done, bf16[5120,3456]{1,0:T(8,128)(2,1)} %param.19), kind=kOutput, calls=%fused_computation.126 | convolution fusion | flops 27179089920 | bytes 53870592 | tf_op jit(solution)/shard_map/dot_general | solution.py:218
  720.2 34.4 %multiply_convert_fusion.3 = bf16[768,3456]{1,0:T(8,128)(2,1)} fusion(f32[768,3456]{1,0:T(8,128)S(1)} %fusion.50, bf16[768,5120]{1,0:T(8,128)(2,1)S(1)} %copy-done.43, bf16[5120,3456]{1,0:T(8,128)(2,1)} %param.20), kind=kOutput, calls=%fused_computation.24 | convolution fusion | flops 27195015168 | bytes 59179008 | tf_op jit(solution)/shard_map/dot_general | solution.py:219
  763.9 23.1 %convolution_convert_fusion.7 = bf16[384,5120]{1,0:T(8,128)(2,1)} fusion(bf16[384,3456]{1,0:T(8,128)(2,1)} %bitcast.258, bf16[3456,5120]{1,0:T(8,128)(2,1)} %param.21), kind=kOutput, calls=%fused_computation.38 | convolution fusion | flops 13591511040 | bytes 41975808 | tf_op jit(solution)/shard_map/dot_general | solution.py:225
  790.4 16.6 %collective-permute-done.6.far_high.near_low = f32[2,96,2560]{2,1,0:T(8,128)S(1)} collective-permute-done((f32[2,96,2560]{2,1,0:T(8,128)}, f32[2,96,2560]{2,1,0:T(8,128)S(1)}, u32[]{:S(2)}, u32[]{:S(2)}) %collective-permute-start.6) | collective-permute-done | bytes 1966112 | tf_op jit(solution)/shard_map/ppermute | solution.py:138
  815.0 22.6 %convolution_convert_fusion.6 = bf16[384,5120]{1,0:T(8,128)(2,1)} fusion(bf16[384,3456]{1,0:T(8,128)(2,1)} %bitcast.256, bf16[3456,5120]{1,0:T(8,128)(2,1)} %param.21), kind=kOutput, calls=%fused_computation.37 | convolution fusion | flops 13591511040 | bytes 41975808 | tf_op jit(solution)/shard_map/dot_general | solution.py:225
  840.4 4.8 shard_map.153
  845.3 35.9 %fusion.51 = f32[768,3456]{1,0:T(8,128)} fusion(bf16[768,5120]{1,0:T(8,128)(2,1)} %all-gather.30.cloned.1.call-done, bf16[5120,3456]{1,0:T(8,128)(2,1)} %param.19), kind=kOutput, calls=%fused_computation.127 | convolution fusion | flops 27179089920 | bytes 53870592 | tf_op jit(solution)/shard_map/dot_general | solution.py:218
  887.0 37.0 %multiply_convert_fusion.2 = bf16[768,3456]{1,0:T(8,128)(2,1)} fusion(f32[768,3456]{1,0:T(8,128)} %fusion.51, bf16[768,5120]{1,0:T(8,128)(2,1)} %all-gather.30.cloned.1.call-done, bf16[5120,3456]{1,0:T(8,128)(2,1)} %param.20), kind=kOutput, calls=%fused_computation.23 | convolution fusion | flops 27195015168 | bytes 59179008 | tf_op jit(solution)/shard_map/dot_general | solution.py:219
  938.1 22.6 %convolution_convert_fusion.5 = bf16[384,5120]{1,0:T(8,128)(2,1)} fusion(bf16[384,3456]{1,0:T(8,128)(2,1)} %bitcast.257, bf16[3456,5120]{1,0:T(8,128)(2,1)} %param.21), kind=kOutput, calls=%fused_computation.36 | convolution fusion | flops 13591511040 | bytes 41975808 | tf_op jit(solution)/shard_map/dot_general | solution.py:225
  966.9 4.8 shard_map.156
  971.8 24.2 %convolution_convert_fusion.4 = bf16[384,5120]{1,0:T(8,128)(2,1)} fusion(bf16[384,3456]{1,0:T(8,128)(2,1)} %bitcast.254, bf16[3456,5120]{1,0:T(8,128)(2,1)} %param.21), kind=kOutput, calls=%fused_computation.35 | convolution fusion | flops 13591511040 | bytes 41975808 | tf_op jit(solution)/shard_map/dot_general | solution.py:225
  996.0 4.6 shard_map.157
  1002.0 35.6 %fusion.52 = f32[768,3456]{1,0:T(8,128)} fusion(bf16[768,5120]{1,0:T(8,128)(2,1)} %all-gather.34.cloned.1.call-done, bf16[5120,3456]{1,0:T(8,128)(2,1)} %param.19), kind=kOutput, calls=%fused_computation.128 | convolution fusion | flops 27179089920 | bytes 53870592 | tf_op jit(solution)/shard_map/dot_general | solution.py:218
  1037.6 16.3 %collective-permute-done.16.far_high.near_low = f32[2,96,2560]{2,1,0:T(8,128)S(1)} collective-permute-done((f32[2,96,2560]{2,1,0:T(8,128)}, f32[2,96,2560]{2,1,0:T(8,128)S(1)}, u32[]{:S(2)}, u32[]{:S(2)}) %collective-permute-start.16) | collective-permute-done | bytes 1966112 | tf_op jit(solution)/shard_map/ppermute | solution.py:138
  1061.8 36.9 %multiply_convert_fusion.1 = bf16[768,3456]{1,0:T(8,128)(2,1)} fusion(f32[768,3456]{1,0:T(8,128)} %fusion.52, bf16[768,5120]{1,0:T(8,128)(2,1)} %all-gather.34.cloned.1.call-done, bf16[5120,3456]{1,0:T(8,128)(2,1)} %param.20), kind=kOutput, calls=%fused_computation.22 | convolution fusion | flops 27195015168 | bytes 59179008 | tf_op jit(solution)/shard_map/dot_general | solution.py:219
  1103.5 4.8 shard_map.159
  1108.3 23.7 %convolution_convert_fusion.3 = bf16[384,5120]{1,0:T(8,128)(2,1)} fusion(bf16[384,3456]{1,0:T(8,128)(2,1)} %bitcast.255, bf16[3456,5120]{1,0:T(8,128)(2,1)} %param.21), kind=kOutput, calls=%fused_computation.34 | convolution fusion | flops 13591511040 | bytes 41975808 | tf_op jit(solution)/shard_map/dot_general | solution.py:225
  1135.5 22.4 %convolution_convert_fusion.2 = bf16[384,5120]{1,0:T(8,128)(2,1)} fusion(bf16[384,3456]{1,0:T(8,128)(2,1)S(1)} %bitcast.265, bf16[3456,5120]{1,0:T(8,128)(2,1)} %param.21), kind=kOutput, calls=%fused_computation.33 | convolution fusion | flops 13591511040 | bytes 41975808 | tf_op jit(solution)/shard_map/dot_general | solution.py:225
  1163.8 43.2 %collective-permute-done.21.far_high.near_low = f32[2,96,2560]{2,1,0:T(8,128)S(1)} collective-permute-done((f32[2,96,2560]{2,1,0:T(8,128)}, f32[2,96,2560]{2,1,0:T(8,128)S(1)}, u32[]{:S(2)}, u32[]{:S(2)}) %collective-permute-start.21) | collective-permute-done | bytes 1966112 | tf_op jit(solution)/shard_map/ppermute | solution.py:138
  1214.9 35.5 %fusion.53 = f32[768,3456]{1,0:T(8,128)} fusion(bf16[768,5120]{1,0:T(8,128)(2,1)} %all-gather.38.cloned.1.call-done, bf16[5120,3456]{1,0:T(8,128)(2,1)} %param.19), kind=kOutput, calls=%fused_computation.129 | convolution fusion | flops 27179089920 | bytes 53870592 | tf_op jit(solution)/shard_map/dot_general | solution.py:218
  1251.6 4.8 shard_map.162
  1256.5 37.5 %multiply_convert_fusion = bf16[768,3456]{1,0:T(8,128)(2,1)} fusion(f32[768,3456]{1,0:T(8,128)} %fusion.53, bf16[768,5120]{1,0:T(8,128)(2,1)} %all-gather.38.cloned.1.call-done, bf16[5120,3456]{1,0:T(8,128)(2,1)} %param.20), kind=kOutput, calls=%fused_computation.21 | convolution fusion | flops 27195015168 | bytes 59179008 | tf_op jit(solution)/shard_map/dot_general | solution.py:219
  1296.0 22.2 %convolution_convert_fusion.1 = bf16[384,5120]{1,0:T(8,128)(2,1)} fusion(bf16[384,3456]{1,0:T(8,128)(2,1)S(1)} %bitcast.266, bf16[3456,5120]{1,0:T(8,128)(2,1)} %param.21), kind=kOutput, calls=%fused_computation.32 | convolution fusion | flops 13591511040 | bytes 41975808 | tf_op jit(solution)/shard_map/dot_general | solution.py:225
  1322.1 22.0 %convolution_convert_fusion = bf16[384,5120]{1,0:T(8,128)(2,1)} fusion(bf16[384,3456]{1,0:T(8,128)(2,1)S(1)} %bitcast.267, bf16[3456,5120]{1,0:T(8,128)(2,1)} %param.21), kind=kOutput, calls=%fused_computation.31 | convolution fusion | flops 13591511040 | bytes 41975808 | tf_op jit(solution)/shard_map/dot_general | solution.py:225
  1350.1 43.2 %collective-permute-done.26.far_high.near_low = f32[2,96,2560]{2,1,0:T(8,128)S(1)} collective-permute-done((f32[2,96,2560]{2,1,0:T(8,128)}, f32[2,96,2560]{2,1,0:T(8,128)S(1)}, u32[]{:S(2)}, u32[]{:S(2)}) %collective-permute-start.26) | collective-permute-done | bytes 1966112 | tf_op jit(solution)/shard_map/ppermute | solution.py:138
  1401.3 21.2 %collective-permute-done.28.run_low = f32[96,2560]{1,0:T(8,128)S(1)} collective-permute-done((f32[96,2560]{1,0:T(8,128)}, f32[96,2560]{1,0:T(8,128)S(1)}, u32[]{:S(2)}, u32[]{:S(2)}) %collective-permute-start.28) | collective-permute-done | bytes 983072 | tf_op jit(solution)/shard_map/ppermute | solution.py:138
  1423.8 4.8 shard_map.165
  1428.7 23.3 %fusion.54 = f32[384,3456]{1,0:T(8,128)S(1)} fusion(bf16[384,5120]{1,0:T(8,128)(2,1)} %all-gather.42.cloned.1.call-done, bf16[5120,3456]{1,0:T(8,128)(2,1)} %param.19), kind=kOutput, calls=%fused_computation.130 | convolution fusion | flops 13589544960 | bytes 44630016 | tf_op jit(solution)/shard_map/dot_general | solution.py:218
  1452.1 21.5 %fusion.21 = bf16[384,3456]{1,0:T(8,128)(2,1)} fusion(bf16[384,5120]{1,0:T(8,128)(2,1)S(1)} %copy-done.45, bf16[5120,3456]{1,0:T(8,128)(2,1)} %param.20, f32[384,3456]{1,0:T(8,128)S(1)} %fusion.54), kind=kOutput, calls=%fused_computation.50 | convolution fusion | flops 13597507584 | bytes 47284224 | tf_op jit(solution)/shard_map/dot_general | solution.py:219
  1475.0 14.9 convolution_convert_fusion.11
  1491.9 16.1 convolution_convert_fusion.10
  1515.2 21.4 %collective-permute-done.31.far_high.near_low = f32[2,48,2560]{2,1,0:T(8,128)S(1)} collective-permute-done((f32[2,48,2560]{2,1,0:T(8,128)}, f32[2,48,2560]{2,1,0:T(8,128)S(1)}, u32[]{:S(2)}, u32[]{:S(2)}) %collective-permute-start.31) | collective-permute-done | bytes 983072 | tf_op jit(solution)/shard_map/ppermute | solution.py:138
  1548.4 8.5 collective-permute-done.33.run_low
  1568.5 4.5 constant_dynamic-update-slice_fusion.14
  1573.0 7.1 constant_dynamic-update-slice_fusion.13
  1580.0 7.1 constant_dynamic-update-slice_fusion.12
  1587.2 7.1 constant_dynamic-update-slice_fusion.11
  1594.2 7.0 constant_dynamic-update-slice_fusion.10
  1601.2 7.1 constant_dynamic-update-slice_fusion.9
  (292 shorter events, 268.0 us)
Async XLA Ops:
  7.2 161.1 %copy-start = (bf16[5120,128]{1,0:T(8,128)(2,1)S(1)}, bf16[5120,128]{1,0:T(8,128)(2,1)}, u32[]{:S(2)}) copy-start(bf16[5120,128]{1,0:T(8,128)(2,1)} %param.17) | copy-start | bytes 3932164
  7.2 319.8 %all-gather.16.cloned.1.call-start = ((), (), s32[]{:S(2)}) async-start(), calls=%async_computation.1 | async-start | bytes 58982400 | tf_op jit(solution)/shard_map/all_gather | solution.py:182
  12.2 20.4 %copy-start.47 = (bf16[5120,128]{1,0:T(8,128)(2,1)S(1)}, bf16[5120,128]{1,0:T(8,128)(2,1)}, u32[]{:S(2)}) copy-start(bf16[5120,128]{1,0:T(8,128)(2,1)} %param.16) | copy-start | bytes 3932164
  62.6 46.8 %copy-start.6 = (bf16[24,192,1,64,2]{1,0,4,3,2:T(8,128)(2,1)}, bf16[24,192,1,64,2]{1,0,4,3,2:T(8,128)(2,1)S(1)}, u32[]{:S(2)}) copy-start(bf16[24,192,1,64,2]{1,0,4,3,2:T(8,128)(2,1)S(1)} %maximum_convert_fusion) | copy-start | bytes 3538948
  109.4 16.0 copy-start.42
  125.5 42.8 %copy-start.38 = (pred[24,192]{1,0:T(8,128)(4,1)}, pred[24,192]{1,0:T(8,128)(4,1)S(1)}, u32[]{:S(2)}) copy-start(pred[24,192]{1,0:T(8,128)(4,1)S(1)} %iota_compare_fusion.1) | copy-start | bytes 13828
  138.9 18.4 %copy-start.13 = (pred[24,192,192]{1,2,0:T(8,128)(4,1)S(1)}, pred[24,192,192]{1,2,0:T(8,128)(4,1)}, u32[]{:S(2)}) copy-start(pred[24,192,192]{1,2,0:T(8,128)(4,1)} %broadcast_and_fusion) | copy-start | bytes 2654212
  230.6 13.2 copy-start.19
  245.7 74.0 %all-to-all-start = ((bf16[8,576,640]{2,1,0:T(8,128)(2,1)}), bf16[8,576,640]{2,1,0:T(8,128)(2,1)}, u32[]{:S(2)}, u32[]{:S(2)}) async-start(bf16[8,576,640]{2,1,0:T(8,128)(2,1)} %constant_dynamic-update-slice_fusion), calls=%async_computation | async-start | bytes 11796480 | tf_op jit(solution)/shard_map/all_to_all | solution.py:198
  252.6 156.4 %all-gather.18.cloned.1.call-start = ((), (), s32[]{:S(2)}) async-start(), calls=%async_computation.2 | async-start | bytes 4423680 | tf_op jit(solution)/shard_map/all_gather | solution.py:215
  351.2 215.7 %all-gather.22.cloned.1.call-start = ((), (), s32[]{:S(2)}) async-start(), calls=%async_computation.4 | async-start | bytes 8847360 | tf_op jit(solution)/shard_map/all_gather | solution.py:215
  403.6 281.3 %all-gather.26.cloned.1.call-start = ((), (), s32[]{:S(2)}) async-start(), calls=%async_computation.6 | async-start | bytes 8847360 | tf_op jit(solution)/shard_map/all_gather | solution.py:215
  404.2 433.4 %all-gather.30.cloned.1.call-start = ((), (), s32[]{:S(2)}) async-start(), calls=%async_computation.8 | async-start | bytes 8847360 | tf_op jit(solution)/shard_map/all_gather | solution.py:215
  404.8 591.1 %all-gather.34.cloned.1.call-start = ((), (), s32[]{:S(2)}) async-start(), calls=%async_computation.10 | async-start | bytes 8847360 | tf_op jit(solution)/shard_map/all_gather | solution.py:215
  405.5 758.3 %all-gather.38.cloned.1.call-start = ((), (), s32[]{:S(2)}) async-start(), calls=%async_computation.12 | async-start | bytes 8847360 | tf_op jit(solution)/shard_map/all_gather | solution.py:215
  406.3 995.0 %all-gather.42.cloned.1.call-start = ((), (), s32[]{:S(2)}) async-start(), calls=%async_computation.14 | async-start | bytes 4423680 | tf_op jit(solution)/shard_map/all_gather | solution.py:215
  408.9 1159.6 %all-gather.20.cloned.1.call-start = ((), (), s32[]{:S(2)}) async-start(), calls=%async_computation.3 | async-start | bytes 4423680 | tf_op jit(solution)/shard_map/all_gather | solution.py:233
  409.0 23.1 %copy-start.46 = (bf16[384,5120]{1,0:T(8,128)(2,1)S(1)}, bf16[384,5120]{1,0:T(8,128)(2,1)}, u32[]{:S(2)}) copy-start(bf16[384,5120]{1,0:T(8,128)(2,1)} %all-gather.18.cloned.1.call-done) | copy-start | bytes 11796484
  455.2 16.6 %copy-start.21 = (bf16[384,3456]{1,0:T(8,128)(2,1)S(1)}, bf16[384,3456]{1,0:T(8,128)(2,1)}, u32[]{:S(2)}) copy-start(bf16[384,3456]{1,0:T(8,128)(2,1)} %fusion.20) | copy-start | bytes 7962628
  471.1 17.4 %collective-permute-start = (bf16[4,48,5120]{2,1,0:T(8,128)(2,1)S(1)}, bf16[4,48,5120]{2,1,0:T(8,128)(2,1)S(1)}, u32[]{:S(2)}, u32[]{:S(2)}) collective-permute-start(bf16[4,48,5120]{2,1,0:T(8,128)(2,1)S(1)} %bitcast.277), channel_id=1, source_target_pairs={{0,1},{1,0},{2,3},{3,2},{4,5},{5,4},{6,7},{7,6},{8,9},{9,8},{10,11... | collective-permute-start | bytes 5898248 | tf_op jit(solution)/shard_map/ppermute | solution.py:138
  493.5 37.8 %collective-permute-start.1 = (f32[2,48,2560]{2,1,0:T(8,128)}, f32[2,48,2560]{2,1,0:T(8,128)S(1)}, u32[]{:S(2)}, u32[]{:S(2)}) collective-permute-start(f32[2,48,2560]{2,1,0:T(8,128)} %get-tuple-element.80), channel_id=1, source_target_pairs={{0,6},{1,7},{2,0},{3,1},{4,2},{5,3},{6,4},{7,5},{8,14},{9,15},{10,... | collective-permute-start | bytes 2949128 | tf_op jit(solution)/shard_map/ppermute | solution.py:138
  495.2 39.5 %collective-permute-start.2 = (f32[2,48,2560]{2,1,0:T(8,128)}, f32[2,48,2560]{2,1,0:T(8,128)S(1)}, u32[]{:S(2)}, u32[]{:S(2)}) collective-permute-start(f32[2,48,2560]{2,1,0:T(8,128)} %get-tuple-element.81), channel_id=1, source_target_pairs={{0,2},{1,3},{2,4},{3,5},{4,6},{5,7},{6,0},{7,1},{8,10},{9,11},{10,... | collective-permute-start | bytes 2949128 | tf_op jit(solution)/shard_map/ppermute | solution.py:138
  539.1 22.4 %collective-permute-start.3 = (f32[48,2560]{1,0:T(8,128)}, f32[48,2560]{1,0:T(8,128)S(1)}, u32[]{:S(2)}, u32[]{:S(2)}) collective-permute-start(f32[48,2560]{1,0:T(8,128)} %get-tuple-element.82), channel_id=1, source_target_pairs={{0,2},{1,3},{2,4},{3,5},{4,6},{5,7},{6,0},{7,1},{8,10},{9,11},{10,... | collective-permute-start | bytes 1474568 | tf_op jit(solution)/shard_map/ppermute | solution.py:138
  539.1 22.4 %collective-permute-start.4 = (f32[48,2560]{1,0:T(8,128)}, f32[48,2560]{1,0:T(8,128)S(1)}, u32[]{:S(2)}, u32[]{:S(2)}) collective-permute-start(f32[48,2560]{1,0:T(8,128)} %get-tuple-element.83), channel_id=1, source_target_pairs={{0,6},{1,7},{2,0},{3,1},{4,2},{5,3},{6,4},{7,5},{8,14},{9,15},{10,... | collective-permute-start | bytes 1474568 | tf_op jit(solution)/shard_map/ppermute | solution.py:138
  566.8 1006.2 %all-gather.24.cloned.1.call-start = ((), (), s32[]{:S(2)}) async-start(), calls=%async_computation.5 | async-start | bytes 8847360 | tf_op jit(solution)/shard_map/all_gather | solution.py:233
  566.9 34.7 %copy-start.44 = (bf16[768,5120]{1,0:T(8,128)(2,1)S(1)}, bf16[768,5120]{1,0:T(8,128)(2,1)}, u32[]{:S(2)}) copy-start(bf16[768,5120]{1,0:T(8,128)(2,1)} %all-gather.22.cloned.1.call-done) | copy-start | bytes 23592964
  684.9 35.3 %copy-start.43 = (bf16[768,5120]{1,0:T(8,128)(2,1)S(1)}, bf16[768,5120]{1,0:T(8,128)(2,1)}, u32[]{:S(2)}) copy-start(bf16[768,5120]{1,0:T(8,128)(2,1)} %all-gather.26.cloned.1.call-done) | copy-start | bytes 23592964
  719.1 38.9 %collective-permute-start.5 = (bf16[4,96,5120]{2,1,0:T(8,128)(2,1)}, bf16[4,96,5120]{2,1,0:T(8,128)(2,1)}, u32[]{:S(2)}, u32[]{:S(2)}) collective-permute-start(bf16[4,96,5120]{2,1,0:T(8,128)(2,1)} %bitcast.30), channel_id=1, source_target_pairs={{0,1},{1,0},{2,3},{3,2},{4,5},{5,4},{6,7},{7,6},{8,9},{9,8},{10,11... | collective-permute-start | bytes 11796488 | tf_op jit(solution)/shard_map/ppermute | solution.py:138
  762.4 44.6 %collective-permute-start.6 = (f32[2,96,2560]{2,1,0:T(8,128)}, f32[2,96,2560]{2,1,0:T(8,128)S(1)}, u32[]{:S(2)}, u32[]{:S(2)}) collective-permute-start(f32[2,96,2560]{2,1,0:T(8,128)} %get-tuple-element.91), channel_id=1, source_target_pairs={{0,6},{1,7},{2,0},{3,1},{4,2},{5,3},{6,4},{7,5},{8,14},{9,15},{10,... | collective-permute-start | bytes 5898248 | tf_op jit(solution)/shard_map/ppermute | solution.py:138
  762.4 45.9 %collective-permute-start.7 = (f32[2,96,2560]{2,1,0:T(8,128)}, f32[2,96,2560]{2,1,0:T(8,128)}, u32[]{:S(2)}, u32[]{:S(2)}) collective-permute-start(f32[2,96,2560]{2,1,0:T(8,128)} %get-tuple-element.92), channel_id=1, source_target_pairs={{0,2},{1,3},{2,4},{3,5},{4,6},{5,7},{6,0},{7,1},{8,10},{9,11},{10,... | collective-permute-start | bytes 5898248 | tf_op jit(solution)/shard_map/ppermute | solution.py:138
  812.3 26.8 %collective-permute-start.8 = (f32[96,2560]{1,0:T(8,128)}, f32[96,2560]{1,0:T(8,128)S(1)}, u32[]{:S(2)}, u32[]{:S(2)}) collective-permute-start(f32[96,2560]{1,0:T(8,128)} %get-tuple-element.93), channel_id=1, source_target_pairs={{0,2},{1,3},{2,4},{3,5},{4,6},{5,7},{6,0},{7,1},{8,10},{9,11},{10,... | collective-permute-start | bytes 2949128 | tf_op jit(solution)/shard_map/ppermute | solution.py:138
  812.3 26.8 %collective-permute-start.9 = (f32[96,2560]{1,0:T(8,128)}, f32[96,2560]{1,0:T(8,128)S(1)}, u32[]{:S(2)}, u32[]{:S(2)}) collective-permute-start(f32[96,2560]{1,0:T(8,128)} %get-tuple-element.94), channel_id=1, source_target_pairs={{0,6},{1,7},{2,0},{3,1},{4,2},{5,3},{6,4},{7,5},{8,14},{9,15},{10,... | collective-permute-start | bytes 2949128 | tf_op jit(solution)/shard_map/ppermute | solution.py:138
  837.6 43.5 %collective-permute-start.10 = (bf16[4,96,5120]{2,1,0:T(8,128)(2,1)}, bf16[4,96,5120]{2,1,0:T(8,128)(2,1)}, u32[]{:S(2)}, u32[]{:S(2)}) collective-permute-start(bf16[4,96,5120]{2,1,0:T(8,128)(2,1)} %bitcast.272), channel_id=1, source_target_pairs={{0,1},{1,0},{2,3},{3,2},{4,5},{5,4},{6,7},{7,6},{8,9},{9,8},{10,11... | collective-permute-start | bytes 11796488 | tf_op jit(solution)/shard_map/ppermute | solution.py:138
  845.2 734.8 %all-gather.28.cloned.1.call-start = ((), (), s32[]{:S(2)}) async-start(), calls=%async_computation.7 | async-start | bytes 8847360 | tf_op jit(solution)/shard_map/all_gather | solution.py:233
  885.5 44.7 %collective-permute-start.11 = (f32[2,96,2560]{2,1,0:T(8,128)}, f32[2,96,2560]{2,1,0:T(8,128)S(1)}, u32[]{:S(2)}, u32[]{:S(2)}) collective-permute-start(f32[2,96,2560]{2,1,0:T(8,128)} %get-tuple-element.101), channel_id=1, source_target_pairs={{0,6},{1,7},{2,0},{3,1},{4,2},{5,3},{6,4},{7,5},{8,14},{9,15},{10,... | collective-permute-start | bytes 5898248 | tf_op jit(solution)/shard_map/ppermute | solution.py:138
  885.6 44.8 %collective-permute-start.12 = (f32[2,96,2560]{2,1,0:T(8,128)}, f32[2,96,2560]{2,1,0:T(8,128)}, u32[]{:S(2)}, u32[]{:S(2)}) collective-permute-start(f32[2,96,2560]{2,1,0:T(8,128)} %get-tuple-element.102), channel_id=1, source_target_pairs={{0,2},{1,3},{2,4},{3,5},{4,6},{5,7},{6,0},{7,1},{8,10},{9,11},{10,... | collective-permute-start | bytes 5898248 | tf_op jit(solution)/shard_map/ppermute | solution.py:138
  935.4 30.2 %collective-permute-start.13 = (f32[96,2560]{1,0:T(8,128)}, f32[96,2560]{1,0:T(8,128)S(1)}, u32[]{:S(2)}, u32[]{:S(2)}) collective-permute-start(f32[96,2560]{1,0:T(8,128)} %get-tuple-element.103), channel_id=1, source_target_pairs={{0,2},{1,3},{2,4},{3,5},{4,6},{5,7},{6,0},{7,1},{8,10},{9,11},{10,... | collective-permute-start | bytes 2949128 | tf_op jit(solution)/shard_map/ppermute | solution.py:138
  935.4 30.2 %collective-permute-start.14 = (f32[96,2560]{1,0:T(8,128)}, f32[96,2560]{1,0:T(8,128)S(1)}, u32[]{:S(2)}, u32[]{:S(2)}) collective-permute-start(f32[96,2560]{1,0:T(8,128)} %get-tuple-element.104), channel_id=1, source_target_pairs={{0,6},{1,7},{2,0},{3,1},{4,2},{5,3},{6,4},{7,5},{8,14},{9,15},{10,... | collective-permute-start | bytes 2949128 | tf_op jit(solution)/shard_map/ppermute | solution.py:138
  960.7 35.3 %collective-permute-start.15 = (bf16[4,96,5120]{2,1,0:T(8,128)(2,1)}, bf16[4,96,5120]{2,1,0:T(8,128)(2,1)}, u32[]{:S(2)}, u32[]{:S(2)}) collective-permute-start(bf16[4,96,5120]{2,1,0:T(8,128)(2,1)} %bitcast.273), channel_id=1, source_target_pairs={{0,1},{1,0},{2,3},{3,2},{4,5},{5,4},{6,7},{7,6},{8,9},{9,8},{10,11... | collective-permute-start | bytes 11796488 | tf_op jit(solution)/shard_map/ppermute | solution.py:138
  971.8 615.4 %all-gather.32.cloned.1.call-start = ((), (), s32[]{:S(2)}) async-start(), calls=%async_computation.9 | async-start | bytes 8847360 | tf_op jit(solution)/shard_map/all_gather | solution.py:233
  1000.6 53.3 %collective-permute-start.16 = (f32[2,96,2560]{2,1,0:T(8,128)}, f32[2,96,2560]{2,1,0:T(8,128)S(1)}, u32[]{:S(2)}, u32[]{:S(2)}) collective-permute-start(f32[2,96,2560]{2,1,0:T(8,128)} %get-tuple-element.111), channel_id=1, source_target_pairs={{0,6},{1,7},{2,0},{3,1},{4,2},{5,3},{6,4},{7,5},{8,14},{9,15},{10,... | collective-permute-start | bytes 5898248 | tf_op jit(solution)/shard_map/ppermute | solution.py:138
  1000.6 53.9 %collective-permute-start.17 = (f32[2,96,2560]{2,1,0:T(8,128)}, f32[2,96,2560]{2,1,0:T(8,128)}, u32[]{:S(2)}, u32[]{:S(2)}) collective-permute-start(f32[2,96,2560]{2,1,0:T(8,128)} %get-tuple-element.112), channel_id=1, source_target_pairs={{0,2},{1,3},{2,4},{3,5},{4,6},{5,7},{6,0},{7,1},{8,10},{9,11},{10,... | collective-permute-start | bytes 5898248 | tf_op jit(solution)/shard_map/ppermute | solution.py:138
  1059.1 43.1 %collective-permute-start.18 = (f32[96,2560]{1,0:T(8,128)}, f32[96,2560]{1,0:T(8,128)S(1)}, u32[]{:S(2)}, u32[]{:S(2)}) collective-permute-start(f32[96,2560]{1,0:T(8,128)} %get-tuple-element.113), channel_id=1, source_target_pairs={{0,2},{1,3},{2,4},{3,5},{4,6},{5,7},{6,0},{7,1},{8,10},{9,11},{10,... | collective-permute-start | bytes 2949128 | tf_op jit(solution)/shard_map/ppermute | solution.py:138
  1060.2 42.0 %collective-permute-start.19 = (f32[96,2560]{1,0:T(8,128)}, f32[96,2560]{1,0:T(8,128)S(1)}, u32[]{:S(2)}, u32[]{:S(2)}) collective-permute-start(f32[96,2560]{1,0:T(8,128)} %get-tuple-element.114), channel_id=1, source_target_pairs={{0,6},{1,7},{2,0},{3,1},{4,2},{5,3},{6,4},{7,5},{8,14},{9,15},{10,... | collective-permute-start | bytes 2949128 | tf_op jit(solution)/shard_map/ppermute | solution.py:138
  1108.3 485.9 %all-gather.36.cloned.1.call-start = ((), (), s32[]{:S(2)}) async-start(), calls=%async_computation.11 | async-start | bytes 8847360 | tf_op jit(solution)/shard_map/all_gather | solution.py:233
  1132.1 25.8 %collective-permute-start.20 = (bf16[4,96,5120]{2,1,0:T(8,128)(2,1)}, bf16[4,96,5120]{2,1,0:T(8,128)(2,1)}, u32[]{:S(2)}, u32[]{:S(2)}) collective-permute-start(bf16[4,96,5120]{2,1,0:T(8,128)(2,1)} %bitcast.274), channel_id=1, source_target_pairs={{0,1},{1,0},{2,3},{3,2},{4,5},{5,4},{6,7},{7,6},{8,9},{9,8},{10,11... | collective-permute-start | bytes 11796488 | tf_op jit(solution)/shard_map/ppermute | solution.py:138
  1162.3 44.6 %collective-permute-start.21 = (f32[2,96,2560]{2,1,0:T(8,128)}, f32[2,96,2560]{2,1,0:T(8,128)S(1)}, u32[]{:S(2)}, u32[]{:S(2)}) collective-permute-start(f32[2,96,2560]{2,1,0:T(8,128)} %get-tuple-element.121), channel_id=1, source_target_pairs={{0,6},{1,7},{2,0},{3,1},{4,2},{5,3},{6,4},{7,5},{8,14},{9,15},{10,... | collective-permute-start | bytes 5898248 | tf_op jit(solution)/shard_map/ppermute | solution.py:138
  1162.4 45.9 %collective-permute-start.22 = (f32[2,96,2560]{2,1,0:T(8,128)}, f32[2,96,2560]{2,1,0:T(8,128)}, u32[]{:S(2)}, u32[]{:S(2)}) collective-permute-start(f32[2,96,2560]{2,1,0:T(8,128)} %get-tuple-element.122), channel_id=1, source_target_pairs={{0,2},{1,3},{2,4},{3,5},{4,6},{5,7},{6,0},{7,1},{8,10},{9,11},{10,... | collective-permute-start | bytes 5898248 | tf_op jit(solution)/shard_map/ppermute | solution.py:138
  1212.2 38.2 %collective-permute-start.23 = (f32[96,2560]{1,0:T(8,128)}, f32[96,2560]{1,0:T(8,128)S(1)}, u32[]{:S(2)}, u32[]{:S(2)}) collective-permute-start(f32[96,2560]{1,0:T(8,128)} %get-tuple-element.123), channel_id=1, source_target_pairs={{0,2},{1,3},{2,4},{3,5},{4,6},{5,7},{6,0},{7,1},{8,10},{9,11},{10,... | collective-permute-start | bytes 2949128 | tf_op jit(solution)/shard_map/ppermute | solution.py:138
  1212.2 38.2 %collective-permute-start.24 = (f32[96,2560]{1,0:T(8,128)}, f32[96,2560]{1,0:T(8,128)S(1)}, u32[]{:S(2)}, u32[]{:S(2)}) collective-permute-start(f32[96,2560]{1,0:T(8,128)} %get-tuple-element.124), channel_id=1, source_target_pairs={{0,6},{1,7},{2,0},{3,1},{4,2},{5,3},{6,4},{7,5},{8,14},{9,15},{10,... | collective-permute-start | bytes 2949128 | tf_op jit(solution)/shard_map/ppermute | solution.py:138
  1256.5 344.7 %all-gather.40.cloned.1.call-start = ((), (), s32[]{:S(2)}) async-start(), calls=%async_computation.13 | async-start | bytes 8847360 | tf_op jit(solution)/shard_map/all_gather | solution.py:233
  1318.1 26.0 %collective-permute-start.25 = (bf16[4,96,5120]{2,1,0:T(8,128)(2,1)}, bf16[4,96,5120]{2,1,0:T(8,128)(2,1)}, u32[]{:S(2)}, u32[]{:S(2)}) collective-permute-start(bf16[4,96,5120]{2,1,0:T(8,128)(2,1)} %bitcast.275), channel_id=1, source_target_pairs={{0,1},{1,0},{2,3},{3,2},{4,5},{5,4},{6,7},{7,6},{8,9},{9,8},{10,11... | collective-permute-start | bytes 11796488 | tf_op jit(solution)/shard_map/ppermute | solution.py:138
  1348.6 44.7 %collective-permute-start.26 = (f32[2,96,2560]{2,1,0:T(8,128)}, f32[2,96,2560]{2,1,0:T(8,128)S(1)}, u32[]{:S(2)}, u32[]{:S(2)}) collective-permute-start(f32[2,96,2560]{2,1,0:T(8,128)} %get-tuple-element.131), channel_id=1, source_target_pairs={{0,6},{1,7},{2,0},{3,1},{4,2},{5,3},{6,4},{7,5},{8,14},{9,15},{10,... | collective-permute-start | bytes 5898248 | tf_op jit(solution)/shard_map/ppermute | solution.py:138
  1348.6 46.0 %collective-permute-start.27 = (f32[2,96,2560]{2,1,0:T(8,128)}, f32[2,96,2560]{2,1,0:T(8,128)}, u32[]{:S(2)}, u32[]{:S(2)}) collective-permute-start(f32[2,96,2560]{2,1,0:T(8,128)} %get-tuple-element.132), channel_id=1, source_target_pairs={{0,2},{1,3},{2,4},{3,5},{4,6},{5,7},{6,0},{7,1},{8,10},{9,11},{10,... | collective-permute-start | bytes 5898248 | tf_op jit(solution)/shard_map/ppermute | solution.py:138
  1398.6 23.9 %collective-permute-start.28 = (f32[96,2560]{1,0:T(8,128)}, f32[96,2560]{1,0:T(8,128)S(1)}, u32[]{:S(2)}, u32[]{:S(2)}) collective-permute-start(f32[96,2560]{1,0:T(8,128)} %get-tuple-element.133), channel_id=1, source_target_pairs={{0,2},{1,3},{2,4},{3,5},{4,6},{5,7},{6,0},{7,1},{8,10},{9,11},{10,... | collective-permute-start | bytes 2949128 | tf_op jit(solution)/shard_map/ppermute | solution.py:138
  1398.6 23.9 %collective-permute-start.29 = (f32[96,2560]{1,0:T(8,128)}, f32[96,2560]{1,0:T(8,128)S(1)}, u32[]{:S(2)}, u32[]{:S(2)}) collective-permute-start(f32[96,2560]{1,0:T(8,128)} %get-tuple-element.134), channel_id=1, source_target_pairs={{0,6},{1,7},{2,0},{3,1},{4,2},{5,3},{6,4},{7,5},{8,14},{9,15},{10,... | collective-permute-start | bytes 2949128 | tf_op jit(solution)/shard_map/ppermute | solution.py:138
  1428.6 179.6 %all-gather.44.cloned.1.call-start = ((), (), s32[]{:S(2)}) async-start(), calls=%async_computation.15 | async-start | bytes 4423680 | tf_op jit(solution)/shard_map/all_gather | solution.py:233
  1428.7 23.4 %copy-start.45 = (bf16[384,5120]{1,0:T(8,128)(2,1)S(1)}, bf16[384,5120]{1,0:T(8,128)(2,1)}, u32[]{:S(2)}) copy-start(bf16[384,5120]{1,0:T(8,128)(2,1)} %all-gather.42.cloned.1.call-done) | copy-start | bytes 11796484
  1475.0 16.8 %copy-start.20 = (bf16[384,3456]{1,0:T(8,128)(2,1)S(1)}, bf16[384,3456]{1,0:T(8,128)(2,1)}, u32[]{:S(2)}) copy-start(bf16[384,3456]{1,0:T(8,128)(2,1)} %fusion.21) | copy-start | bytes 7962628
  1490.0 18.1 %collective-permute-start.30 = (bf16[4,48,5120]{2,1,0:T(8,128)(2,1)S(1)}, bf16[4,48,5120]{2,1,0:T(8,128)(2,1)S(1)}, u32[]{:S(2)}, u32[]{:S(2)}) collective-permute-start(bf16[4,48,5120]{2,1,0:T(8,128)(2,1)S(1)} %bitcast.276), channel_id=1, source_target_pairs={{0,1},{1,0},{2,3},{3,2},{4,5},{5,4},{6,7},{7,6},{8,9},{9,8},{10,11... | collective-permute-start | bytes 5898248 | tf_op jit(solution)/shard_map/ppermute | solution.py:138
  1513.0 23.6 %collective-permute-start.31 = (f32[2,48,2560]{2,1,0:T(8,128)}, f32[2,48,2560]{2,1,0:T(8,128)S(1)}, u32[]{:S(2)}, u32[]{:S(2)}) collective-permute-start(f32[2,48,2560]{2,1,0:T(8,128)} %get-tuple-element.141), channel_id=1, source_target_pairs={{0,6},{1,7},{2,0},{3,1},{4,2},{5,3},{6,4},{7,5},{8,14},{9,15},{10,... | collective-permute-start | bytes 2949128 | tf_op jit(solution)/shard_map/ppermute | solution.py:138
  1515.2 24.4 %collective-permute-start.32 = (f32[2,48,2560]{2,1,0:T(8,128)}, f32[2,48,2560]{2,1,0:T(8,128)S(1)}, u32[]{:S(2)}, u32[]{:S(2)}) collective-permute-start(f32[2,48,2560]{2,1,0:T(8,128)} %get-tuple-element.142), channel_id=1, source_target_pairs={{0,2},{1,3},{2,4},{3,5},{4,6},{5,7},{6,0},{7,1},{8,10},{9,11},{10,... | collective-permute-start | bytes 2949128 | tf_op jit(solution)/shard_map/ppermute | solution.py:138
  1543.9 13.0 collective-permute-start.33
  1543.9 13.0 collective-permute-start.34
  (35 other events, 86.0 us)
Sparse Core Ops, SparseCore 0:
  12.3 235.0 all-gather.15
  351.3 27.7 all-gather.17
  403.7 44.2 all-gather.21
  449.4 43.4 all-gather.25
  494.4 67.1 all-gather.29
  563.0 43.2 all-gather.33
  607.8 43.4 all-gather.37
  653.0 26.9 all-gather.41
  681.6 26.7 all-gather.19
  845.3 43.0 all-gather.23
  971.9 50.0 all-gather.27
  1108.4 43.7 all-gather.31
  1256.6 43.0 all-gather.35
  1428.8 44.9 all-gather.39
  1562.5 28.4 all-gather.43

commit v3 on v2

--- a/solution.py
+++ b/solution.py
@@ -8,8 +8,8 @@
 
 EPS = 1e-5
 ROPE_BASE = 10000.0
-CHUNK_SEQS = (2, 4, 4, 4, 4, 4, 2)
-TILE = 48
+CHUNK_PARTS = (3, 4, 4, 4, 3)
+TILE = 32
 
 
 def rms_norm(rows, gain):
@@ -74,7 +74,7 @@
 
 
 def wide(ref):
-    return ref[0].astype(jnp.float32)
+    return ref[...].reshape(ref.shape[-2:]).astype(jnp.float32)
 
 
 def pieces_kernel(where_ref, far_a, far_b, far_c, far_d, up_a, up_b, down_a, down_b, plus_ref, minus_ref):
@@ -125,10 +125,11 @@
     partner_perm = [(index, index ^ 1) for index in range(tp_size)]
 
     def places():
-        chip = lax.shift_right_logical(lax.axis_index("tp"), 1)
-        return jnp.stack([(chip + shift) & (chips - 1) for shift in (0, 1, 2, chips - 1)]).astype(jnp.int32)
-
-    def reduce_rows(keep, give, resid_rows, where):
+        index = lax.axis_index("tp")
+        chip = lax.shift_right_logical(index, 1)
+        return jnp.stack([(chip + shift) & (chips - 1) for shift in (0, 1, 2, chips - 1)] + [index & 1]).astype(jnp.int32)
+
+    def reduce_rows(partial, give, resid_rows, where):
         rows, width = resid_rows.shape
         half = width // 2
         own, up, far, down = range(4)
@@ -138,7 +139,9 @@
             return lax.ppermute(piece, "tp", perm)
 
         def at(place, side):
-            return pl.BlockSpec((1, TILE, half), lambda n, where_ref: (where_ref[place], n, side))
+            mine = pl.BlockSpec((1, 1, TILE, half), lambda n, where_ref: (where_ref[place], where_ref[4], n, side))
+            theirs = pl.BlockSpec((1, TILE, half), lambda n, where_ref: (where_ref[place], n, side))
+            return [mine, theirs]
 
         def part(side):
             return pl.BlockSpec((1, TILE, half), lambda n, where_ref: (side, n, 0))
@@ -151,22 +154,22 @@
 
         got = move(give, partner_perm)
         plus, minus = ring_call(
-            pieces_kernel, where, [keep, got] * 4,
-            [at(far, low), at(far, low), at(far, high), at(far, high), at(up, high), at(up, high), at(down, low), at(down, low)],
+            pieces_kernel, where, [partial, got] * 4,
+            at(far, low) + at(far, high) + at(up, high) + at(down, low),
             [message, message], [message_spec, message_spec], rows,
         )
         plus = move(plus, chip_perm(1))
         minus = move(minus, chip_perm(-1))
         run_low, run_high = ring_call(
-            runs_kernel, where, [keep, got] * 2 + [plus, minus],
-            [at(up, low), at(up, low), at(down, high), at(down, high), part(0), part(0)],
+            runs_kernel, where, [partial, got] * 2 + [plus, minus],
+            at(up, low) + at(down, high) + [part(0), part(0)],
             [running, running], [flat, flat], rows,
         )
         run_low = move(run_low, chip_perm(1))
         run_high = move(run_high, chip_perm(-1))
         return ring_call(
-            final_kernel, where, [keep, got] * 2 + [minus, plus, run_low, run_high, resid_rows],
-            [at(own, low), at(own, low), at(own, high), at(own, high), part(1), part(1), flat, flat, full],
+            final_kernel, where, [partial, got] * 2 + [minus, plus, run_low, run_high, resid_rows],
+            at(own, low) + at(own, high) + [part(1), part(1), flat, flat, full],
             jax.ShapeDtypeStruct((rows, width), jnp.bfloat16), full, rows,
         )
 
@@ -176,7 +179,8 @@
         kv_local = k_cache.shape[2]
         group_size = w_query.shape[1] // (head_dim * kv_local)
         all_rows = batch_size * seq_len
-        chunk_rows = [seqs * seq_len for seqs in CHUNK_SEQS]
+        owned = all_rows // tp_size
+        chunk_rows = [owned * share // sum(CHUNK_PARTS) for share in CHUNK_PARTS]
         starts = [sum(chunk_rows[:chunk]) for chunk in range(len(chunk_rows))]
         tp_index = lax.axis_index("tp")
         w_out_full = lax.all_gather(w_out, "tp", axis=0, tiled=True)
@@ -189,49 +193,37 @@
         values = jnp.where(valid, values, jnp.zeros_like(values))
         k_cache_out = lax.dynamic_update_slice(k_cache, keys, (0, 0, 0, 0))
         v_cache_out = lax.dynamic_update_slice(v_cache, values, (0, 0, 0, 0))
-        attn_rows = causal_attention(queries, keys, values, seq_lens).reshape(all_rows, -1)
-
-        def by_owner(array):
-            pieces = [array[start:start + size].reshape(tp_size, size // tp_size, array.shape[1]) for start, size in zip(starts, chunk_rows)]
-            return jnp.concatenate(pieces, axis=1)
-
-        o_rows = lax.all_to_all(by_owner(attn_rows), "tp", 0, 0, tiled=True)
-        x_rows = jnp.concatenate([lax.dynamic_slice_in_dim(x.reshape(all_rows, model_width), start + tp_index * (size // tp_size), size // tp_size, axis=0) for start, size in zip(starts, chunk_rows)], axis=0)
-        first = chunk_rows[0] // tp_size
+        attn_rows = causal_attention(queries, keys, values, seq_lens).reshape(tp_size, owned, -1)
+        o_rows = lax.all_to_all(attn_rows, "tp", 0, 0, tiled=True)
+        x_rows = lax.dynamic_slice_in_dim(x.reshape(all_rows, model_width), tp_index * owned, owned, axis=0)
+        first = chunk_rows[0]
         fence = lax.optimization_barrier
         hidden_first = out_project(o_rows[:, :first], w_out_full, x_rows[:first], 512)
         normed_first, o_rest = fence((rms_norm(hidden_first, mlp_gain), o_rows[:, first:]))
         hidden_rest = out_project(o_rest, w_out_full, x_rows[first:], 512)
         hidden = [hidden_first, hidden_rest]
         normed_parts = [normed_first, rms_norm(hidden_rest, mlp_gain)]
-        keep = hidden_first
+        partial = hidden_first
         where = places()
-        core = lax.axis_index("tp") & 1
-        y = unwritten((all_rows, model_width), jnp.bfloat16)
-        for chunk, (start, size) in enumerate(zip(starts, chunk_rows)):
-            rows = size // tp_size
-            begin = start // tp_size - (first if chunk else 0)
+        core = tp_index & 1
+        y = unwritten((tp_size, owned, model_width), jnp.bfloat16)
+        for chunk, (start, rows) in enumerate(zip(starts, chunk_rows)):
+            begin = start - first if chunk else 0
             own = slice(begin, begin + rows)
             normed_mlp = lax.all_gather(normed_parts[min(chunk, 1)][own], "tp", axis=0, tiled=True)
             if chunk:
-                normed_mlp, keep = fence((normed_mlp, keep))
+                normed_mlp, partial = fence((normed_mlp, partial))
             gate_pre = jnp.dot(normed_mlp, w_gate, preferred_element_type=jnp.float32)
             up_pre = jnp.dot(normed_mlp, w_up, preferred_element_type=jnp.float32)
             gated = (jax.nn.silu(gate_pre) * up_pre).astype(jnp.bfloat16)
-
-            def down(which, gated):
-                blocks = gated.reshape(chips, cores, rows, gated.shape[1])
-                picked = lax.dynamic_slice(blocks, (0, which, 0, 0), (chips, 1, rows, gated.shape[1]), allow_negative_indices=False)
-                partial = jnp.dot(picked.reshape(chips * rows, gated.shape[1]), w_down, preferred_element_type=jnp.float32)
-                return partial.astype(jnp.bfloat16).reshape(chips, rows, model_width)
-
-            gated, core = fence((gated, core))
-            give = down(1 - core, gated)
-            gated, give, core = fence((gated, give, core))
-            keep = down(core, gated)
-            out_rows = reduce_rows(keep, give, hidden[min(chunk, 1)][own], where)
-            y_chunk = lax.all_gather(out_rows, "tp", axis=0, tiled=True)
-            y = lax.dynamic_update_slice(y, y_chunk, (start, 0))
+            partial = jnp.dot(gated, w_down, preferred_element_type=jnp.float32).astype(jnp.bfloat16)
+            partial, core = fence((partial, core))
+            blocks = partial.reshape(chips, cores, rows, model_width)
+            give = lax.dynamic_slice(blocks, (0, 1 - core, 0, 0), (chips, 1, rows, model_width), allow_negative_indices=False)
+            give, core = fence((give.reshape(chips, rows, model_width), core))
+            out_rows = reduce_rows(blocks, give, hidden[min(chunk, 1)][own], where)
+            y_chunk = lax.all_gather(out_rows, "tp", axis=0)
+            y = lax.dynamic_update_slice(y, y_chunk, (0, start, 0))
         return y.reshape(batch_size, seq_len, model_width), k_cache_out, v_cache_out
 
     cache_spec = P("dp", None, "tp", None)

time: 1630 us -> 1580 us (0.969)
  matrix products: 859 us -> 741 us
  waiting for transfers between devices: 292 us -> 410 us
  local copies, waits for them, and re-layouts: 197 us -> 155 us
    ppermute x35 -> x25, waiting for transfers between devices: 235 us -> 337 us  [move(): return lax.ppermute(piece, 'tp', perm)]
    dot_general x14 -> x5, matrix products: 291 us -> 201 us  [layer_shard(): jnp.dot(gated, w_down, preferred_element_type=jnp.float32)]
    reshape x7, local copies, waits for them, and re-layouts: 13.1 us -> 43.6 us  [the longest x2 26 us: layer_shard(): causal_attention(queries, keys, values, seq_lens)]
    dynamic_slice x14 -> x0, local copies, waits for them, and re-layouts: 30.1 us -> none  [down(): lax.dynamic_slice(blocks, (0, which, 0, 0), (chips, 1, rows, gated.shape[...]
    unnamed x109 -> x54, local copies, waits for them, and re-layouts: 45.4 us -> 18.8 us
    dot_general x7 -> x5, matrix products: 223 us -> 209 us  [layer_shard(): up_pre = jnp.dot(normed_mlp, w_up, preferred_element_type=jnp.float32)]
    dot_general x7 -> x5, matrix products: 222 us -> 208 us  [layer_shard(): gate_pre = jnp.dot(normed_mlp, w_gate, preferred_element_type=jnp.float32)]
    ppermute x35 -> x25, starting transfers between devices: 40.1 us -> 30.8 us  [move(): return lax.ppermute(piece, 'tp', perm)]
  transfers between devices with their start and end apart: 51 -> 37, of which waited for: 18 -> 18; matrix products, arithmetic and copies ran while one was open for 67% -> 59% of each run, Pallas kernels for 8% -> 8%
where the time goes in v3:
time: 1580 us; the launch traced here: 1560 us
  matrix products  741 us (47%)
  waiting for transfers between devices  410 us (26%)
  local copies, waits for them, and re-layouts  155 us (10%)
  Pallas kernels  145 us (9%)
  other arithmetic  60.8 us (4%)
  starting transfers between devices  38.4 us (2%)
    ppermute x25, waiting for transfers between devices, move(): return lax.ppermute(piece, 'tp', perm)  337 us
    dot_general x5, matrix products, layer_shard(): up_pre = jnp.dot(normed_mlp, w_up, preferred_element_type=jnp.float32)  209 us
    dot_general x5, matrix products, layer_shard(): gate_pre = jnp.dot(normed_mlp, w_gate, preferred_element_type=jnp.float32)  208 us
    dot_general x5, matrix products, layer_shard(): jnp.dot(gated, w_down, preferred_element_type=jnp.float32)  201 us
    pallas_call x15, Pallas kernels, ring_call(): pl.pallas_call(kernel, grid_spec=pltpu.PrefetchScalarGridSpec(num_scalar_...  84.1 us
    all_to_all x1, waiting for transfers between devices, layer_shard(): o_rows = lax.all_to_all(attn_rows, 'tp', 0, 0, tiled=True)  67.1 us
    pallas_call x2, Pallas kernels, out_project(): pl.pallas_call(out_kernel, grid=(width // tile,), in_specs=[pl.BlockSpec(...  60.5 us
    dot_general x1, matrix products, layer_shard(): jnp.einsum('bsd,dk->bsk', normed, w_query, preferred_element_type=jnp.flo...  44.9 us
  transfers between devices with their start and end apart: 37, of which 18 were waited for; matrix products, arithmetic and copies ran while one was open for 59% of the time, Pallas kernels for 8%

profile of v3, /device:TPU:113, one launch (start us, length us, event | category | flops | bytes accessed | tf_op | source)
XLA Modules:
  0.0 1564.5 jit_solution(15591628869472841244)
XLA Ops:
  14.1 20.4 %fusion = f32[24,192]{1,0:T(8,128)S(1)} fusion(bf16[24,192,5120]{2,1,0:T(8,128)(2,1)} %param.13), kind=kLoop, calls=%fused_computation.2 | loop fusion | flops 70774272 | bytes 47204352 | tf_op jit(solution)/shard_map/reduce_sum | solution.py:17
  34.5 23.4 %fusion.5 = f32[24,192,128]{2,1,0:T(8,128)} fusion(bf16[24,192,5120]{2,1,0:T(8,128)(2,1)} %param.13, f32[5120]{0:T(1024)S(1)} %convert_element_type.140, f32[24,192]{1,0:T(8,128)S(1)} %add_rsqrt_fusion, bf16[5120,128]{1,0:T(8,128)(2,1)S(1)} %copy-done.25), kind=kOutput, calls=%fused_computation.6 | convolution fusion | flops 6134169600 | bytes 50894848 | tf_op jit(solution)/shard_map/bsd,dk->bsk/dot_general | solution.py:189
  66.3 44.9 %fusion.3 = f32[24,192,640]{2,1,0:T(8,128)} fusion(bf16[24,192,5120]{2,1,0:T(8,128)(2,1)} %param.13, f32[5120]{0:T(1024)S(1)} %convert_element_type.140, f32[24,192]{1,0:T(8,128)S(1)} %add_rsqrt_fusion, bf16[5120,640]{1,0:T(8,128)(2,1)} %param.15), kind=kOutput, calls=%fused_computation.5 | convolution fusion | flops 30293360640 | bytes 65574912 | tf_op jit(solution)/shard_map/bsd,dk->bsk/dot_general | solution.py:188
  111.2 16.0 %copy.22 = f32[24,192,640]{1,0,2:T(8,128)} copy(f32[24,192,640]{2,1,0:T(8,128)} %fusion.3) | data formatting | bytes 23592960 | tf_op jit(solution)/shard_map/bsd,dk->bsk/dot_general | solution.py:188
  129.4 7.0 subtract_convert_fusion
  140.8 18.4 %fusion.10 = (f32[24,5,192]{2,1,0:T(8,128)S(1)}, f32[24,192,192,5]{2,1,3,0:T(8,128)}) fusion(pred[24,192,192]{1,2,0:T(8,128)(4,1)} %broadcast_and_fusion, bf16[24,192,5,128]{1,0,3,2:T(8,128)(2,1)} %bitcast.174, bf16[24,192,128]{2,1,0:T(8,128)(2,1)} %copy.21, pred[24,192]{1,0:T(8,128)(4,1)S(1)} %iota_compare_fusion.1), kind=kOutput, calls=%fused_computation.12 | convolution fusion | flops 1146299904 | bytes 25754112 | tf_op jit(solution)/shard_map/bqkgh,bskh->bkgqs/dot_general | solution.py:40
  159.2 11.0 fusion.9
  170.2 21.9 %bitcast_dynamic-update-slice_fusion = (bf16[24,384,1,128]{3,1,2,0:T(8,128)(2,1)}, bf16[24,192,128]{2,1,0:T(8,128)(2,1)}) fusion(bf16[24,384,1,128]{3,1,2,0:T(8,128)(2,1)} %copy.48, bf16[5120,128]{1,0:T(8,128)(2,1)S(1)} %copy-done, bf16[24,192,5120]{2,1,0:T(8,128)(2,1)} %param.13, f32[5120]{0:T(1024)S(1)} %convert_element_type.140, ...), kind=kOutput, calls=%fused_computation.56 | convolution fusion | flops 6135349248 | bytes 50899456 | tf_op jit(solution)/shard_map/bsd,dk->bsk/dot_general | solution.py:190
  192.1 14.3 convert_bitcast_fusion
  206.4 11.7 copy.32
  218.1 14.3 reshape.365
  232.4 7.0 all-to-all-start
  241.7 67.1 %all-to-all-done = bf16[8,576,640]{2,1,0:T(8,128)(2,1)} async-done(((bf16[8,576,640]{2,1,0:T(8,128)(2,1)}), bf16[8,576,640]{2,1,0:T(8,128)(2,1)}, u32[]{:S(2)}, u32[]{:S(2)}) %all-to-all-start) | async-done | bytes 5898272 | tf_op jit(solution)/shard_map/all_to_all | solution.py:197
  311.0 5.1 slice.69.o_ref
  316.0 21.5 %out_project.2.resid_ref = bf16[96,5120]{1,0:T(8,128)(2,1)} custom-call(bf16[8,96,640]{2,1,0:T(8,128)(2,1)} %slice.68.o_ref, bf16[5120,5120]{1,0:T(8,128)(2,1)} %all-gather.17.cloned.1.call-done.w_ref, bf16[96,5120]{1,0:T(8,128)(2,1)} %constant_dynamic-slice_fusion.x_ref), custom_call_target="tpu_custom_call" | custom-call | flops 5033164800 | bytes 52428800 | tf_op jit(solution)/shard_map/out_project/pallas_call | solution.py:60
  341.7 4.9 constant_dynamic-slice_fusion.1.x_ref
  346.6 39.0 %out_project.3 = bf16[480,5120]{1,0:T(8,128)(2,1)} custom-call(bf16[8,480,640]{2,1,0:T(8,128)(2,1)} %slice.69.o_ref, bf16[5120,5120]{1,0:T(8,128)(2,1)} %all-gather.17.cloned.1.call-done.w_ref, bf16[480,5120]{1,0:T(8,128)(2,1)} %constant_dynamic-slice_fusion.1.x_ref), custom_call_target="tpu_custom_call" | custom-call | flops 25165824000 | bytes 52428800 | tf_op jit(solution)/shard_map/out_project/pallas_call | solution.py:60
  401.2 34.9 %fusion.44 = f32[768,3456]{1,0:T(8,128)S(1)} fusion(bf16[768,5120]{1,0:T(8,128)(2,1)} %all-gather.19.cloned.1.call-done, bf16[5120,3456]{1,0:T(8,128)(2,1)} %param.19), kind=kOutput, calls=%fused_computation.85 | convolution fusion | flops 27179089920 | bytes 53870592 | tf_op jit(solution)/shard_map/dot_general | solution.py:216
  436.2 33.8 %multiply_convert_fusion.4 = bf16[768,3456]{1,0:T(8,128)(2,1)S(1)} fusion(f32[768,3456]{1,0:T(8,128)S(1)} %fusion.44, bf16[768,5120]{1,0:T(8,128)(2,1)S(1)} %copy-done.24, bf16[5120,3456]{1,0:T(8,128)(2,1)} %param.20), kind=kOutput, calls=%fused_computation.22 | convolution fusion | flops 27195015168 | bytes 59179008 | tf_op jit(solution)/shard_map/dot_general | solution.py:217
  469.9 33.9 %convolution_convert_fusion.4 = bf16[768,5120]{1,0:T(8,128)(2,1)} fusion(bf16[768,3456]{1,0:T(8,128)(2,1)S(1)} %multiply_convert_fusion.4, bf16[3456,5120]{1,0:T(8,128)(2,1)} %param.21), kind=kOutput, calls=%fused_computation.30 | convolution fusion | flops 27183022080 | bytes 48562176 | tf_op jit(solution)/shard_map/dot_general | solution.py:219
  508.7 47.3 %fusion.45 = f32[1024,3456]{1,0:T(8,128)} fusion(bf16[1024,5120]{1,0:T(8,128)(2,1)} %all-gather.21.cloned.1.call-done, bf16[5120,3456]{1,0:T(8,128)(2,1)} %param.19), kind=kOutput, calls=%fused_computation.86 | convolution fusion | flops 36238786560 | bytes 60030976 | tf_op jit(solution)/shard_map/dot_general | solution.py:216
  555.9 44.2 %multiply_convert_fusion.2 = bf16[1024,3456]{1,0:T(8,128)(2,1)S(1)} fusion(f32[1024,3456]{1,0:T(8,128)} %fusion.45, bf16[1024,5120]{1,0:T(8,128)(2,1)S(1)} %copy-done.23, bf16[5120,3456]{1,0:T(8,128)(2,1)} %param.20), kind=kOutput, calls=%fused_computation.15 | convolution fusion | flops 36260020224 | bytes 67108864 | tf_op jit(solution)/shard_map/dot_general | solution.py:217
  600.1 43.7 %convolution_convert_fusion.2 = bf16[1024,5120]{1,0:T(8,128)(2,1)} fusion(bf16[1024,3456]{1,0:T(8,128)(2,1)S(1)} %multiply_convert_fusion.2, bf16[3456,5120]{1,0:T(8,128)(2,1)} %param.21), kind=kOutput, calls=%fused_computation.28 | convolution fusion | flops 36244029440 | bytes 52953088 | tf_op jit(solution)/shard_map/dot_general | solution.py:219
  643.9 5.2 dynamic-slice_bitcast_fusion.2
  649.7 5.7 shard_map.148
  657.5 42.3 %collective-permute-done.1.far_high.near_low = f32[2,96,2560]{2,1,0:T(8,128)S(1)} collective-permute-done((f32[2,96,2560]{2,1,0:T(8,128)}, f32[2,96,2560]{2,1,0:T(8,128)S(1)}, u32[]{:S(2)}, u32[]{:S(2)}) %collective-permute-start.1) | collective-permute-done | bytes 1966112 | tf_op jit(solution)/shard_map/ppermute | solution.py:139
  702.7 4.9 shard_map.149
  714.4 16.4 %collective-permute-done.3.run_low = f32[96,2560]{1,0:T(8,128)S(1)} collective-permute-done((f32[96,2560]{1,0:T(8,128)}, f32[96,2560]{1,0:T(8,128)S(1)}, u32[]{:S(2)}, u32[]{:S(2)}) %collective-permute-start.3) | collective-permute-done | bytes 983072 | tf_op jit(solution)/shard_map/ppermute | solution.py:139
  732.8 5.3 shard_map.150
  738.3 6.1 shard_map.151
  745.9 46.6 %fusion.46 = f32[1024,3456]{1,0:T(8,128)} fusion(bf16[1024,5120]{1,0:T(8,128)(2,1)} %all-gather.23.cloned.1.call-done, bf16[5120,3456]{1,0:T(8,128)(2,1)} %param.19), kind=kOutput, calls=%fused_computation.87 | convolution fusion | flops 36238786560 | bytes 60030976 | tf_op jit(solution)/shard_map/dot_general | solution.py:216
  792.5 40.1 %collective-permute-done.6.far_high.near_low = f32[2,128,2560]{2,1,0:T(8,128)} collective-permute-done((f32[2,128,2560]{2,1,0:T(8,128)}, f32[2,128,2560]{2,1,0:T(8,128)}, u32[]{:S(2)}, u32[]{:S(2)}) %collective-permute-start.6) | collective-permute-done | bytes 2621472 | tf_op jit(solution)/shard_map/ppermute | solution.py:139
  836.4 5.3 shard_map.152
  844.3 47.8 %multiply_convert_fusion.1 = bf16[1024,3456]{1,0:T(8,128)(2,1)} fusion(f32[1024,3456]{1,0:T(8,128)} %fusion.46, bf16[1024,5120]{1,0:T(8,128)(2,1)} %all-gather.23.cloned.1.call-done, bf16[5120,3456]{1,0:T(8,128)(2,1)} %param.20), kind=kOutput, calls=%fused_computation.14 | convolution fusion | flops 36260020224 | bytes 67108864 | tf_op jit(solution)/shard_map/dot_general | solution.py:217
  893.7 6.0 shard_map.153
  899.8 45.6 %convolution_convert_fusion.1 = bf16[1024,5120]{1,0:T(8,128)(2,1)} fusion(bf16[1024,3456]{1,0:T(8,128)(2,1)} %multiply_convert_fusion.1, bf16[3456,5120]{1,0:T(8,128)(2,1)} %param.21), kind=kOutput, calls=%fused_computation.27 | convolution fusion | flops 36244029440 | bytes 52953088 | tf_op jit(solution)/shard_map/dot_general | solution.py:219
  951.7 8.9 collective-permute-done.10.far_b.far_d.up_b.down_b.low_b.high_b
  960.6 6.1 shard_map.154
  968.2 56.9 %collective-permute-done.11.far_high.near_low = f32[2,128,2560]{2,1,0:T(8,128)} collective-permute-done((f32[2,128,2560]{2,1,0:T(8,128)}, f32[2,128,2560]{2,1,0:T(8,128)}, u32[]{:S(2)}, u32[]{:S(2)}) %collective-permute-start.11) | collective-permute-done | bytes 2621472 | tf_op jit(solution)/shard_map/ppermute | solution.py:139
  1026.4 5.2 shard_map.155
  1034.3 45.9 %fusion.47 = f32[1024,3456]{1,0:T(8,128)} fusion(bf16[1024,5120]{1,0:T(8,128)(2,1)} %all-gather.25.cloned.1.call-done, bf16[5120,3456]{1,0:T(8,128)(2,1)} %param.19), kind=kOutput, calls=%fused_computation.88 | convolution fusion | flops 36238786560 | bytes 60030976 | tf_op jit(solution)/shard_map/dot_general | solution.py:216
  1081.8 6.0 shard_map.156
  1087.9 47.7 %multiply_convert_fusion = bf16[1024,3456]{1,0:T(8,128)(2,1)S(1)} fusion(f32[1024,3456]{1,0:T(8,128)} %fusion.47, bf16[1024,5120]{1,0:T(8,128)(2,1)} %all-gather.25.cloned.1.call-done, bf16[5120,3456]{1,0:T(8,128)(2,1)} %param.20), kind=kOutput, calls=%fused_computation.13 | convolution fusion | flops 36260020224 | bytes 67108864 | tf_op jit(solution)/shard_map/dot_general | solution.py:217
  1135.6 43.5 %convolution_convert_fusion = bf16[1024,5120]{1,0:T(8,128)(2,1)} fusion(bf16[1024,3456]{1,0:T(8,128)(2,1)S(1)} %multiply_convert_fusion, bf16[3456,5120]{1,0:T(8,128)(2,1)} %param.21), kind=kOutput, calls=%fused_computation.26 | convolution fusion | flops 36244029440 | bytes 52953088 | tf_op jit(solution)/shard_map/dot_general | solution.py:219
  1184.6 8.4 collective-permute-done.15.far_b.far_d.up_b.down_b.low_b.high_b
  1193.0 6.1 shard_map.157
  1200.6 56.9 %collective-permute-done.16.far_high.near_low = f32[2,128,2560]{2,1,0:T(8,128)} collective-permute-done((f32[2,128,2560]{2,1,0:T(8,128)}, f32[2,128,2560]{2,1,0:T(8,128)}, u32[]{:S(2)}, u32[]{:S(2)}) %collective-permute-start.16) | collective-permute-done | bytes 2621472 | tf_op jit(solution)/shard_map/ppermute | solution.py:139
  1258.8 5.3 shard_map.158
  1266.8 27.8 %collective-permute-done.18.run_low = f32[128,2560]{1,0:T(8,128)S(1)} collective-permute-done((f32[128,2560]{1,0:T(8,128)}, f32[128,2560]{1,0:T(8,128)S(1)}, u32[]{:S(2)}, u32[]{:S(2)}) %collective-permute-start.18) | collective-permute-done | bytes 1310752 | tf_op jit(solution)/shard_map/ppermute | solution.py:139
  1296.1 6.0 shard_map.159
  1302.3 33.6 %fusion.48 = f32[768,3456]{1,0:T(8,128)S(1)} fusion(bf16[768,5120]{1,0:T(8,128)(2,1)} %all-gather.27.cloned.1.call-done, bf16[5120,3456]{1,0:T(8,128)(2,1)} %param.19), kind=kOutput, calls=%fused_computation.89 | convolution fusion | flops 27179089920 | bytes 53870592 | tf_op jit(solution)/shard_map/dot_general | solution.py:216
  1335.9 36.0 %multiply_convert_fusion.3 = bf16[768,3456]{1,0:T(8,128)(2,1)S(1)} fusion(f32[768,3456]{1,0:T(8,128)S(1)} %fusion.48, bf16[768,5120]{1,0:T(8,128)(2,1)} %all-gather.27.cloned.1.call-done, bf16[5120,3456]{1,0:T(8,128)(2,1)} %param.20), kind=kOutput, calls=%fused_computation.21 | convolution fusion | flops 27195015168 | bytes 59179008 | tf_op jit(solution)/shard_map/dot_general | solution.py:217
  1371.9 33.8 %convolution_convert_fusion.3 = bf16[768,5120]{1,0:T(8,128)(2,1)} fusion(bf16[768,3456]{1,0:T(8,128)(2,1)S(1)} %multiply_convert_fusion.3, bf16[3456,5120]{1,0:T(8,128)(2,1)} %param.21), kind=kOutput, calls=%fused_computation.29 | convolution fusion | flops 27183022080 | bytes 48562176 | tf_op jit(solution)/shard_map/dot_general | solution.py:219
  1410.2 6.5 collective-permute-done.20.far_b.far_d.up_b.down_b.low_b.high_b
  1416.8 5.7 shard_map.160
  1424.7 42.1 %collective-permute-done.21.far_high.near_low = f32[2,96,2560]{2,1,0:T(8,128)S(1)} collective-permute-done((f32[2,96,2560]{2,1,0:T(8,128)}, f32[2,96,2560]{2,1,0:T(8,128)S(1)}, u32[]{:S(2)}, u32[]{:S(2)}) %collective-permute-start.21) | collective-permute-done | bytes 1966112 | tf_op jit(solution)/shard_map/ppermute | solution.py:139
  1469.9 4.9 shard_map.161
  1479.7 18.3 %collective-permute-done.23.run_low = f32[96,2560]{1,0:T(8,128)S(1)} collective-permute-done((f32[96,2560]{1,0:T(8,128)}, f32[96,2560]{1,0:T(8,128)S(1)}, u32[]{:S(2)}, u32[]{:S(2)}) %collective-permute-start.23) | collective-permute-done | bytes 983072 | tf_op jit(solution)/shard_map/ppermute | solution.py:139
  1499.9 5.3 shard_map.162
  1511.7 8.0 constant_dynamic-update-slice_fusion.5
  1519.7 9.1 constant_dynamic-update-slice_fusion.4
  1528.7 9.0 constant_dynamic-update-slice_fusion.3
  1537.7 9.1 constant_dynamic-update-slice_fusion.2
  1550.6 7.0 constant_dynamic-update-slice_fusion.1
  (161 shorter events, 127.5 us)
Async XLA Ops:
  7.2 163.0 %copy-start = (bf16[5120,128]{1,0:T(8,128)(2,1)S(1)}, bf16[5120,128]{1,0:T(8,128)(2,1)}, u32[]{:S(2)}) copy-start(bf16[5120,128]{1,0:T(8,128)(2,1)} %param.17) | copy-start | bytes 3932164
  7.2 6.8 copy-start.20
  7.2 308.8 %all-gather.17.cloned.1.call-start = ((), (), s32[]{:S(2)}) async-start(), calls=%async_computation.1 | async-start | bytes 58982400 | tf_op jit(solution)/shard_map/all_gather | solution.py:186
  14.0 20.4 %copy-start.25 = (bf16[5120,128]{1,0:T(8,128)(2,1)S(1)}, bf16[5120,128]{1,0:T(8,128)(2,1)}, u32[]{:S(2)}) copy-start(bf16[5120,128]{1,0:T(8,128)(2,1)} %param.16) | copy-start | bytes 3932164
  64.4 46.8 %copy-start.3 = (bf16[24,192,1,64,2]{1,0,4,3,2:T(8,128)(2,1)}, bf16[24,192,1,64,2]{1,0,4,3,2:T(8,128)(2,1)S(1)}, u32[]{:S(2)}) copy-start(bf16[24,192,1,64,2]{1,0,4,3,2:T(8,128)(2,1)S(1)} %maximum_convert_fusion) | copy-start | bytes 3538948
  111.2 16.0 %copy-start.22 = (s32[24]{0:T(128)S(1)}, s32[24]{0:T(128)}, u32[]{:S(2)}) copy-start(s32[24]{0:T(128)} %param.14) | copy-start | bytes 292
  127.3 42.9 %copy-start.18 = (pred[24,192]{1,0:T(8,128)(4,1)}, pred[24,192]{1,0:T(8,128)(4,1)S(1)}, u32[]{:S(2)}) copy-start(pred[24,192]{1,0:T(8,128)(4,1)S(1)} %iota_compare_fusion.1) | copy-start | bytes 13828
  140.8 18.4 %copy-start.7 = (pred[24,192,192]{1,2,0:T(8,128)(4,1)S(1)}, pred[24,192,192]{1,2,0:T(8,128)(4,1)}, u32[]{:S(2)}) copy-start(pred[24,192,192]{1,2,0:T(8,128)(4,1)} %broadcast_and_fusion) | copy-start | bytes 2654212
  218.1 21.3 %copy-start.21 = (bf16[5120]{0:T(1024)(128)(2,1)S(1)}, bf16[5120]{0:T(1024)(128)(2,1)}, u32[]{:S(2)}) copy-start(bf16[5120]{0:T(1024)(128)(2,1)} %param.23) | copy-start | bytes 30724
  232.4 76.3 %all-to-all-start = ((bf16[8,576,640]{2,1,0:T(8,128)(2,1)}), bf16[8,576,640]{2,1,0:T(8,128)(2,1)}, u32[]{:S(2)}, u32[]{:S(2)}) async-start(bf16[8,576,640]{2,1,0:T(8,128)(2,1)} %reshape.365), calls=%async_computation | async-start | bytes 11796480 | tf_op jit(solution)/shard_map/all_to_all | solution.py:197
  239.4 161.8 %all-gather.19.cloned.1.call-start = ((), (), s32[]{:S(2)}) async-start(), calls=%async_computation.2 | async-start | bytes 8847360 | tf_op jit(solution)/shard_map/all_gather | solution.py:213
  341.6 167.1 %all-gather.21.cloned.1.call-start = ((), (), s32[]{:S(2)}) async-start(), calls=%async_computation.3 | async-start | bytes 11796480 | tf_op jit(solution)/shard_map/all_gather | solution.py:213
  393.1 2.3 copy-start.2
  397.5 316.9 %all-gather.23.cloned.1.call-start = ((), (), s32[]{:S(2)}) async-start(), calls=%async_computation.4 | async-start | bytes 11796480 | tf_op jit(solution)/shard_map/all_gather | solution.py:213
  398.1 570.0 %all-gather.25.cloned.1.call-start = ((), (), s32[]{:S(2)}) async-start(), calls=%async_computation.5 | async-start | bytes 11796480 | tf_op jit(solution)/shard_map/all_gather | solution.py:213
  398.8 868.0 %all-gather.27.cloned.1.call-start = ((), (), s32[]{:S(2)}) async-start(), calls=%async_computation.6 | async-start | bytes 8847360 | tf_op jit(solution)/shard_map/all_gather | solution.py:213
  401.1 1110.6 %all-gather.29.cloned.1.call-start = ((), (), s32[]{:S(2)}) async-start(), calls=%async_computation.7 | async-start | bytes 8847360 | tf_op jit(solution)/shard_map/all_gather | solution.py:225
  401.2 34.9 %copy-start.24 = (bf16[768,5120]{1,0:T(8,128)(2,1)S(1)}, bf16[768,5120]{1,0:T(8,128)(2,1)}, u32[]{:S(2)}) copy-start(bf16[768,5120]{1,0:T(8,128)(2,1)} %all-gather.19.cloned.1.call-done) | copy-start | bytes 23592964
  508.2 141.6 %collective-permute-start = (bf16[4,96,5120]{2,1,0:T(8,128)(2,1)}, bf16[4,96,5120]{2,1,0:T(8,128)(2,1)}, u32[]{:S(2)}, u32[]{:S(2)}) collective-permute-start(bf16[4,96,5120]{2,1,0:T(8,128)(2,1)} %dynamic-slice_bitcast_fusion.4), channel_id=1, source_target_pairs={{0,1},{1,0},{2,3},{3,2},{4,5},{5,4},{6,7},{7,6},{8,9},{9,8},{10,11... | collective-permute-start | bytes 11796488 | tf_op jit(solution)/shard_map/ppermute | solution.py:139
  508.7 47.3 %copy-start.23 = (bf16[1024,5120]{1,0:T(8,128)(2,1)S(1)}, bf16[1024,5120]{1,0:T(8,128)(2,1)}, u32[]{:S(2)}) copy-start(bf16[1024,5120]{1,0:T(8,128)(2,1)} %all-gather.21.cloned.1.call-done) | copy-start | bytes 31457284
  649.1 89.2 %collective-permute-start.5 = (bf16[4,128,5120]{2,1,0:T(8,128)(2,1)}, bf16[4,128,5120]{2,1,0:T(8,128)(2,1)}, u32[]{:S(2)}, u32[]{:S(2)}) collective-permute-start(bf16[4,128,5120]{2,1,0:T(8,128)(2,1)} %dynamic-slice_bitcast_fusion.2), channel_id=1, source_target_pairs={{0,1},{1,0},{2,3},{3,2},{4,5},{5,4},{6,7},{7,6},{8,9},{9,8},{10,11... | collective-permute-start | bytes 15728648 | tf_op jit(solution)/shard_map/ppermute | solution.py:139
  655.4 44.4 %collective-permute-start.1 = (f32[2,96,2560]{2,1,0:T(8,128)}, f32[2,96,2560]{2,1,0:T(8,128)S(1)}, u32[]{:S(2)}, u32[]{:S(2)}) collective-permute-start(f32[2,96,2560]{2,1,0:T(8,128)} %get-tuple-element.52), channel_id=1, source_target_pairs={{0,6},{1,7},{2,0},{3,1},{4,2},{5,3},{6,4},{7,5},{8,14},{9,15},{10,... | collective-permute-start | bytes 5898248 | tf_op jit(solution)/shard_map/ppermute | solution.py:139
  657.5 45.2 %collective-permute-start.2 = (f32[2,96,2560]{2,1,0:T(8,128)}, f32[2,96,2560]{2,1,0:T(8,128)}, u32[]{:S(2)}, u32[]{:S(2)}) collective-permute-start(f32[2,96,2560]{2,1,0:T(8,128)} %get-tuple-element.53), channel_id=1, source_target_pairs={{0,2},{1,3},{2,4},{3,5},{4,6},{5,7},{6,0},{7,1},{8,10},{9,11},{10,... | collective-permute-start | bytes 5898248 | tf_op jit(solution)/shard_map/ppermute | solution.py:139
  699.8 2.9 copy-start.5
  707.6 23.2 %collective-permute-start.3 = (f32[96,2560]{1,0:T(8,128)}, f32[96,2560]{1,0:T(8,128)S(1)}, u32[]{:S(2)}, u32[]{:S(2)}) collective-permute-start(f32[96,2560]{1,0:T(8,128)} %get-tuple-element.54), channel_id=1, source_target_pairs={{0,2},{1,3},{2,4},{3,5},{4,6},{5,7},{6,0},{7,1},{8,10},{9,11},{10,... | collective-permute-start | bytes 2949128 | tf_op jit(solution)/shard_map/ppermute | solution.py:139
  707.6 23.2 %collective-permute-start.4 = (f32[96,2560]{1,0:T(8,128)}, f32[96,2560]{1,0:T(8,128)S(1)}, u32[]{:S(2)}, u32[]{:S(2)}) collective-permute-start(f32[96,2560]{1,0:T(8,128)} %get-tuple-element.55), channel_id=1, source_target_pairs={{0,6},{1,7},{2,0},{3,1},{4,2},{5,3},{6,4},{7,5},{8,14},{9,15},{10,... | collective-permute-start | bytes 2949128 | tf_op jit(solution)/shard_map/ppermute | solution.py:139
  730.8 0.9 copy-start.14
  731.8 1.0 copy-start.15
  738.2 781.5 %all-gather.31.cloned.1.call-start = ((), (), s32[]{:S(2)}) async-start(), calls=%async_computation.8 | async-start | bytes 11796480 | tf_op jit(solution)/shard_map/all_gather | solution.py:225
  744.4 88.2 %collective-permute-start.6 = (f32[2,128,2560]{2,1,0:T(8,128)}, f32[2,128,2560]{2,1,0:T(8,128)}, u32[]{:S(2)}, u32[]{:S(2)}) collective-permute-start(f32[2,128,2560]{2,1,0:T(8,128)} %get-tuple-element.62), channel_id=1, source_target_pairs={{0,6},{1,7},{2,0},{3,1},{4,2},{5,3},{6,4},{7,5},{8,14},{9,15},{10,... | collective-permute-start | bytes 7864328 | tf_op jit(solution)/shard_map/ppermute | solution.py:139
  745.9 90.4 %collective-permute-start.7 = (f32[2,128,2560]{2,1,0:T(8,128)}, f32[2,128,2560]{2,1,0:T(8,128)}, u32[]{:S(2)}, u32[]{:S(2)}) collective-permute-start(f32[2,128,2560]{2,1,0:T(8,128)} %get-tuple-element.63), channel_id=1, source_target_pairs={{0,2},{1,3},{2,4},{3,5},{4,6},{5,7},{6,0},{7,1},{8,10},{9,11},{10,... | collective-permute-start | bytes 7864328 | tf_op jit(solution)/shard_map/ppermute | solution.py:139
  841.6 50.5 %collective-permute-start.8 = (f32[128,2560]{1,0:T(8,128)}, f32[128,2560]{1,0:T(8,128)S(1)}, u32[]{:S(2)}, u32[]{:S(2)}) collective-permute-start(f32[128,2560]{1,0:T(8,128)} %get-tuple-element.64), channel_id=1, source_target_pairs={{0,2},{1,3},{2,4},{3,5},{4,6},{5,7},{6,0},{7,1},{8,10},{9,11},{10,... | collective-permute-start | bytes 3932168 | tf_op jit(solution)/shard_map/ppermute | solution.py:139
  841.6 50.5 %collective-permute-start.9 = (f32[128,2560]{1,0:T(8,128)}, f32[128,2560]{1,0:T(8,128)S(1)}, u32[]{:S(2)}, u32[]{:S(2)}) collective-permute-start(f32[128,2560]{1,0:T(8,128)} %get-tuple-element.65), channel_id=1, source_target_pairs={{0,6},{1,7},{2,0},{3,1},{4,2},{5,3},{6,4},{7,5},{8,14},{9,15},{10,... | collective-permute-start | bytes 3932168 | tf_op jit(solution)/shard_map/ppermute | solution.py:139
  892.1 1.1 copy-start.9
  892.1 1.5 copy-start.12
  899.7 629.0 %all-gather.33.cloned.1.call-start = ((), (), s32[]{:S(2)}) async-start(), calls=%async_computation.9 | async-start | bytes 11796480 | tf_op jit(solution)/shard_map/all_gather | solution.py:225
  948.4 12.2 collective-permute-start.10
  966.7 58.4 %collective-permute-start.11 = (f32[2,128,2560]{2,1,0:T(8,128)}, f32[2,128,2560]{2,1,0:T(8,128)}, u32[]{:S(2)}, u32[]{:S(2)}) collective-permute-start(f32[2,128,2560]{2,1,0:T(8,128)} %get-tuple-element.71), channel_id=1, source_target_pairs={{0,6},{1,7},{2,0},{3,1},{4,2},{5,3},{6,4},{7,5},{8,14},{9,15},{10,... | collective-permute-start | bytes 7864328 | tf_op jit(solution)/shard_map/ppermute | solution.py:139
  966.7 59.7 %collective-permute-start.12 = (f32[2,128,2560]{2,1,0:T(8,128)}, f32[2,128,2560]{2,1,0:T(8,128)}, u32[]{:S(2)}, u32[]{:S(2)}) collective-permute-start(f32[2,128,2560]{2,1,0:T(8,128)} %get-tuple-element.72), channel_id=1, source_target_pairs={{0,2},{1,3},{2,4},{3,5},{4,6},{5,7},{6,0},{7,1},{8,10},{9,11},{10,... | collective-permute-start | bytes 7864328 | tf_op jit(solution)/shard_map/ppermute | solution.py:139
  1031.6 48.6 %collective-permute-start.13 = (f32[128,2560]{1,0:T(8,128)}, f32[128,2560]{1,0:T(8,128)S(1)}, u32[]{:S(2)}, u32[]{:S(2)}) collective-permute-start(f32[128,2560]{1,0:T(8,128)} %get-tuple-element.73), channel_id=1, source_target_pairs={{0,2},{1,3},{2,4},{3,5},{4,6},{5,7},{6,0},{7,1},{8,10},{9,11},{10,... | collective-permute-start | bytes 3932168 | tf_op jit(solution)/shard_map/ppermute | solution.py:139
  1031.6 48.6 %collective-permute-start.14 = (f32[128,2560]{1,0:T(8,128)}, f32[128,2560]{1,0:T(8,128)S(1)}, u32[]{:S(2)}, u32[]{:S(2)}) collective-permute-start(f32[128,2560]{1,0:T(8,128)} %get-tuple-element.74), channel_id=1, source_target_pairs={{0,6},{1,7},{2,0},{3,1},{4,2},{5,3},{6,4},{7,5},{8,14},{9,15},{10,... | collective-permute-start | bytes 3932168 | tf_op jit(solution)/shard_map/ppermute | solution.py:139
  1080.2 1.1 copy-start.10
  1080.2 1.5 copy-start.13
  1087.8 449.9 %all-gather.35.cloned.1.call-start = ((), (), s32[]{:S(2)}) async-start(), calls=%async_computation.10 | async-start | bytes 11796480 | tf_op jit(solution)/shard_map/all_gather | solution.py:225
  1181.9 11.1 collective-permute-start.15
  1199.1 58.4 %collective-permute-start.16 = (f32[2,128,2560]{2,1,0:T(8,128)}, f32[2,128,2560]{2,1,0:T(8,128)}, u32[]{:S(2)}, u32[]{:S(2)}) collective-permute-start(f32[2,128,2560]{2,1,0:T(8,128)} %get-tuple-element.80), channel_id=1, source_target_pairs={{0,6},{1,7},{2,0},{3,1},{4,2},{5,3},{6,4},{7,5},{8,14},{9,15},{10,... | collective-permute-start | bytes 7864328 | tf_op jit(solution)/shard_map/ppermute | solution.py:139
  1199.1 59.7 %collective-permute-start.17 = (f32[2,128,2560]{2,1,0:T(8,128)}, f32[2,128,2560]{2,1,0:T(8,128)}, u32[]{:S(2)}, u32[]{:S(2)}) collective-permute-start(f32[2,128,2560]{2,1,0:T(8,128)} %get-tuple-element.81), channel_id=1, source_target_pairs={{0,2},{1,3},{2,4},{3,5},{4,6},{5,7},{6,0},{7,1},{8,10},{9,11},{10,... | collective-permute-start | bytes 7864328 | tf_op jit(solution)/shard_map/ppermute | solution.py:139
  1264.1 30.5 %collective-permute-start.18 = (f32[128,2560]{1,0:T(8,128)}, f32[128,2560]{1,0:T(8,128)S(1)}, u32[]{:S(2)}, u32[]{:S(2)}) collective-permute-start(f32[128,2560]{1,0:T(8,128)} %get-tuple-element.82), channel_id=1, source_target_pairs={{0,2},{1,3},{2,4},{3,5},{4,6},{5,7},{6,0},{7,1},{8,10},{9,11},{10,... | collective-permute-start | bytes 3932168 | tf_op jit(solution)/shard_map/ppermute | solution.py:139
  1264.1 30.5 %collective-permute-start.19 = (f32[128,2560]{1,0:T(8,128)}, f32[128,2560]{1,0:T(8,128)S(1)}, u32[]{:S(2)}, u32[]{:S(2)}) collective-permute-start(f32[128,2560]{1,0:T(8,128)} %get-tuple-element.83), channel_id=1, source_target_pairs={{0,6},{1,7},{2,0},{3,1},{4,2},{5,3},{6,4},{7,5},{8,14},{9,15},{10,... | collective-permute-start | bytes 3932168 | tf_op jit(solution)/shard_map/ppermute | solution.py:139
  1294.6 1.1 copy-start.8
  1294.6 1.5 copy-start.11
  1302.2 248.4 %all-gather.37.cloned.1.call-start = ((), (), s32[]{:S(2)}) async-start(), calls=%async_computation.11 | async-start | bytes 8847360 | tf_op jit(solution)/shard_map/all_gather | solution.py:225
  1408.1 8.7 collective-permute-start.20
  1422.5 44.3 %collective-permute-start.21 = (f32[2,96,2560]{2,1,0:T(8,128)}, f32[2,96,2560]{2,1,0:T(8,128)S(1)}, u32[]{:S(2)}, u32[]{:S(2)}) collective-permute-start(f32[2,96,2560]{2,1,0:T(8,128)} %get-tuple-element.89), channel_id=1, source_target_pairs={{0,6},{1,7},{2,0},{3,1},{4,2},{5,3},{6,4},{7,5},{8,14},{9,15},{10,... | collective-permute-start | bytes 5898248 | tf_op jit(solution)/shard_map/ppermute | solution.py:139
  1424.7 45.2 %collective-permute-start.22 = (f32[2,96,2560]{2,1,0:T(8,128)}, f32[2,96,2560]{2,1,0:T(8,128)}, u32[]{:S(2)}, u32[]{:S(2)}) collective-permute-start(f32[2,96,2560]{2,1,0:T(8,128)} %get-tuple-element.90), channel_id=1, source_target_pairs={{0,2},{1,3},{2,4},{3,5},{4,6},{5,7},{6,0},{7,1},{8,10},{9,11},{10,... | collective-permute-start | bytes 5898248 | tf_op jit(solution)/shard_map/ppermute | solution.py:139
  1466.8 3.1 copy-start.6
  1474.8 23.2 %collective-permute-start.23 = (f32[96,2560]{1,0:T(8,128)}, f32[96,2560]{1,0:T(8,128)S(1)}, u32[]{:S(2)}, u32[]{:S(2)}) collective-permute-start(f32[96,2560]{1,0:T(8,128)} %get-tuple-element.91), channel_id=1, source_target_pairs={{0,2},{1,3},{2,4},{3,5},{4,6},{5,7},{6,0},{7,1},{8,10},{9,11},{10,... | collective-permute-start | bytes 2949128 | tf_op jit(solution)/shard_map/ppermute | solution.py:139
  1474.8 23.2 %collective-permute-start.24 = (f32[96,2560]{1,0:T(8,128)}, f32[96,2560]{1,0:T(8,128)S(1)}, u32[]{:S(2)}, u32[]{:S(2)}) collective-permute-start(f32[96,2560]{1,0:T(8,128)} %get-tuple-element.92), channel_id=1, source_target_pairs={{0,6},{1,7},{2,0},{3,1},{4,2},{5,3},{6,4},{7,5},{8,14},{9,15},{10,... | collective-permute-start | bytes 2949128 | tf_op jit(solution)/shard_map/ppermute | solution.py:139
  1498.0 0.9 copy-start.16
  1499.0 1.0 copy-start.17
  1505.3 1.4 copy-start.4
  1505.3 1.4 copy-start.19
  1537.7 19.9 %copy-start.1 = (bf16[5120,128]{1,0:T(8,128)(2,1)S(1)}, bf16[5120,128]{1,0:T(8,128)(2,1)}, u32[]{:S(2)}) copy-start(bf16[5120,128]{1,0:T(8,128)(2,1)} %param.17) | copy-start | bytes 3932164
Sparse Core Ops, SparseCore 0:
  14.1 238.6 all-gather.16
  341.7 44.3 all-gather.18
  397.6 55.3 all-gather.20
  454.4 54.6 all-gather.22
  510.5 54.8 all-gather.24
  566.9 43.6 all-gather.26
  738.3 76.6 all-gather.28
  899.8 55.8 all-gather.30
  1088.0 54.5 all-gather.32
  1302.3 56.2 all-gather.34
  1505.5 45.0 all-gather.36

commit v4 on v3

--- a/solution.py
+++ b/solution.py
@@ -8,8 +8,8 @@
 
 EPS = 1e-5
 ROPE_BASE = 10000.0
-CHUNK_PARTS = (3, 4, 4, 4, 3)
-TILE = 32
+CHUNK_PARTS = (8, 7, 6, 6, 6, 3)
+TILES = (32, 16)
 
 
 def rms_norm(rows, gain):
@@ -73,6 +73,10 @@
     )(o_rows, w_full, x_rows)
 
 
+def row_tile(rows):
+    return next(tile for tile in TILES if rows % tile == 0)
+
+
 def wide(ref):
     return ref[...].reshape(ref.shape[-2:]).astype(jnp.float32)
 
@@ -100,7 +104,7 @@
 def ring_call(kernel, where, operands, specs, out_shapes, out_specs, rows):
     return pl.pallas_call(
         kernel,
-        grid_spec=pltpu.PrefetchScalarGridSpec(num_scalar_prefetch=1, grid=(rows // TILE,), in_specs=specs, out_specs=out_specs),
+        grid_spec=pltpu.PrefetchScalarGridSpec(num_scalar_prefetch=1, grid=(rows // row_tile(rows),), in_specs=specs, out_specs=out_specs),
         out_shape=out_shapes,
     )(where, *operands)
 
@@ -132,6 +136,7 @@
     def reduce_rows(partial, give, resid_rows, where):
         rows, width = resid_rows.shape
         half = width // 2
+        tile = row_tile(rows)
         own, up, far, down = range(4)
         low, high = 0, 1
 
@@ -139,17 +144,17 @@
             return lax.ppermute(piece, "tp", perm)
 
         def at(place, side):
-            mine = pl.BlockSpec((1, 1, TILE, half), lambda n, where_ref: (where_ref[place], where_ref[4], n, side))
-            theirs = pl.BlockSpec((1, TILE, half), lambda n, where_ref: (where_ref[place], n, side))
+            mine = pl.BlockSpec((1, 1, tile, half), lambda n, where_ref: (where_ref[place], where_ref[4], n, side))
+            theirs = pl.BlockSpec((1, tile, half), lambda n, where_ref: (where_ref[place], n, side))
             return [mine, theirs]
 
         def part(side):
-            return pl.BlockSpec((1, TILE, half), lambda n, where_ref: (side, n, 0))
-
-        flat = pl.BlockSpec((TILE, half), lambda n, where_ref: (n, 0))
-        full = pl.BlockSpec((TILE, width), lambda n, where_ref: (n, 0))
+            return pl.BlockSpec((1, tile, half), lambda n, where_ref: (side, n, 0))
+
+        flat = pl.BlockSpec((tile, half), lambda n, where_ref: (n, 0))
+        full = pl.BlockSpec((tile, width), lambda n, where_ref: (n, 0))
         message = jax.ShapeDtypeStruct((2, rows, half), jnp.float32)
-        message_spec = pl.BlockSpec((2, TILE, half), lambda n, where_ref: (0, n, 0))
+        message_spec = pl.BlockSpec((2, tile, half), lambda n, where_ref: (0, n, 0))
         running = jax.ShapeDtypeStruct((rows, half), jnp.float32)
 
         got = move(give, partner_perm)

time: 1580 us -> 1560 us (0.987)
  waiting for transfers between devices: 410 us -> 337 us
  matrix products: 741 us -> 767 us
    ppermute x25 -> x30, waiting for transfers between devices: 337 us -> 268 us  [move(): return lax.ppermute(piece, 'tp', perm)]
    pallas_call x15 -> x18, Pallas kernels: 84.1 us -> 99.3 us  [ring_call(): pl.pallas_call(kernel, grid_spec=pltpu.PrefetchScalarGridSpec(num_scalar_...]
    dot_general x5 -> x6, matrix products: 201 us -> 211 us  [layer_shard(): jnp.dot(gated, w_down, preferred_element_type=jnp.float32)]
    dot_general x5 -> x6, matrix products: 209 us -> 217 us  [layer_shard(): up_pre = jnp.dot(normed_mlp, w_up, preferred_element_type=jnp.float32)]
    dot_general x5 -> x6, matrix products: 208 us -> 216 us  [layer_shard(): gate_pre = jnp.dot(normed_mlp, w_gate, preferred_element_type=jnp.float32)]
    ppermute x25 -> x30, starting transfers between devices: 30.8 us -> 37.7 us  [move(): return lax.ppermute(piece, 'tp', perm)]
    dynamic_update_slice x5 -> x6, local copies, waits for them, and re-layouts: 42.1 us -> 42.8 us  [layer_shard(): y = lax.dynamic_update_slice(y, y_chunk, (0, start, 0))]
  transfers between devices with their start and end apart: 37 -> 44, of which waited for: 18 -> 20; matrix products, arithmetic and copies ran while one was open for 59% -> 62% of each run, Pallas kernels for 8% -> 9%
where the time goes in v4:
time: 1560 us; the launch traced here: 1550 us
  matrix products  767 us (49%)
  waiting for transfers between devices  337 us (22%)
  local copies, waits for them, and re-layouts  164 us (11%)
  Pallas kernels  158 us (10%)
  other arithmetic  60.9 us (4%)
  starting transfers between devices  45.6 us (3%)
    ppermute x30, waiting for transfers between devices, move(): return lax.ppermute(piece, 'tp', perm)  268 us
    dot_general x6, matrix products, layer_shard(): up_pre = jnp.dot(normed_mlp, w_up, preferred_element_type=jnp.float32)  217 us
    dot_general x6, matrix products, layer_shard(): gate_pre = jnp.dot(normed_mlp, w_gate, preferred_element_type=jnp.float32)  216 us
    dot_general x6, matrix products, layer_shard(): jnp.dot(gated, w_down, preferred_element_type=jnp.float32)  211 us
    pallas_call x18, Pallas kernels, ring_call(): pl.pallas_call(kernel, grid_spec=pltpu.PrefetchScalarGridSpec(num_scalar_...  99.3 us
    all_to_all x1, waiting for transfers between devices, layer_shard(): o_rows = lax.all_to_all(attn_rows, 'tp', 0, 0, tiled=True)  66.7 us
    pallas_call x2, Pallas kernels, out_project(): pl.pallas_call(out_kernel, grid=(width // tile,), in_specs=[pl.BlockSpec(...  58.4 us
    dot_general x1, matrix products, layer_shard(): jnp.einsum('bsd,dk->bsk', normed, w_query, preferred_element_type=jnp.flo...  44.9 us
  transfers between devices with their start and end apart: 44, of which 20 were waited for; matrix products, arithmetic and copies ran while one was open for 62% of the time, Pallas kernels for 9%

profile of v4, /device:TPU:113, one launch (start us, length us, event | category | flops | bytes accessed | tf_op | source)
XLA Modules:
  0.0 1546.6 jit_solution(17303648359614916692)
XLA Ops:
  14.1 20.4 %fusion = f32[24,192]{1,0:T(8,128)S(1)} fusion(bf16[24,192,5120]{2,1,0:T(8,128)(2,1)} %param.13), kind=kLoop, calls=%fused_computation.2 | loop fusion | flops 70774272 | bytes 47204352 | tf_op jit(solution)/shard_map/reduce_sum | solution.py:17
  34.5 23.4 %fusion.5 = f32[24,192,128]{2,1,0:T(8,128)} fusion(bf16[24,192,5120]{2,1,0:T(8,128)(2,1)} %param.13, f32[5120]{0:T(1024)S(1)} %convert_element_type.146, f32[24,192]{1,0:T(8,128)S(1)} %add_rsqrt_fusion, bf16[5120,128]{1,0:T(8,128)(2,1)S(1)} %copy-done.32), kind=kOutput, calls=%fused_computation.6 | convolution fusion | flops 6134169600 | bytes 50894848 | tf_op jit(solution)/shard_map/bsd,dk->bsk/dot_general | solution.py:194
  66.4 44.9 %fusion.3 = f32[24,192,640]{2,1,0:T(8,128)} fusion(bf16[24,192,5120]{2,1,0:T(8,128)(2,1)} %param.13, f32[5120]{0:T(1024)S(1)} %convert_element_type.146, f32[24,192]{1,0:T(8,128)S(1)} %add_rsqrt_fusion, bf16[5120,640]{1,0:T(8,128)(2,1)} %param.15), kind=kOutput, calls=%fused_computation.5 | convolution fusion | flops 30293360640 | bytes 65574912 | tf_op jit(solution)/shard_map/bsd,dk->bsk/dot_general | solution.py:193
  111.3 15.9 %copy.22 = f32[24,192,640]{1,0,2:T(8,128)} copy(f32[24,192,640]{2,1,0:T(8,128)} %fusion.3) | data formatting | bytes 23592960 | tf_op jit(solution)/shard_map/bsd,dk->bsk/dot_general | solution.py:193
  129.5 7.0 subtract_convert_fusion
  140.8 18.4 %fusion.10 = (f32[24,5,192]{2,1,0:T(8,128)S(1)}, f32[24,192,192,5]{2,1,3,0:T(8,128)}) fusion(pred[24,192,192]{1,2,0:T(8,128)(4,1)} %broadcast_and_fusion, bf16[24,192,5,128]{1,0,3,2:T(8,128)(2,1)} %bitcast.202, bf16[24,192,128]{2,1,0:T(8,128)(2,1)} %copy.21, pred[24,192]{1,0:T(8,128)(4,1)S(1)} %iota_compare_fusion.1), kind=kOutput, calls=%fused_computation.12 | convolution fusion | flops 1146299904 | bytes 25754112 | tf_op jit(solution)/shard_map/bqkgh,bskh->bkgqs/dot_general | solution.py:40
  159.2 11.0 fusion.9
  170.2 21.9 %bitcast_dynamic-update-slice_fusion = (bf16[24,384,1,128]{3,1,2,0:T(8,128)(2,1)}, bf16[24,192,128]{2,1,0:T(8,128)(2,1)}) fusion(bf16[24,384,1,128]{3,1,2,0:T(8,128)(2,1)} %copy.49, bf16[5120,128]{1,0:T(8,128)(2,1)S(1)} %copy-done, bf16[24,192,5120]{2,1,0:T(8,128)(2,1)} %param.13, f32[5120]{0:T(1024)S(1)} %convert_element_type.146, ...), kind=kOutput, calls=%fused_computation.66 | convolution fusion | flops 6135349248 | bytes 50899456 | tf_op jit(solution)/shard_map/bsd,dk->bsk/dot_general | solution.py:195
  192.1 14.3 convert_bitcast_fusion
  206.4 11.7 copy.32
  218.1 14.4 reshape.374
  232.4 7.1 all-to-all-start
  242.0 66.7 %all-to-all-done = bf16[8,576,640]{2,1,0:T(8,128)(2,1)} async-done(((bf16[8,576,640]{2,1,0:T(8,128)(2,1)}), bf16[8,576,640]{2,1,0:T(8,128)(2,1)}, u32[]{:S(2)}, u32[]{:S(2)}) %all-to-all-start) | async-done | bytes 5898272 | tf_op jit(solution)/shard_map/all_to_all | solution.py:202
  316.1 21.4 %out_project.2.resid_ref = bf16[128,5120]{1,0:T(8,128)(2,1)} custom-call(bf16[8,128,640]{2,1,0:T(8,128)(2,1)} %slice.76.o_ref, bf16[5120,5120]{1,0:T(8,128)(2,1)} %all-gather.20.cloned.1.call-done.w_ref, bf16[128,5120]{1,0:T(8,128)(2,1)} %constant_dynamic-slice_fusion.x_ref), custom_call_target="tpu_custom_call" | custom-call | flops 6710886400 | bytes 52428800 | tf_op jit(solution)/shard_map/out_project/pallas_call | solution.py:60
  346.8 37.0 %out_project.3 = bf16[448,5120]{1,0:T(8,128)(2,1)} custom-call(bf16[8,448,640]{2,1,0:T(8,128)(2,1)} %slice.77.o_ref, bf16[5120,5120]{1,0:T(8,128)(2,1)} %all-gather.20.cloned.1.call-done.w_ref, bf16[448,5120]{1,0:T(8,128)(2,1)} %constant_dynamic-slice_fusion.1.x_ref), custom_call_target="tpu_custom_call" | custom-call | flops 23488102400 | bytes 52428800 | tf_op jit(solution)/shard_map/out_project/pallas_call | solution.py:60
  399.6 47.3 %fusion.52 = f32[1024,3456]{1,0:T(8,128)} fusion(bf16[1024,5120]{1,0:T(8,128)(2,1)} %all-gather.22.cloned.1.call-done, bf16[5120,3456]{1,0:T(8,128)(2,1)} %param.19), kind=kOutput, calls=%fused_computation.97 | convolution fusion | flops 36238786560 | bytes 60030976 | tf_op jit(solution)/shard_map/dot_general | solution.py:221
  446.9 44.1 %multiply_convert_fusion = bf16[1024,3456]{1,0:T(8,128)(2,1)S(1)} fusion(f32[1024,3456]{1,0:T(8,128)} %fusion.52, bf16[1024,5120]{1,0:T(8,128)(2,1)S(1)} %copy-done.29, bf16[5120,3456]{1,0:T(8,128)(2,1)} %param.20), kind=kOutput, calls=%fused_computation.13 | convolution fusion | flops 36260020224 | bytes 67108864 | tf_op jit(solution)/shard_map/dot_general | solution.py:222
  491.0 44.0 %convolution_convert_fusion = bf16[1024,5120]{1,0:T(8,128)(2,1)} fusion(bf16[1024,3456]{1,0:T(8,128)(2,1)S(1)} %multiply_convert_fusion, bf16[3456,5120]{1,0:T(8,128)(2,1)} %param.21), kind=kOutput, calls=%fused_computation.23 | convolution fusion | flops 36244029440 | bytes 52953088 | tf_op jit(solution)/shard_map/dot_general | solution.py:224
  535.0 5.3 dynamic-slice_bitcast_fusion
  545.7 5.0 collective-permute-done.far_b.far_d.up_b.down_b.low_b.high_b
  550.7 6.2 shard_map.148
  558.9 40.8 %fusion.53 = f32[896,3456]{1,0:T(8,128)} fusion(bf16[896,5120]{1,0:T(8,128)(2,1)} %all-gather.24.cloned.1.call-done, bf16[5120,3456]{1,0:T(8,128)(2,1)} %param.19), kind=kOutput, calls=%fused_computation.98 | convolution fusion | flops 31708938240 | bytes 56950784 | tf_op jit(solution)/shard_map/dot_general | solution.py:221
  599.8 52.7 %collective-permute-done.1.far_high.near_low = f32[2,128,2560]{2,1,0:T(8,128)} collective-permute-done((f32[2,128,2560]{2,1,0:T(8,128)}, f32[2,128,2560]{2,1,0:T(8,128)}, u32[]{:S(2)}, u32[]{:S(2)}) %collective-permute-start.1) | collective-permute-done | bytes 2621472 | tf_op jit(solution)/shard_map/ppermute | solution.py:144
  653.0 5.3 shard_map.149
  660.9 42.4 %multiply_convert_fusion.1 = bf16[896,3456]{1,0:T(8,128)(2,1)} fusion(f32[896,3456]{1,0:T(8,128)} %fusion.53, bf16[896,5120]{1,0:T(8,128)(2,1)} %all-gather.24.cloned.1.call-done, bf16[5120,3456]{1,0:T(8,128)(2,1)} %param.20), kind=kOutput, calls=%fused_computation.14 | convolution fusion | flops 31727517696 | bytes 63143936 | tf_op jit(solution)/shard_map/dot_general | solution.py:222
  705.4 6.0 shard_map.150
  711.6 40.4 %convolution_convert_fusion.1 = bf16[896,5120]{1,0:T(8,128)(2,1)} fusion(bf16[896,3456]{1,0:T(8,128)(2,1)} %multiply_convert_fusion.1, bf16[3456,5120]{1,0:T(8,128)(2,1)} %param.21), kind=kOutput, calls=%fused_computation.27 | convolution fusion | flops 31713525760 | bytes 50757632 | tf_op jit(solution)/shard_map/dot_general | solution.py:224
  756.7 33.4 %fusion.54 = f32[768,3456]{1,0:T(8,128)} fusion(bf16[768,5120]{1,0:T(8,128)(2,1)S(1)} %copy-done.30, bf16[5120,3456]{1,0:T(8,128)(2,1)} %param.19), kind=kOutput, calls=%fused_computation.99 | convolution fusion | flops 27179089920 | bytes 53870592 | tf_op jit(solution)/shard_map/dot_general | solution.py:221
  790.1 7.7 shard_map.151
  799.3 37.0 %multiply_convert_fusion.4 = bf16[768,3456]{1,0:T(8,128)(2,1)} fusion(f32[768,3456]{1,0:T(8,128)} %fusion.54, bf16[768,5120]{1,0:T(8,128)(2,1)} %all-gather.26.cloned.1.call-done, bf16[5120,3456]{1,0:T(8,128)(2,1)} %param.20), kind=kOutput, calls=%fused_computation.22 | convolution fusion | flops 27195015168 | bytes 59179008 | tf_op jit(solution)/shard_map/dot_general | solution.py:222
  836.3 11.6 collective-permute-done.6.far_high.near_low
  849.2 6.5 shard_map.152
  858.4 35.2 %convolution_convert_fusion.4 = bf16[768,5120]{1,0:T(8,128)(2,1)} fusion(bf16[768,3456]{1,0:T(8,128)(2,1)} %multiply_convert_fusion.4, bf16[3456,5120]{1,0:T(8,128)(2,1)} %param.21), kind=kOutput, calls=%fused_computation.30 | convolution fusion | flops 27183022080 | bytes 48562176 | tf_op jit(solution)/shard_map/dot_general | solution.py:224
  895.7 7.2 shard_map.153
  912.2 7.0 collective-permute-done.10.far_b.far_d.up_b.down_b.low_b.high_b
  919.2 5.7 shard_map.154
  926.4 35.7 %fusion.55 = f32[768,3456]{1,0:T(8,128)} fusion(bf16[768,5120]{1,0:T(8,128)(2,1)} %all-gather.28.cloned.1.call-done, bf16[5120,3456]{1,0:T(8,128)(2,1)} %param.19), kind=kOutput, calls=%fused_computation.100 | convolution fusion | flops 27179089920 | bytes 53870592 | tf_op jit(solution)/shard_map/dot_general | solution.py:221
  962.2 30.8 %collective-permute-done.11.far_high.near_low = f32[2,96,2560]{2,1,0:T(8,128)S(1)} collective-permute-done((f32[2,96,2560]{2,1,0:T(8,128)}, f32[2,96,2560]{2,1,0:T(8,128)S(1)}, u32[]{:S(2)}, u32[]{:S(2)}) %collective-permute-start.11) | collective-permute-done | bytes 1966112 | tf_op jit(solution)/shard_map/ppermute | solution.py:144
  1001.8 37.0 %multiply_convert_fusion.3 = bf16[768,3456]{1,0:T(8,128)(2,1)} fusion(f32[768,3456]{1,0:T(8,128)} %fusion.55, bf16[768,5120]{1,0:T(8,128)(2,1)} %all-gather.28.cloned.1.call-done, bf16[5120,3456]{1,0:T(8,128)(2,1)} %param.20), kind=kOutput, calls=%fused_computation.21 | convolution fusion | flops 27195015168 | bytes 59179008 | tf_op jit(solution)/shard_map/dot_general | solution.py:222
  1040.1 5.3 shard_map.156
  1045.5 35.5 %convolution_convert_fusion.3 = bf16[768,5120]{1,0:T(8,128)(2,1)} fusion(bf16[768,3456]{1,0:T(8,128)(2,1)} %multiply_convert_fusion.3, bf16[3456,5120]{1,0:T(8,128)(2,1)} %param.21), kind=kOutput, calls=%fused_computation.29 | convolution fusion | flops 27183022080 | bytes 48562176 | tf_op jit(solution)/shard_map/dot_general | solution.py:224
  1084.9 7.2 collective-permute-done.15.far_b.far_d.up_b.down_b.low_b.high_b
  1092.1 5.7 shard_map.157
  1099.3 42.9 %collective-permute-done.16.far_high.near_low = f32[2,96,2560]{2,1,0:T(8,128)S(1)} collective-permute-done((f32[2,96,2560]{2,1,0:T(8,128)}, f32[2,96,2560]{2,1,0:T(8,128)S(1)}, u32[]{:S(2)}, u32[]{:S(2)}) %collective-permute-start.16) | collective-permute-done | bytes 1966112 | tf_op jit(solution)/shard_map/ppermute | solution.py:144
  1143.5 4.9 shard_map.158
  1151.0 35.5 %fusion.56 = f32[768,3456]{1,0:T(8,128)} fusion(bf16[768,5120]{1,0:T(8,128)(2,1)} %all-gather.30.cloned.1.call-done, bf16[5120,3456]{1,0:T(8,128)(2,1)} %param.19), kind=kOutput, calls=%fused_computation.101 | convolution fusion | flops 27179089920 | bytes 53870592 | tf_op jit(solution)/shard_map/dot_general | solution.py:221
  1187.9 5.3 shard_map.159
  1193.3 36.5 %multiply_convert_fusion.2 = bf16[768,3456]{1,0:T(8,128)(2,1)S(1)} fusion(f32[768,3456]{1,0:T(8,128)} %fusion.56, bf16[768,5120]{1,0:T(8,128)(2,1)} %all-gather.30.cloned.1.call-done, bf16[5120,3456]{1,0:T(8,128)(2,1)} %param.20), kind=kOutput, calls=%fused_computation.20 | convolution fusion | flops 27195015168 | bytes 59179008 | tf_op jit(solution)/shard_map/dot_general | solution.py:222
  1229.8 33.4 %convolution_convert_fusion.2 = bf16[768,5120]{1,0:T(8,128)(2,1)} fusion(bf16[768,3456]{1,0:T(8,128)(2,1)S(1)} %multiply_convert_fusion.2, bf16[3456,5120]{1,0:T(8,128)(2,1)} %param.21), kind=kOutput, calls=%fused_computation.28 | convolution fusion | flops 27183022080 | bytes 48562176 | tf_op jit(solution)/shard_map/dot_general | solution.py:224
  1268.0 6.5 collective-permute-done.20.far_b.far_d.up_b.down_b.low_b.high_b
  1274.5 5.7 shard_map.160
  1281.7 42.9 %collective-permute-done.21.far_high.near_low = f32[2,96,2560]{2,1,0:T(8,128)S(1)} collective-permute-done((f32[2,96,2560]{2,1,0:T(8,128)}, f32[2,96,2560]{2,1,0:T(8,128)S(1)}, u32[]{:S(2)}, u32[]{:S(2)}) %collective-permute-start.21) | collective-permute-done | bytes 1966112 | tf_op jit(solution)/shard_map/ppermute | solution.py:144
  1333.4 20.8 %collective-permute-done.23.run_low = f32[96,2560]{1,0:T(8,128)S(1)} collective-permute-done((f32[96,2560]{1,0:T(8,128)}, f32[96,2560]{1,0:T(8,128)S(1)}, u32[]{:S(2)}, u32[]{:S(2)}) %collective-permute-start.23) | collective-permute-done | bytes 983072 | tf_op jit(solution)/shard_map/ppermute | solution.py:144
  1355.6 5.3 shard_map.162
  1361.1 23.5 %fusion.57 = f32[384,3456]{1,0:T(8,128)S(1)} fusion(bf16[384,5120]{1,0:T(8,128)(2,1)} %all-gather.32.cloned.1.call-done, bf16[5120,3456]{1,0:T(8,128)(2,1)} %param.19), kind=kOutput, calls=%fused_computation.102 | convolution fusion | flops 13589544960 | bytes 44630016 | tf_op jit(solution)/shard_map/dot_general | solution.py:221
  1384.6 20.6 %fusion.20.clone.4 = bf16[384,3456]{1,0:T(8,128)(2,1)S(1)} fusion(bf16[384,5120]{1,0:T(8,128)(2,1)S(1)} %copy-done.31, bf16[5120,3456]{1,0:T(8,128)(2,1)} %param.20, f32[384,3456]{1,0:T(8,128)S(1)} %fusion.57), kind=kOutput, calls=%fused_computation.40.clone.clone.clone.1 | convolution fusion | flops 13597507584 | bytes 47284224 | tf_op jit(solution)/shard_map/dot_general | solution.py:222
  1405.2 22.0 %convolution_convert_fusion.5 = bf16[384,5120]{1,0:T(8,128)(2,1)} fusion(bf16[3456,5120]{1,0:T(8,128)(2,1)} %param.21, bf16[384,3456]{1,0:T(8,128)(2,1)S(1)} %fusion.20.clone.4), kind=kOutput, calls=%fused_computation.36 | convolution fusion | flops 13591511040 | bytes 41975808 | tf_op jit(solution)/shard_map/dot_general | solution.py:224
  1442.8 21.1 %collective-permute-done.26.far_high.near_low = f32[2,48,2560]{2,1,0:T(8,128)S(1)} collective-permute-done((f32[2,48,2560]{2,1,0:T(8,128)}, f32[2,48,2560]{2,1,0:T(8,128)S(1)}, u32[]{:S(2)}, u32[]{:S(2)}) %collective-permute-start.26) | collective-permute-done | bytes 983072 | tf_op jit(solution)/shard_map/ppermute | solution.py:144
  1476.4 8.1 collective-permute-done.28.run_low
  1496.8 9.4 constant_dynamic-update-slice_fusion.6
  1506.2 8.1 constant_dynamic-update-slice_fusion.5
  1514.2 7.0 constant_dynamic-update-slice_fusion.4
  1521.3 7.0 constant_dynamic-update-slice_fusion.3
  1528.2 7.1 constant_dynamic-update-slice_fusion.2
  (206 shorter events, 174.6 us)
Async XLA Ops:
  7.2 163.0 %copy-start = (bf16[5120,128]{1,0:T(8,128)(2,1)S(1)}, bf16[5120,128]{1,0:T(8,128)(2,1)}, u32[]{:S(2)}) copy-start(bf16[5120,128]{1,0:T(8,128)(2,1)} %param.17) | copy-start | bytes 3932164
  7.2 6.8 copy-start.26
  7.2 308.9 %all-gather.20.cloned.1.call-start = ((), (), s32[]{:S(2)}) async-start(), calls=%async_computation.1 | async-start | bytes 58982400 | tf_op jit(solution)/shard_map/all_gather | solution.py:191
  14.0 20.4 %copy-start.32 = (bf16[5120,128]{1,0:T(8,128)(2,1)S(1)}, bf16[5120,128]{1,0:T(8,128)(2,1)}, u32[]{:S(2)}) copy-start(bf16[5120,128]{1,0:T(8,128)(2,1)} %param.16) | copy-start | bytes 3932164
  64.5 46.9 %copy-start.4 = (bf16[24,192,1,64,2]{1,0,4,3,2:T(8,128)(2,1)}, bf16[24,192,1,64,2]{1,0,4,3,2:T(8,128)(2,1)S(1)}, u32[]{:S(2)}) copy-start(bf16[24,192,1,64,2]{1,0,4,3,2:T(8,128)(2,1)S(1)} %maximum_convert_fusion) | copy-start | bytes 3538948
  111.3 16.0 %copy-start.28 = (s32[24]{0:T(128)S(1)}, s32[24]{0:T(128)}, u32[]{:S(2)}) copy-start(s32[24]{0:T(128)} %param.14) | copy-start | bytes 292
  127.4 42.8 %copy-start.24 = (pred[24,192]{1,0:T(8,128)(4,1)}, pred[24,192]{1,0:T(8,128)(4,1)S(1)}, u32[]{:S(2)}) copy-start(pred[24,192]{1,0:T(8,128)(4,1)S(1)} %iota_compare_fusion.1) | copy-start | bytes 13828
  140.8 18.4 %copy-start.9 = (pred[24,192,192]{1,2,0:T(8,128)(4,1)S(1)}, pred[24,192,192]{1,2,0:T(8,128)(4,1)}, u32[]{:S(2)}) copy-start(pred[24,192,192]{1,2,0:T(8,128)(4,1)} %broadcast_and_fusion) | copy-start | bytes 2654212
  232.4 7.1 copy-start.27
  232.4 76.3 %all-to-all-start = ((bf16[8,576,640]{2,1,0:T(8,128)(2,1)}), bf16[8,576,640]{2,1,0:T(8,128)(2,1)}, u32[]{:S(2)}, u32[]{:S(2)}) async-start(bf16[8,576,640]{2,1,0:T(8,128)(2,1)} %reshape.374), calls=%async_computation | async-start | bytes 11796480 | tf_op jit(solution)/shard_map/all_to_all | solution.py:202
  239.5 160.1 %all-gather.22.cloned.1.call-start = ((), (), s32[]{:S(2)}) async-start(), calls=%async_computation.2 | async-start | bytes 11796480 | tf_op jit(solution)/shard_map/all_gather | solution.py:218
  342.0 203.6 %all-gather.24.cloned.1.call-start = ((), (), s32[]{:S(2)}) async-start(), calls=%async_computation.3 | async-start | bytes 10321920 | tf_op jit(solution)/shard_map/all_gather | solution.py:218
  391.2 2.1 copy-start.3
  394.5 357.5 %all-gather.26.cloned.1.call-start = ((), (), s32[]{:S(2)}) async-start(), calls=%async_computation.4 | async-start | bytes 8847360 | tf_op jit(solution)/shard_map/all_gather | solution.py:218
  398.2 514.0 %all-gather.28.cloned.1.call-start = ((), (), s32[]{:S(2)}) async-start(), calls=%async_computation.5 | async-start | bytes 8847360 | tf_op jit(solution)/shard_map/all_gather | solution.py:218
  398.9 700.4 %all-gather.30.cloned.1.call-start = ((), (), s32[]{:S(2)}) async-start(), calls=%async_computation.6 | async-start | bytes 8847360 | tf_op jit(solution)/shard_map/all_gather | solution.py:218
  399.5 934.0 %all-gather.32.cloned.1.call-start = ((), (), s32[]{:S(2)}) async-start(), calls=%async_computation.7 | async-start | bytes 4423680 | tf_op jit(solution)/shard_map/all_gather | solution.py:218
  399.6 47.4 %copy-start.29 = (bf16[1024,5120]{1,0:T(8,128)(2,1)S(1)}, bf16[1024,5120]{1,0:T(8,128)(2,1)}, u32[]{:S(2)}) copy-start(bf16[1024,5120]{1,0:T(8,128)(2,1)} %all-gather.22.cloned.1.call-done) | copy-start | bytes 31457284
  540.3 10.4 collective-permute-start
  545.6 951.3 %all-gather.34.cloned.1.call-start = ((), (), s32[]{:S(2)}) async-start(), calls=%async_computation.8 | async-start | bytes 11796480 | tf_op jit(solution)/shard_map/all_gather | solution.py:230
  556.9 95.6 %collective-permute-start.1 = (f32[2,128,2560]{2,1,0:T(8,128)}, f32[2,128,2560]{2,1,0:T(8,128)}, u32[]{:S(2)}, u32[]{:S(2)}) collective-permute-start(f32[2,128,2560]{2,1,0:T(8,128)} %get-tuple-element.61), channel_id=1, source_target_pairs={{0,6},{1,7},{2,0},{3,1},{4,2},{5,3},{6,4},{7,5},{8,14},{9,15},{10,... | collective-permute-start | bytes 7864328 | tf_op jit(solution)/shard_map/ppermute | solution.py:144
  558.9 94.0 %collective-permute-start.2 = (f32[2,128,2560]{2,1,0:T(8,128)}, f32[2,128,2560]{2,1,0:T(8,128)}, u32[]{:S(2)}, u32[]{:S(2)}) collective-permute-start(f32[2,128,2560]{2,1,0:T(8,128)} %get-tuple-element.62), channel_id=1, source_target_pairs={{0,2},{1,3},{2,4},{3,5},{4,6},{5,7},{6,0},{7,1},{8,10},{9,11},{10,... | collective-permute-start | bytes 7864328 | tf_op jit(solution)/shard_map/ppermute | solution.py:144
  658.2 45.1 %collective-permute-start.3 = (f32[128,2560]{1,0:T(8,128)}, f32[128,2560]{1,0:T(8,128)S(1)}, u32[]{:S(2)}, u32[]{:S(2)}) collective-permute-start(f32[128,2560]{1,0:T(8,128)} %get-tuple-element.63), channel_id=1, source_target_pairs={{0,2},{1,3},{2,4},{3,5},{4,6},{5,7},{6,0},{7,1},{8,10},{9,11},{10,... | collective-permute-start | bytes 3932168 | tf_op jit(solution)/shard_map/ppermute | solution.py:144
  658.9 44.4 %collective-permute-start.4 = (f32[128,2560]{1,0:T(8,128)}, f32[128,2560]{1,0:T(8,128)S(1)}, u32[]{:S(2)}, u32[]{:S(2)}) collective-permute-start(f32[128,2560]{1,0:T(8,128)} %get-tuple-element.64), channel_id=1, source_target_pairs={{0,6},{1,7},{2,0},{3,1},{4,2},{5,3},{6,4},{7,5},{8,14},{9,15},{10,... | collective-permute-start | bytes 3932168 | tf_op jit(solution)/shard_map/ppermute | solution.py:144
  711.5 794.7 %all-gather.36.cloned.1.call-start = ((), (), s32[]{:S(2)}) async-start(), calls=%async_computation.9 | async-start | bytes 10321920 | tf_op jit(solution)/shard_map/all_gather | solution.py:230
  752.0 4.7 copy-start.30
  754.7 35.4 %collective-permute-start.5 = (bf16[4,112,5120]{2,1,0:T(8,128)(2,1)S(1)}, bf16[4,112,5120]{2,1,0:T(8,128)(2,1)}, u32[]{:S(2)}, u32[]{:S(2)}) collective-permute-start(bf16[4,112,5120]{2,1,0:T(8,128)(2,1)S(1)} %dynamic-slice_bitcast_fusion.1), channel_id=1, source_target_pairs={{0,1},{1,0},{2,3},{3,2},{4,5},{5,4},{6,7},{7,6},{8,9},{9,8},{10,11... | collective-permute-start | bytes 13762568 | tf_op jit(solution)/shard_map/ppermute | solution.py:144
  797.8 50.1 %collective-permute-start.6 = (f32[2,112,2560]{2,1,0:T(8,128)}, f32[2,112,2560]{2,1,0:T(8,128)}, u32[]{:S(2)}, u32[]{:S(2)}) collective-permute-start(f32[2,112,2560]{2,1,0:T(8,128)} %get-tuple-element.71), channel_id=1, source_target_pairs={{0,6},{1,7},{2,0},{3,1},{4,2},{5,3},{6,4},{7,5},{8,14},{9,15},{10,... | collective-permute-start | bytes 6881288 | tf_op jit(solution)/shard_map/ppermute | solution.py:144
  797.9 51.4 %collective-permute-start.7 = (f32[2,112,2560]{2,1,0:T(8,128)}, f32[2,112,2560]{2,1,0:T(8,128)}, u32[]{:S(2)}, u32[]{:S(2)}) collective-permute-start(f32[2,112,2560]{2,1,0:T(8,128)} %get-tuple-element.72), channel_id=1, source_target_pairs={{0,2},{1,3},{2,4},{3,5},{4,6},{5,7},{6,0},{7,1},{8,10},{9,11},{10,... | collective-permute-start | bytes 6881288 | tf_op jit(solution)/shard_map/ppermute | solution.py:144
  855.7 37.9 %collective-permute-start.8 = (f32[112,2560]{1,0:T(8,128)}, f32[112,2560]{1,0:T(8,128)S(1)}, u32[]{:S(2)}, u32[]{:S(2)}) collective-permute-start(f32[112,2560]{1,0:T(8,128)} %get-tuple-element.73), channel_id=1, source_target_pairs={{0,2},{1,3},{2,4},{3,5},{4,6},{5,7},{6,0},{7,1},{8,10},{9,11},{10,... | collective-permute-start | bytes 3440648 | tf_op jit(solution)/shard_map/ppermute | solution.py:144
  855.7 37.9 %collective-permute-start.9 = (f32[112,2560]{1,0:T(8,128)}, f32[112,2560]{1,0:T(8,128)S(1)}, u32[]{:S(2)}, u32[]{:S(2)}) collective-permute-start(f32[112,2560]{1,0:T(8,128)} %get-tuple-element.74), channel_id=1, source_target_pairs={{0,6},{1,7},{2,0},{3,1},{4,2},{5,3},{6,4},{7,5},{8,14},{9,15},{10,... | collective-permute-start | bytes 3440648 | tf_op jit(solution)/shard_map/ppermute | solution.py:144
  902.8 7.7 slice-start
  902.9 611.3 %all-gather.38.cloned.1.call-start = ((), (), s32[]{:S(2)}) async-start(), calls=%async_computation.10 | async-start | bytes 8847360 | tf_op jit(solution)/shard_map/all_gather | solution.py:230
  903.0 7.5 slice-start.1
  907.4 11.8 collective-permute-start.10
  925.0 68.0 %collective-permute-start.11 = (f32[2,96,2560]{2,1,0:T(8,128)}, f32[2,96,2560]{2,1,0:T(8,128)S(1)}, u32[]{:S(2)}, u32[]{:S(2)}) collective-permute-start(f32[2,96,2560]{2,1,0:T(8,128)} %get-tuple-element.80), channel_id=1, source_target_pairs={{0,6},{1,7},{2,0},{3,1},{4,2},{5,3},{6,4},{7,5},{8,14},{9,15},{10,... | collective-permute-start | bytes 5898248 | tf_op jit(solution)/shard_map/ppermute | solution.py:144
  925.0 68.5 %collective-permute-start.12 = (f32[2,96,2560]{2,1,0:T(8,128)}, f32[2,96,2560]{2,1,0:T(8,128)}, u32[]{:S(2)}, u32[]{:S(2)}) collective-permute-start(f32[2,96,2560]{2,1,0:T(8,128)} %get-tuple-element.81), channel_id=1, source_target_pairs={{0,2},{1,3},{2,4},{3,5},{4,6},{5,7},{6,0},{7,1},{8,10},{9,11},{10,... | collective-permute-start | bytes 5898248 | tf_op jit(solution)/shard_map/ppermute | solution.py:144
  999.1 39.6 %collective-permute-start.13 = (f32[96,2560]{1,0:T(8,128)}, f32[96,2560]{1,0:T(8,128)S(1)}, u32[]{:S(2)}, u32[]{:S(2)}) collective-permute-start(f32[96,2560]{1,0:T(8,128)} %get-tuple-element.82), channel_id=1, source_target_pairs={{0,2},{1,3},{2,4},{3,5},{4,6},{5,7},{6,0},{7,1},{8,10},{9,11},{10,... | collective-permute-start | bytes 2949128 | tf_op jit(solution)/shard_map/ppermute | solution.py:144
  1000.2 38.6 %collective-permute-start.14 = (f32[96,2560]{1,0:T(8,128)}, f32[96,2560]{1,0:T(8,128)S(1)}, u32[]{:S(2)}, u32[]{:S(2)}) collective-permute-start(f32[96,2560]{1,0:T(8,128)} %get-tuple-element.83), channel_id=1, source_target_pairs={{0,6},{1,7},{2,0},{3,1},{4,2},{5,3},{6,4},{7,5},{8,14},{9,15},{10,... | collective-permute-start | bytes 2949128 | tf_op jit(solution)/shard_map/ppermute | solution.py:144
  1045.5 475.8 %all-gather.40.cloned.1.call-start = ((), (), s32[]{:S(2)}) async-start(), calls=%async_computation.11 | async-start | bytes 8847360 | tf_op jit(solution)/shard_map/all_gather | solution.py:230
  1083.4 8.8 collective-permute-start.15
  1097.8 44.3 %collective-permute-start.16 = (f32[2,96,2560]{2,1,0:T(8,128)}, f32[2,96,2560]{2,1,0:T(8,128)S(1)}, u32[]{:S(2)}, u32[]{:S(2)}) collective-permute-start(f32[2,96,2560]{2,1,0:T(8,128)} %get-tuple-element.89), channel_id=1, source_target_pairs={{0,6},{1,7},{2,0},{3,1},{4,2},{5,3},{6,4},{7,5},{8,14},{9,15},{10,... | collective-permute-start | bytes 5898248 | tf_op jit(solution)/shard_map/ppermute | solution.py:144
  1097.9 45.6 %collective-permute-start.17 = (f32[2,96,2560]{2,1,0:T(8,128)}, f32[2,96,2560]{2,1,0:T(8,128)}, u32[]{:S(2)}, u32[]{:S(2)}) collective-permute-start(f32[2,96,2560]{2,1,0:T(8,128)} %get-tuple-element.90), channel_id=1, source_target_pairs={{0,2},{1,3},{2,4},{3,5},{4,6},{5,7},{6,0},{7,1},{8,10},{9,11},{10,... | collective-permute-start | bytes 5898248 | tf_op jit(solution)/shard_map/ppermute | solution.py:144
  1142.2 1.3 copy-start.6
  1148.4 38.2 %collective-permute-start.18 = (f32[96,2560]{1,0:T(8,128)}, f32[96,2560]{1,0:T(8,128)S(1)}, u32[]{:S(2)}, u32[]{:S(2)}) collective-permute-start(f32[96,2560]{1,0:T(8,128)} %get-tuple-element.91), channel_id=1, source_target_pairs={{0,2},{1,3},{2,4},{3,5},{4,6},{5,7},{6,0},{7,1},{8,10},{9,11},{10,... | collective-permute-start | bytes 2949128 | tf_op jit(solution)/shard_map/ppermute | solution.py:144
  1148.4 38.2 %collective-permute-start.19 = (f32[96,2560]{1,0:T(8,128)}, f32[96,2560]{1,0:T(8,128)S(1)}, u32[]{:S(2)}, u32[]{:S(2)}) collective-permute-start(f32[96,2560]{1,0:T(8,128)} %get-tuple-element.92), channel_id=1, source_target_pairs={{0,6},{1,7},{2,0},{3,1},{4,2},{5,3},{6,4},{7,5},{8,14},{9,15},{10,... | collective-permute-start | bytes 2949128 | tf_op jit(solution)/shard_map/ppermute | solution.py:144
  1193.2 335.0 %all-gather.42.cloned.1.call-start = ((), (), s32[]{:S(2)}) async-start(), calls=%async_computation.12 | async-start | bytes 8847360 | tf_op jit(solution)/shard_map/all_gather | solution.py:230
  1265.6 8.9 collective-permute-start.20
  1280.3 44.3 %collective-permute-start.21 = (f32[2,96,2560]{2,1,0:T(8,128)}, f32[2,96,2560]{2,1,0:T(8,128)S(1)}, u32[]{:S(2)}, u32[]{:S(2)}) collective-permute-start(f32[2,96,2560]{2,1,0:T(8,128)} %get-tuple-element.98), channel_id=1, source_target_pairs={{0,6},{1,7},{2,0},{3,1},{4,2},{5,3},{6,4},{7,5},{8,14},{9,15},{10,... | collective-permute-start | bytes 5898248 | tf_op jit(solution)/shard_map/ppermute | solution.py:144
  1280.3 45.6 %collective-permute-start.22 = (f32[2,96,2560]{2,1,0:T(8,128)}, f32[2,96,2560]{2,1,0:T(8,128)}, u32[]{:S(2)}, u32[]{:S(2)}) collective-permute-start(f32[2,96,2560]{2,1,0:T(8,128)} %get-tuple-element.99), channel_id=1, source_target_pairs={{0,2},{1,3},{2,4},{3,5},{4,6},{5,7},{6,0},{7,1},{8,10},{9,11},{10,... | collective-permute-start | bytes 5898248 | tf_op jit(solution)/shard_map/ppermute | solution.py:144
  1324.6 1.3 copy-start.7
  1330.8 23.5 %collective-permute-start.23 = (f32[96,2560]{1,0:T(8,128)}, f32[96,2560]{1,0:T(8,128)S(1)}, u32[]{:S(2)}, u32[]{:S(2)}) collective-permute-start(f32[96,2560]{1,0:T(8,128)} %get-tuple-element.100), channel_id=1, source_target_pairs={{0,2},{1,3},{2,4},{3,5},{4,6},{5,7},{6,0},{7,1},{8,10},{9,11},{10,... | collective-permute-start | bytes 2949128 | tf_op jit(solution)/shard_map/ppermute | solution.py:144
  1330.8 23.5 %collective-permute-start.24 = (f32[96,2560]{1,0:T(8,128)}, f32[96,2560]{1,0:T(8,128)S(1)}, u32[]{:S(2)}, u32[]{:S(2)}) collective-permute-start(f32[96,2560]{1,0:T(8,128)} %get-tuple-element.101), channel_id=1, source_target_pairs={{0,6},{1,7},{2,0},{3,1},{4,2},{5,3},{6,4},{7,5},{8,14},{9,15},{10,... | collective-permute-start | bytes 2949128 | tf_op jit(solution)/shard_map/ppermute | solution.py:144
  1361.0 174.4 %all-gather.44.cloned.1.call-start = ((), (), s32[]{:S(2)}) async-start(), calls=%async_computation.13 | async-start | bytes 4423680 | tf_op jit(solution)/shard_map/all_gather | solution.py:230
  1361.0 23.5 %copy-start.31 = (bf16[384,5120]{1,0:T(8,128)(2,1)S(1)}, bf16[384,5120]{1,0:T(8,128)(2,1)}, u32[]{:S(2)}) copy-start(bf16[384,5120]{1,0:T(8,128)(2,1)} %all-gather.32.cloned.1.call-done) | copy-start | bytes 11796484
  1428.9 5.7 collective-permute-start.25
  1440.4 23.5 %collective-permute-start.26 = (f32[2,48,2560]{2,1,0:T(8,128)}, f32[2,48,2560]{2,1,0:T(8,128)S(1)}, u32[]{:S(2)}, u32[]{:S(2)}) collective-permute-start(f32[2,48,2560]{2,1,0:T(8,128)} %get-tuple-element.107), channel_id=1, source_target_pairs={{0,6},{1,7},{2,0},{3,1},{4,2},{5,3},{6,4},{7,5},{8,14},{9,15},{10,... | collective-permute-start | bytes 2949128 | tf_op jit(solution)/shard_map/ppermute | solution.py:144
  1442.8 24.1 %collective-permute-start.27 = (f32[2,48,2560]{2,1,0:T(8,128)}, f32[2,48,2560]{2,1,0:T(8,128)S(1)}, u32[]{:S(2)}, u32[]{:S(2)}) collective-permute-start(f32[2,48,2560]{2,1,0:T(8,128)} %get-tuple-element.108), channel_id=1, source_target_pairs={{0,2},{1,3},{2,4},{3,5},{4,6},{5,7},{6,0},{7,1},{8,10},{9,11},{10,... | collective-permute-start | bytes 2949128 | tf_op jit(solution)/shard_map/ppermute | solution.py:144
  1463.9 3.0 copy-start.10
  1471.9 12.7 collective-permute-start.28
  1471.9 12.7 collective-permute-start.29
  1490.5 1.4 copy-start.5
  1490.5 1.4 copy-start.25
  1528.2 11.4 copy-start.1
  (15 other events, 16.0 us)
Sparse Core Ops, SparseCore 0:
  14.1 238.4 all-gather.19
  342.1 55.2 all-gather.21
  399.0 49.1 all-gather.23
  449.6 43.5 all-gather.25
  494.6 43.4 all-gather.27
  539.6 63.3 all-gather.29
  604.6 44.4 all-gather.31
  711.6 54.5 all-gather.33
  903.0 72.7 all-gather.35
  1045.6 44.2 all-gather.37
  1193.4 43.5 all-gather.39
  1361.1 45.7 all-gather.41
  1490.6 29.0 all-gather.43
